TPU v7x, 32 devices: a whole 2x2x4 slice. The times are simulated.
32 devices in a mesh: dp: 4 (over z), expert: 8 (over y, x, core).
Axes of the slice: x: 2, y: 2, z: 4, core: 2. Of those that a mesh axis runs over, the one named last changes fastest.
Arguments:
- hidden_in: bfloat16 [8192, 2048], P(('dp', 'expert')), may hold values from -8 to 8
- segment_ids: int32 [8192], P(('dp', 'expert')), may hold values from 0 to 127, never falling along the last dimension, each value on 1 to 256 neighbouring positions
- expert_ids: int32 [8192, 8], P(('dp', 'expert')), may hold values from 0 to 31, as said below
- attn_gain: bfloat16 [2048], P(('dp', 'expert')), may hold values from 0.5 to 1.5
- query_gain: bfloat16 [128], P(('dp', 'expert')), may hold values from 0.5 to 1.5
- key_gain: bfloat16 [128], P(('dp', 'expert')), may hold values from 0.5 to 1.5
- w_query: bfloat16 [2048, 4096], P(('dp', 'expert')), may hold values from -0.125 to 0.125
- w_key: bfloat16 [2048, 512], P(('dp', 'expert')), may hold values from -0.125 to 0.125
- w_value: bfloat16 [2048, 512], P(('dp', 'expert')), may hold values from -0.125 to 0.125
- w_output: bfloat16 [4096, 2048], P(('dp', 'expert')), may hold values from -0.375 to 0.375
- mlp_gain: bfloat16 [2048], P(('dp', 'expert')), may hold values from 0.5 to 1.5
- w_router: bfloat16 [2048, 32], P(('dp', 'expert')), may hold values from -0.019897461 to 0.019897461
- w_gate: bfloat16 [32, 2048, 768], P(('dp', 'expert')), may hold values from -0.125 to 0.125
- w_up: bfloat16 [32, 2048, 768], P(('dp', 'expert')), may hold values from -0.125 to 0.125
- w_down: bfloat16 [32, 768, 2048], P(('dp', 'expert')), may hold values from -0.875 to 0.875
- out_grad: bfloat16 [8192, 2048], P(('dp', 'expert')), may hold values from -6 to 6
Outputs:
- block_out: float32 [8192, 2048], P(('dp', 'expert'))
- grad_in: float32 [8192, 2048], P(('dp', 'expert'))
- grad_attn_gain: float32 [2048], P(('dp', 'expert'))
- grad_query_gain: float32 [128], P(('dp', 'expert'))
- grad_key_gain: float32 [128], P(('dp', 'expert'))
- grad_w_query: float32 [2048, 4096], P(('dp', 'expert'))
- grad_w_key: float32 [2048, 512], P(('dp', 'expert'))
- grad_w_value: float32 [2048, 512], P(('dp', 'expert'))
- grad_w_output: float32 [4096, 2048], P(('dp', 'expert'))
- grad_mlp_gain: float32 [2048], P(('dp', 'expert'))
- grad_w_router: float32 [2048, 32], P(('dp', 'expert'))
- grad_w_gate: float32 [32, 2048, 768], P(('dp', 'expert'))
- grad_w_up: float32 [32, 2048, 768], P(('dp', 'expert'))
- grad_w_down: float32 [32, 768, 2048], P(('dp', 'expert'))
Inputs may be any that keep to these rules, and one draw needn't show every extreme that they name: `expert_ids`: each row names 8 different experts. On one device the experts fall into 4 groups of 8, and each row names all experts of one group. The rows of one device name each expert at least 26 and at most 80 times; one expert is named exactly 80 times by the rows of every device.
All inputs are finite; a program needn't handle non-finite values.
Results may differ from a plain program's by a relative error of at most 0.02.
Values may be sent and summed in bfloat16 or wider, within the bound.
A program may use at most 384 MiB of HBM per device.

v0:
```python
import math

import jax
import jax.numpy as jnp
from jax import lax
from jax.sharding import PartitionSpec as P

HEADS = 32
KV_HEADS = 4
HEAD_DIM = 128
TOK_DEV = 256


EPS = 1e-06
ROPE_BASE = 1000000.0


def rms_scale(values):
    return lax.rsqrt(jnp.mean(values * values, -1, keepdims=True) + EPS)


def norm_grad(upstream, values, inverse, gain_vec):
    weighted = upstream * gain_vec
    return inverse * weighted - values * inverse**3 * jnp.mean(weighted * values, -1, keepdims=True)


def rope_tables(positions, head_dim):
    half_dim = head_dim // 2
    frequency = ROPE_BASE ** (-(jnp.arange(half_dim).astype(jnp.float32) * 2.0 / head_dim))
    angles = positions.astype(jnp.float32)[:, None] * frequency[None, :]
    return (jnp.cos(angles)[:, None, :], jnp.sin(angles)[:, None, :])


def rotate(values, cosine_table, sine_table):
    half_dim = values.shape[-1] // 2
    first_half = values[..., :half_dim]
    second_half = values[..., half_dim:]
    return jnp.concatenate(
        [
            first_half * cosine_table - second_half * sine_table,
            second_half * cosine_table + first_half * sine_table,
        ],
        -1,
    )


def unrotate(values, cosine_table, sine_table):
    half_dim = values.shape[-1] // 2
    first_half = values[..., :half_dim]
    second_half = values[..., half_dim:]
    return jnp.concatenate(
        [
            first_half * cosine_table + second_half * sine_table,
            second_half * cosine_table - first_half * sine_table,
        ],
        -1,
    )


def attend(query_rot, key_rot, value_rows, allowed):
    score_scale = 1.0 / math.sqrt(HEAD_DIM)
    scores = (
        jnp.einsum("qkgd,tkd->kgqt", query_rot, key_rot, preferred_element_type=jnp.float32)
        * score_scale
    )
    exp_scores = jnp.where(allowed, jnp.exp(scores), 0.0)
    totals = jnp.sum(exp_scores, -1, keepdims=True)
    probs_low = (exp_scores / totals).astype(jnp.bfloat16)
    attended = jnp.einsum(
        "kgqt,tkd->qkgd", probs_low, value_rows, preferred_element_type=jnp.float32
    ).astype(jnp.bfloat16)
    return (attended, jnp.log(totals))


def attend_grad(query_rot, key_rot, value_rows, allowed, log_totals, attended_grad):
    score_scale = 1.0 / math.sqrt(HEAD_DIM)
    scores = (
        jnp.einsum("qkgd,tkd->kgqt", query_rot, key_rot, preferred_element_type=jnp.float32)
        * score_scale
    )
    probs_back = jnp.where(allowed, jnp.exp(scores - log_totals), 0.0)
    probs_low = probs_back.astype(jnp.bfloat16)
    value_sum_grad = jnp.einsum(
        "kgqt,qkgd->tkd", probs_low, attended_grad, preferred_element_type=jnp.float32
    )
    prob_grad = jnp.einsum(
        "qkgd,tkd->kgqt", attended_grad, value_rows, preferred_element_type=jnp.float32
    )
    score_grad = (
        probs_back * (prob_grad - jnp.sum(probs_back * prob_grad, -1, keepdims=True))
    ).astype(jnp.bfloat16)
    query_rot_grad = (
        jnp.einsum("kgqt,tkd->qkgd", score_grad, key_rot, preferred_element_type=jnp.float32)
        * score_scale
    )
    key_rot_grad = (
        jnp.einsum("kgqt,qkgd->tkd", score_grad, query_rot, preferred_element_type=jnp.float32)
        * score_scale
    )
    return (query_rot_grad, key_rot_grad, value_sum_grad)


def mixer_forward(block_in, block_segments, weights):
    w_query, w_key, w_value, w_output, w_router, attn_gain, mlp_gain, query_gain, key_gain = weights
    row_count = block_in.shape[0]
    seq_count = row_count // TOK_DEV
    group_size = HEADS // KV_HEADS
    plain_in = block_in.astype(jnp.float32)
    inv_attn = rms_scale(plain_in)
    normed_attn = (plain_in * inv_attn * attn_gain).astype(jnp.bfloat16)
    query_raw = jnp.dot(normed_attn, w_query, preferred_element_type=jnp.float32).reshape(
        row_count, HEADS, HEAD_DIM
    )
    key_raw = jnp.dot(normed_attn, w_key, preferred_element_type=jnp.float32).reshape(
        row_count, KV_HEADS, HEAD_DIM
    )
    value_rows = jnp.dot(normed_attn, w_value, preferred_element_type=jnp.float32).astype(
        jnp.bfloat16
    )
    value_rows = value_rows.reshape(seq_count, TOK_DEV, KV_HEADS, HEAD_DIM)
    query_scale = rms_scale(query_raw)
    key_scale = rms_scale(key_raw)
    cosine_table, sine_table = rope_tables(jnp.arange(row_count) % TOK_DEV, HEAD_DIM)
    query_rot = rotate(query_raw * query_scale * query_gain, cosine_table, sine_table).astype(
        jnp.bfloat16
    )
    query_rot = query_rot.reshape(seq_count, TOK_DEV, KV_HEADS, group_size, HEAD_DIM)
    key_rot = rotate(key_raw * key_scale * key_gain, cosine_table, sine_table).astype(jnp.bfloat16)
    key_rot = key_rot.reshape(seq_count, TOK_DEV, KV_HEADS, HEAD_DIM)
    segments = block_segments.reshape(seq_count, TOK_DEV)
    position = jnp.arange(TOK_DEV)
    allowed = (segments[:, :, None] == segments[:, None, :]) & (
        position[None, None, :] <= position[None, :, None]
    )
    attended, log_totals = jax.vmap(attend)(query_rot, key_rot, value_rows, allowed)
    attended = attended.reshape(row_count, HEADS * HEAD_DIM)
    residual = plain_in + jnp.dot(attended, w_output, preferred_element_type=jnp.float32)
    saved_state = (
        plain_in,
        inv_attn,
        normed_attn,
        query_raw,
        key_raw,
        value_rows,
        query_scale,
        key_scale,
        query_rot,
        key_rot,
        allowed,
        log_totals,
        attended,
        cosine_table,
        sine_table,
    )
    return (residual, saved_state)


def mixer_backward(residual_grad, saved_state, weights):
    w_query, w_key, w_value, w_output, w_router, attn_gain, mlp_gain, query_gain, key_gain = weights
    (
        plain_in,
        inv_attn,
        normed_attn,
        query_raw,
        key_raw,
        value_rows,
        query_scale,
        key_scale,
        query_rot,
        key_rot,
        allowed,
        log_totals,
        attended,
        cosine_table,
        sine_table,
    ) = saved_state
    row_count = residual_grad.shape[0]
    seq_count = row_count // TOK_DEV
    group_size = HEADS // KV_HEADS
    branch_grad = residual_grad.astype(jnp.bfloat16)
    grad_w_output = jnp.dot(attended.T, branch_grad, preferred_element_type=jnp.float32)
    attended_grad = jnp.dot(branch_grad, w_output.T, preferred_element_type=jnp.float32).astype(
        jnp.bfloat16
    )
    attended_grad = attended_grad.reshape(seq_count, TOK_DEV, KV_HEADS, group_size, HEAD_DIM)
    query_rot_grad, key_rot_grad, value_sum_grad = jax.vmap(attend_grad)(
        query_rot, key_rot, value_rows, allowed, log_totals, attended_grad
    )
    query_normed_grad = unrotate(
        query_rot_grad.reshape(row_count, HEADS, HEAD_DIM), cosine_table, sine_table
    )
    key_normed_grad = unrotate(
        key_rot_grad.reshape(row_count, KV_HEADS, HEAD_DIM), cosine_table, sine_table
    )
    grad_query_gain = jnp.sum(query_normed_grad * query_raw * query_scale, (0, 1))
    grad_key_gain = jnp.sum(key_normed_grad * key_raw * key_scale, (0, 1))
    query_grad = norm_grad(query_normed_grad, query_raw, query_scale, query_gain).astype(
        jnp.bfloat16
    )
    query_grad = query_grad.reshape(row_count, HEADS * HEAD_DIM)
    key_grad = norm_grad(key_normed_grad, key_raw, key_scale, key_gain).astype(jnp.bfloat16)
    key_grad = key_grad.reshape(row_count, KV_HEADS * HEAD_DIM)
    value_grad = value_sum_grad.astype(jnp.bfloat16).reshape(row_count, KV_HEADS * HEAD_DIM)
    grad_w_query = jnp.dot(normed_attn.T, query_grad, preferred_element_type=jnp.float32)
    grad_w_key = jnp.dot(normed_attn.T, key_grad, preferred_element_type=jnp.float32)
    grad_w_value = jnp.dot(normed_attn.T, value_grad, preferred_element_type=jnp.float32)
    normed_attn_grad = (
        jnp.dot(query_grad, w_query.T, preferred_element_type=jnp.float32)
        + jnp.dot(key_grad, w_key.T, preferred_element_type=jnp.float32)
        + jnp.dot(value_grad, w_value.T, preferred_element_type=jnp.float32)
    )
    grad_attn_gain = jnp.sum(normed_attn_grad * plain_in * inv_attn, 0)
    grad_in = residual_grad + norm_grad(normed_attn_grad, plain_in, inv_attn, attn_gain)
    return (
        grad_in,
        (
            grad_attn_gain,
            grad_query_gain,
            grad_key_gain,
            grad_w_query,
            grad_w_key,
            grad_w_value,
            grad_w_output,
        ),
    )


def dispatch_table(expert_rows, experts, capacity):
    length, choices = expert_rows.shape
    flat_ids = expert_rows.reshape(length * choices)
    marks = (flat_ids[:, None] == jnp.arange(experts)[None, :]).astype(jnp.int32)
    earlier = jnp.cumsum(marks, 0) - marks
    destination = flat_ids * capacity + jnp.sum(earlier * marks, -1)
    pair_ids = (
        jnp.zeros((experts * capacity,), jnp.int32)
        .at[destination]
        .set(jnp.arange(length * choices, dtype=jnp.int32))
    )
    filled = jnp.zeros((experts * capacity,), jnp.bfloat16).at[destination].set(1.0)
    return (destination, pair_ids, filled)


def move_rows(row_block, section_name):
    if section_name == "dispatch":
        return lax.all_to_all(row_block, ("dp", "expert"), split_axis=0, concat_axis=0, tiled=True)
    if section_name == "combine":
        return lax.all_to_all(row_block, ("dp", "expert"), split_axis=0, concat_axis=0, tiled=True)
    if section_name == "grad_dispatch":
        return lax.all_to_all(row_block, ("dp", "expert"), split_axis=0, concat_axis=0, tiled=True)
    return lax.all_to_all(row_block, ("dp", "expert"), split_axis=0, concat_axis=0, tiled=True)


def per_device(
    hidden_in,
    segment_ids,
    expert_ids,
    attn_gain,
    query_gain,
    key_gain,
    w_query,
    w_key,
    w_value,
    w_output,
    mlp_gain,
    w_router,
    w_gate,
    w_up,
    w_down,
    out_grad,
):
    weights = (
        lax.all_gather(w_query, ("dp", "expert"), axis=0, tiled=True),
        lax.all_gather(w_key, ("dp", "expert"), axis=0, tiled=True),
        lax.all_gather(w_value, ("dp", "expert"), axis=0, tiled=True),
        lax.all_gather(w_output, ("dp", "expert"), axis=0, tiled=True),
        lax.all_gather(w_router, ("dp", "expert"), axis=0, tiled=True),
        lax.all_gather(attn_gain, ("dp", "expert"), axis=0, tiled=True),
        lax.all_gather(mlp_gain, ("dp", "expert"), axis=0, tiled=True),
        lax.all_gather(query_gain, ("dp", "expert"), axis=0, tiled=True),
        lax.all_gather(key_gain, ("dp", "expert"), axis=0, tiled=True),
    )
    residual, saved_state = mixer_forward(hidden_in, segment_ids, weights)
    full_router = weights[4]
    full_mlp_gain = weights[6]
    inv_mlp = rms_scale(residual)
    normed_mlp = (residual * inv_mlp * full_mlp_gain).astype(jnp.bfloat16)
    logits = jnp.dot(normed_mlp, full_router, preferred_element_type=jnp.float32)
    device_count = lax.axis_size(("dp", "expert"))
    local_experts = w_gate.shape[0]
    experts = local_experts * device_count
    length, choices = expert_ids.shape
    model_width = hidden_in.shape[1]
    capacity = 5 * length * choices // (4 * experts)
    one_hot = expert_ids[:, :, None] == jnp.arange(experts)[None, None, :]
    chosen = jnp.sum(jnp.where(one_hot, logits[:, None, :], 0.0), -1)
    raised = jnp.exp(chosen)
    gate_weights = raised / jnp.sum(raised, -1, keepdims=True)
    destination, pair_ids, filled = dispatch_table(expert_ids, experts, capacity)
    send_rows = normed_mlp[pair_ids // choices] * filled[:, None]
    received = move_rows(
        send_rows.reshape(device_count, local_experts * capacity, model_width), "dispatch"
    )
    received = received.reshape(device_count, local_experts, capacity, model_width)
    pre_gate = jnp.einsum("secd,edf->secf", received, w_gate, preferred_element_type=jnp.float32)
    pre_up = jnp.einsum("secd,edf->secf", received, w_up, preferred_element_type=jnp.float32)
    gate_sigmoid = jax.nn.sigmoid(pre_gate)
    silu_gate = pre_gate * gate_sigmoid
    activation = (silu_gate * pre_up).astype(jnp.bfloat16)
    expert_out = jnp.einsum(
        "secf,efd->secd", activation, w_down, preferred_element_type=jnp.float32
    ).astype(jnp.bfloat16)
    returned = move_rows(
        expert_out.reshape(device_count, local_experts * capacity, model_width), "combine"
    )
    picked = returned.reshape(experts * capacity, model_width)[destination].reshape(
        length, choices, model_width
    )
    block_out = residual + jnp.sum(gate_weights[:, :, None] * picked.astype(jnp.float32), 1)
    weights = (
        lax.all_gather(w_query, ("dp", "expert"), axis=0, tiled=True),
        lax.all_gather(w_key, ("dp", "expert"), axis=0, tiled=True),
        lax.all_gather(w_value, ("dp", "expert"), axis=0, tiled=True),
        lax.all_gather(w_output, ("dp", "expert"), axis=0, tiled=True),
        lax.all_gather(w_router, ("dp", "expert"), axis=0, tiled=True),
        lax.all_gather(attn_gain, ("dp", "expert"), axis=0, tiled=True),
        lax.all_gather(mlp_gain, ("dp", "expert"), axis=0, tiled=True),
        lax.all_gather(query_gain, ("dp", "expert"), axis=0, tiled=True),
        lax.all_gather(key_gain, ("dp", "expert"), axis=0, tiled=True),
    )
    full_router = weights[4]
    full_mlp_gain = weights[6]
    cotangent = out_grad.astype(jnp.float32)
    gate_grad = jnp.sum(cotangent[:, None, :] * picked.astype(jnp.float32), -1)
    down_in = (
        (gate_weights[:, :, None] * cotangent[:, None, :])
        .astype(jnp.bfloat16)
        .reshape(length * choices, model_width)
    )
    send_grad = down_in[pair_ids] * filled[:, None]
    recv_grad = move_rows(
        send_grad.reshape(device_count, local_experts * capacity, model_width), "grad_dispatch"
    )
    recv_grad = recv_grad.reshape(device_count, local_experts, capacity, model_width)
    act_grad = jnp.einsum("secd,efd->secf", recv_grad, w_down, preferred_element_type=jnp.float32)
    grad_w_down = jnp.einsum(
        "secf,secd->efd", activation, recv_grad, preferred_element_type=jnp.float32
    )
    gate_pre_grad = (
        act_grad * pre_up * gate_sigmoid * (1.0 + pre_gate * (1.0 - gate_sigmoid))
    ).astype(jnp.bfloat16)
    up_pre_grad = (act_grad * silu_gate).astype(jnp.bfloat16)
    grad_w_gate = jnp.einsum(
        "secd,secf->edf", received, gate_pre_grad, preferred_element_type=jnp.float32
    )
    grad_w_up = jnp.einsum(
        "secd,secf->edf", received, up_pre_grad, preferred_element_type=jnp.float32
    )
    row_grad = (
        jnp.einsum("secf,edf->secd", gate_pre_grad, w_gate, preferred_element_type=jnp.float32)
        + jnp.einsum("secf,edf->secd", up_pre_grad, w_up, preferred_element_type=jnp.float32)
    ).astype(jnp.bfloat16)
    row_back = move_rows(
        row_grad.reshape(device_count, local_experts * capacity, model_width), "grad_return"
    )
    row_back = row_back.reshape(experts * capacity, model_width)[destination].reshape(
        length, choices, model_width
    )
    sel_grad = gate_weights * (gate_grad - jnp.sum(gate_weights * gate_grad, -1, keepdims=True))
    logit_grad = jnp.sum(jnp.where(one_hot, sel_grad[:, :, None], 0.0), 1).astype(jnp.bfloat16)
    grad_w_router = jnp.dot(normed_mlp.T, logit_grad, preferred_element_type=jnp.float32)
    normed_mlp_grad = jnp.sum(row_back.astype(jnp.float32), 1) + jnp.dot(
        logit_grad, full_router.T, preferred_element_type=jnp.float32
    )
    grad_mlp_gain = jnp.sum(normed_mlp_grad * residual * inv_mlp, 0)
    residual_grad = cotangent + norm_grad(normed_mlp_grad, residual, inv_mlp, full_mlp_gain)
    grad_in, mixer_terms = mixer_backward(residual_grad, saved_state, weights)
    (
        grad_attn_gain,
        grad_query_gain,
        grad_key_gain,
        grad_w_query,
        grad_w_key,
        grad_w_value,
        grad_w_output,
    ) = mixer_terms
    summed = (
        lax.psum_scatter(grad_w_query, ("dp", "expert"), scatter_dimension=0, tiled=True),
        lax.psum_scatter(grad_w_key, ("dp", "expert"), scatter_dimension=0, tiled=True),
        lax.psum_scatter(grad_w_value, ("dp", "expert"), scatter_dimension=0, tiled=True),
        lax.psum_scatter(grad_w_output, ("dp", "expert"), scatter_dimension=0, tiled=True),
        lax.psum_scatter(grad_w_router, ("dp", "expert"), scatter_dimension=0, tiled=True),
        lax.psum_scatter(grad_attn_gain, ("dp", "expert"), scatter_dimension=0, tiled=True),
        lax.psum_scatter(grad_mlp_gain, ("dp", "expert"), scatter_dimension=0, tiled=True),
        lax.psum_scatter(grad_query_gain, ("dp", "expert"), scatter_dimension=0, tiled=True),
        lax.psum_scatter(grad_key_gain, ("dp", "expert"), scatter_dimension=0, tiled=True),
    )
    (
        share_w_query,
        share_w_key,
        share_w_value,
        share_w_output,
        share_w_router,
        share_attn_gain,
        share_mlp_gain,
        share_query_gain,
        share_key_gain,
    ) = summed
    return (
        block_out,
        grad_in,
        share_attn_gain,
        share_query_gain,
        share_key_gain,
        share_w_query,
        share_w_key,
        share_w_value,
        share_w_output,
        share_mlp_gain,
        share_w_router,
        grad_w_gate,
        grad_w_up,
        grad_w_down,
    )


def solution(mesh):
    in_specs = (
        P(("dp", "expert"), None),
        P(("dp", "expert")),
        P(("dp", "expert"), None),
        P(("dp", "expert")),
        P(("dp", "expert")),
        P(("dp", "expert")),
        P(("dp", "expert"), None),
        P(("dp", "expert"), None),
        P(("dp", "expert"), None),
        P(("dp", "expert"), None),
        P(("dp", "expert")),
        P(("dp", "expert"), None),
        P(("dp", "expert"), None, None),
        P(("dp", "expert"), None, None),
        P(("dp", "expert"), None, None),
        P(("dp", "expert"), None),
    )
    out_specs = (
        P(("dp", "expert"), None),
        P(("dp", "expert"), None),
        P(("dp", "expert")),
        P(("dp", "expert")),
        P(("dp", "expert")),
        P(("dp", "expert"), None),
        P(("dp", "expert"), None),
        P(("dp", "expert"), None),
        P(("dp", "expert"), None),
        P(("dp", "expert")),
        P(("dp", "expert"), None),
        P(("dp", "expert"), None, None),
        P(("dp", "expert"), None, None),
        P(("dp", "expert"), None, None),
    )
    return jax.shard_map(
        per_device, mesh=mesh, in_specs=in_specs, out_specs=out_specs, check_vma=False
    )
```

profile of v0, /device:TPU:0, one launch (start us, length us, event | category | flops | bytes accessed | tf_op | source)
XLA Modules:
  0.0 2517.8 jit_solution(725001799840933317)
XLA Ops:
  14.5 42.3 %all-reduce.9 = (bf16[128]{0:T(256)(128)(2,1)S(1)}, bf16[2048]{0:T(1024)(128)(2,1)S(1)}, bf16[128]{0:T(256)(128)(2,1)S(1)}, bf16[2048]{0:T(1024)(128)(2,1)S(1)}) all-reduce(bf16[128]{0:T(256)(128)(2,1)S(1)} %dynamic-update-slice.2, bf16[2048]{0:T(1024)(128)(2,1)S(1)} %dynamic-update-slice, ...), channel_id=1, replica_groups=mesh['dp'=4,'expert'=8] {'dp','expert'}, use_global_device_ids=true, to_apply=%add.2 | all-reduce | flops 4352 | bytes 17408
  59.5 15.9 reduce-window.6
  77.9 14.6 scatter_custom_fusion.1
  101.8 41.4 %all-gather = bf16[32,64,32]{1,2,0:T(8,128)(2,1)S(1)} all-gather(bf16[1,64,32]{1,2,0:T(8,128)(2,1)S(1)} %bitcast.391), channel_id=1, replica_groups=mesh['dp'=4,'expert'=8] {'dp','expert'}, dimensions={0}, use_global_device_ids=true | all-gather | bytes 135168 | tf_op jit(solution)/shard_map/all_gather | solution.py:276
  169.7 74.5 %all-gather.10.cloned.1.call-done = bf16[2048,4096]{1,0:T(8,128)(2,1)} async-done(((bf16[64,4096]{1,0:T(8,128)(2,1)}), bf16[2048,4096]{1,0:T(8,128)(2,1)}) %all-gather.10.cloned.1.call-update) | async-done | bytes 16777232 | tf_op jit(solution)/shard_map/all_gather | solution.py:272
  272.7 86.8 %all-gather.12.cloned.1.call-done = bf16[4096,2048]{1,0:T(8,128)(2,1)} async-done(((bf16[128,2048]{1,0:T(8,128)(2,1)}), bf16[4096,2048]{1,0:T(8,128)(2,1)}) %all-gather.12.cloned.1.call-update) | async-done | bytes 16777232 | tf_op jit(solution)/shard_map/all_gather | solution.py:275
  373.9 21.5 gather_fusion
  401.3 24.6 gather_fusion.2
  438.4 231.2 %all_to_all.20 = bf16[32,80,2048]{2,1,0:T(8,128)(2,1)} all-to-all(bf16[32,80,2048]{2,1,0:T(8,128)(2,1)S(1)} %get-tuple-element.58), channel_id=1, replica_groups=mesh['dp'=4,'expert'=8] {'dp','expert'}, dimensions={0} | all-to-all | bytes 20971520 | tf_op jit(solution)/shard_map/all_to_all | solution.py:245
  687.5 218.1 %all-to-all-done.2 = bf16[32,80,2048]{2,1,0:T(8,128)(2,1)} async-done(((bf16[32,80,2048]{2,1,0:T(8,128)(2,1)}), bf16[32,80,2048]{2,1,0:T(8,128)(2,1)}, u32[]{:S(2)}, u32[]{:S(2)}) %all-to-all-start.2) | async-done | bytes 10485792 | tf_op jit(solution)/shard_map/all_to_all | solution.py:249
  905.5 13.9 fusion.39
  919.4 19.7 fusion.31
  969.8 16.5 add_convert_fusion
  986.4 202.2 %all-to-all-done.1 = bf16[32,80,2048]{2,1,0:T(8,128)(2,1)} async-done(((bf16[32,80,2048]{2,1,0:T(8,128)(2,1)}), bf16[32,80,2048]{2,1,0:T(8,128)(2,1)}, u32[]{:S(2)}, u32[]{:S(2)}) %all-to-all-start.1) | async-done | bytes 10485792 | tf_op jit(solution)/shard_map/all_to_all | solution.py:247
  1192.5 21.8 gather_fusion.1
  1225.7 204.0 %all-to-all-done.3 = bf16[32,80,2048]{2,1,0:T(8,128)(2,1)} async-done(((bf16[32,80,2048]{2,1,0:T(8,128)(2,1)}), bf16[32,80,2048]{2,1,0:T(8,128)(2,1)}, u32[]{:S(2)}, u32[]{:S(2)}) %all-to-all-start.3) | async-done | bytes 10485792 | tf_op jit(solution)/shard_map/all_to_all | solution.py:250
  1429.7 21.8 gather_fusion.3
  1523.6 15.3 fusion.71
  1569.6 18.1 fusion.26
  1601.1 14.3 convolution_bitcast_fusion
  1655.4 37.8 %all-reduce.8 = (f32[2048]{0:T(1024)S(1)}, f32[128]{0:T(128)S(1)}, f32[128]{0:T(128)S(1)}, f32[2048]{0:T(1024)S(1)}) all-reduce(f32[2048]{0:T(1024)S(1)} %get-tuple-element.18, f32[128]{0:T(128)S(1)} %bitcast_reduce_fusion, f32[128]{0:T(128)S(1)} %bitcast_reduce_fusion.1, ...), channel_id=2, replica_groups=mesh['dp'=4,'expert'=8] {'dp','expert'}, use_global_device_ids=true, to_apply=%region_23.24.clone | all-reduce | flops 4352 | bytes 34816
  1701.5 91.1 %reduce-scatter.10.cloned.1.call-done = f32[64,512]{1,0:T(8,128)} async-done(((f32[2048,512]{1,0:T(8,128)}), f32[64,512]{1,0:T(8,128)}) %reduce-scatter.10.cloned.1.call-update) | async-done | bytes 131088 | tf_op jit(solution)/shard_map/reduce_scatter | solution.py:388
  1792.7 353.1 %reduce-scatter.14.cloned.1.call-done = f32[128,2048]{1,0:T(8,128)} async-done(((f32[4096,2048]{1,0:T(8,128)}), f32[128,2048]{1,0:T(8,128)}) %reduce-scatter.14.cloned.1.call-update) | async-done | bytes 1048592 | tf_op jit(solution)/shard_map/reduce_scatter | solution.py:390
  2145.8 365.0 %reduce-scatter.8.cloned.1.call-done = f32[64,4096]{1,0:T(8,128)} async-done(((f32[2048,4096]{1,0:T(8,128)}), f32[64,4096]{1,0:T(8,128)}) %reduce-scatter.8.cloned.1.call-update) | async-done | bytes 1048592 | tf_op jit(solution)/shard_map/reduce_scatter | solution.py:387
  (332 shorter events, 336.8 us)
Async XLA Ops:
  7.2 912.3 %copy-start = (bf16[1,2048,768]{2,1,0:T(8,128)(2,1)S(1)}, bf16[1,2048,768]{2,1,0:T(8,128)(2,1)}, u32[]{:S(2)}) copy-start(bf16[1,2048,768]{2,1,0:T(8,128)(2,1)} %param.28) | copy-start | bytes 9437188
  7.2 94.6 %copy-start.71 = (bf16[64,32]{0,1:T(8,128)(2,1)S(1)}, bf16[64,32]{0,1:T(8,128)(2,1)}, u32[]{:S(2)}) copy-start(bf16[64,32]{0,1:T(8,128)(2,1)} %param.27) | copy-start | bytes 12292
  7.2 144.0 %all-gather.6.cloned.1.call-start = ((), (), s32[]{:S(2)}) async-start(), calls=%async_computation.9 | async-start | bytes 2162688 | tf_op jit(solution)/shard_map/all_gather | solution.py:274
  7.9 148.5 %all-gather.8.cloned.1.call-start = ((), (), s32[]{:S(2)}) async-start(), calls=%async_computation.10 | async-start | bytes 2162688 | tf_op jit(solution)/shard_map/all_gather | solution.py:273
  8.7 235.5 %all-gather.10.cloned.1.call-start = ((), (), s32[]{:S(2)}) async-start(), calls=%async_computation.11 | async-start | bytes 17301504 | tf_op jit(solution)/shard_map/all_gather | solution.py:272
  9.4 350.0 %all-gather.12.cloned.1.call-start = ((), (), s32[]{:S(2)}) async-start(), calls=%async_computation.12 | async-start | bytes 17301504 | tf_op jit(solution)/shard_map/all_gather | solution.py:275
  57.8 186.3 %copy-start.37 = (f32[2048]{0:T(1024)}, f32[2048]{0:T(1024)S(1)}, u32[]{:S(2)}) copy-start(f32[2048]{0:T(1024)S(1)} %convert_element_type.207) | copy-start | bytes 24580
  57.8 313.5 %copy-start.53 = (f32[2048]{0:T(1024)}, f32[2048]{0:T(1024)S(1)}, u32[]{:S(2)}) copy-start(f32[2048]{0:T(1024)S(1)} %convert_element_type.218) | copy-start | bytes 24580
  77.9 65.3 %copy-start.61 = (s32[2048,1]{0,1:T(1,128)}, s32[2048,1]{0,1:T(1,128)S(1)}, u32[]{:S(2)}) copy-start(s32[2048,1]{0,1:T(1,128)S(1)} %compare_select_fusion) | copy-start | bytes 24580
  143.6 228.0 %copy-start.35 = (bf16[2048,32]{0,1:T(8,128)(2,1)}, bf16[2048,32]{0,1:T(8,128)(2,1)S(1)}, u32[]{:S(2)}) copy-start(bf16[2048,32]{0,1:T(8,128)(2,1)S(1)} %reshape.608) | copy-start | bytes 393220
  151.2 107.9 %copy-start.22 = (f32[256,64]{1,0:T(8,128)}, f32[256,64]{1,0:T(8,128)S(1)}, u32[]{:S(2)}) copy-start(f32[256,64]{1,0:T(8,128)S(1)} %get-tuple-element.61) | copy-start | bytes 196612
  151.2 107.9 %copy-start.24 = (f32[256,64]{1,0:T(8,128)}, f32[256,64]{1,0:T(8,128)S(1)}, u32[]{:S(2)}) copy-start(f32[256,64]{1,0:T(8,128)S(1)} %get-tuple-element.62) | copy-start | bytes 196612
  669.5 236.0 %all-to-all-start.2 = ((bf16[32,80,2048]{2,1,0:T(8,128)(2,1)}), bf16[32,80,2048]{2,1,0:T(8,128)(2,1)}, u32[]{:S(2)}, u32[]{:S(2)}) async-start(bf16[32,80,2048]{2,1,0:T(8,128)(2,1)} %get-tuple-element.57), calls=%async_computation.2 | async-start | bytes 20971520 | tf_op jit(solution)/shard_map/all_to_all | solution.py:249
  952.6 236.0 %all-to-all-start.1 = ((bf16[32,80,2048]{2,1,0:T(8,128)(2,1)}), bf16[32,80,2048]{2,1,0:T(8,128)(2,1)}, u32[]{:S(2)}, u32[]{:S(2)}) async-start(bf16[32,80,2048]{2,1,0:T(8,128)(2,1)} %convolution_convert_fusion), calls=%async_computation.1 | async-start | bytes 20971520 | tf_op jit(solution)/shard_map/all_to_all | solution.py:247
  986.4 206.0 %copy-start.62 = (s32[2048,1]{0,1:T(1,128)S(1)}, s32[2048,1]{0,1:T(1,128)}, u32[]{:S(2)}) copy-start(s32[2048,1]{0,1:T(1,128)} %copy-done.61) | copy-start | bytes 24580
  986.4 206.0 %copy-start.64 = (f32[4,8,256]{2,1,0:T(8,128)S(1)}, f32[4,8,256]{2,1,0:T(8,128)}, u32[]{:S(2)}) copy-start(f32[4,8,256]{2,1,0:T(8,128)} %copy-done.63) | copy-start | bytes 98308
  1188.6 241.2 %all-to-all-start.3 = ((bf16[32,80,2048]{2,1,0:T(8,128)(2,1)}), bf16[32,80,2048]{2,1,0:T(8,128)(2,1)}, u32[]{:S(2)}, u32[]{:S(2)}) async-start(bf16[32,80,2048]{2,1,0:T(8,128)(2,1)} %add_convert_fusion), calls=%async_computation.3 | async-start | bytes 20971520 | tf_op jit(solution)/shard_map/all_to_all | solution.py:250
  1192.3 507.7 %reduce-scatter.16.cloned.1.call-start = ((), (), s32[]{:S(2)}) async-start(), calls=%async_computation.17 | async-start | bytes 1081344
  1225.7 475.8 %reduce-scatter.12.cloned.1.call-start = ((), (), s32[]{:S(2)}) async-start(), calls=%async_computation.15 | async-start | bytes 4325376 | tf_op jit(solution)/shard_map/reduce_scatter | solution.py:389
  1510.0 282.6 %reduce-scatter.10.cloned.1.call-start = ((), (), s32[]{:S(2)}) async-start(), calls=%async_computation.14 | async-start | bytes 4325376 | tf_op jit(solution)/shard_map/reduce_scatter | solution.py:388
  1522.0 623.8 %reduce-scatter.14.cloned.1.call-start = ((), (), s32[]{:S(2)}) async-start(), calls=%async_computation.16 | async-start | bytes 34603008 | tf_op jit(solution)/shard_map/reduce_scatter | solution.py:390
  1538.9 971.9 %reduce-scatter.8.cloned.1.call-start = ((), (), s32[]{:S(2)}) async-start(), calls=%async_computation.13 | async-start | bytes 34603008 | tf_op jit(solution)/shard_map/reduce_scatter | solution.py:387
  1653.0 42.6 %copy-start.76 = (f32[256]{0:T(256)S(1)}, f32[256]{0:T(256)}, u32[]{:S(2)}) copy-start(f32[256]{0:T(256)} %get-tuple-element.63) | copy-start | bytes 3076
  1653.0 857.8 %copy-start.1 = (bf16[1,2048,768]{2,1,0:T(8,128)(2,1)S(1)}, bf16[1,2048,768]{2,1,0:T(8,128)(2,1)}, u32[]{:S(2)}) copy-start(bf16[1,2048,768]{2,1,0:T(8,128)(2,1)} %param.28) | copy-start | bytes 9437188
  (75 other events, 486.7 us)
Sparse Core Ops, SparseCore 0:
  10.9 59.0 all-gather.5
  72.8 55.0 all-gather.7
  130.7 113.3 all-gather.9
  246.9 112.5 all-gather.11
  1225.8 162.7 reduce-scatter.15
  1510.1 140.6 reduce-scatter.11
  1653.6 138.9 reduce-scatter.9
  1795.5 350.2 reduce-scatter.13
  2148.7 362.0 reduce-scatter.7
where the time goes:
time: 2530 us; the launch traced here: 2520 us
  waiting for transfers between devices  1600 us (63%)
  blocking collectives  353 us (14%)
  matrix products  248 us (10%)
  local copies, waits for them, and re-layouts  172 us (7%)
  other arithmetic  120 us (5%)
    all_to_all x3, waiting for transfers between devices, move_rows(): lax.all_to_all(row_block, ('dp', 'expert'), split_axis=0, concat_axis=0,...  624 us
    reduce_scatter x1, waiting for transfers between devices, per_device(): lax.psum_scatter(grad_w_query, ('dp', 'expert'), scatter_dimension=0, til...  365 us
    reduce_scatter x1, waiting for transfers between devices, per_device(): lax.psum_scatter(grad_w_output, ('dp', 'expert'), scatter_dimension=0, ti...  353 us
    all_to_all x1, blocking collectives, move_rows(): lax.all_to_all(row_block, ('dp', 'expert'), split_axis=0, concat_axis=0,...  231 us
    reduce_scatter x1, waiting for transfers between devices, per_device(): lax.psum_scatter(grad_w_key, ('dp', 'expert'), scatter_dimension=0, tiled...  91.1 us
    all_gather x1, waiting for transfers between devices, per_device(): lax.all_gather(w_output, ('dp', 'expert'), axis=0, tiled=True)  86.8 us
    unnamed x2, blocking collectives  80.1 us
    all_gather x1, waiting for transfers between devices, per_device(): lax.all_gather(w_query, ('dp', 'expert'), axis=0, tiled=True)  74.5 us
  transfers between devices with their start and end apart: 12, of which 8 were waited for; matrix products, arithmetic and copies ran while one was open for 16% of the time, Pallas kernels for 0%

commit v1 on v0

--- a/solution.py
+++ b/solution.py
@@ -1,9 +1,17 @@
+import functools
 import math
 
 import jax
 import jax.numpy as jnp
 from jax import lax
+from jax.experimental import pallas as pl
+from jax.experimental.pallas import tpu as pltpu
 from jax.sharding import PartitionSpec as P
+
+F32, BF16 = jnp.float32, jnp.bfloat16
+MESH = pl.DeviceIdType.MESH
+VMEM_LIMIT = 63 * 1024 * 1024
+
 
 HEADS = 32
 KV_HEADS = 4
@@ -250,7 +258,7 @@
     return lax.all_to_all(row_block, ("dp", "expert"), split_axis=0, concat_axis=0, tiled=True)
 
 
-def per_device(
+def per_device_exchange(
     hidden_in,
     segment_ids,
     expert_ids,
@@ -423,6 +431,719 @@
     )
 
 
+def place():
+    z = lax.axis_index("dp")
+    e = lax.axis_index("expert")
+    return z, e
+
+
+def line_order(z, nz, j):
+    near = jnp.minimum(z, nz - 1 - z)
+    step = (j + 1) // 2
+    zigzag = z + (step if j % 2 == 0 else -step)
+    tail = jnp.where(z < nz - 1 - z, j, nz - 1 - j)
+    return jnp.where(j <= 2 * near, zigzag, tail)
+
+
+def greet(z, e, nz):
+    barrier = pltpu.get_barrier_semaphore()
+    for mate in (e ^ 1, e ^ 2, e ^ 4):
+        pl.semaphore_signal(barrier, inc=1, device_id=(z, mate), device_id_type=MESH)
+
+    @pl.when(z > 0)
+    def _():
+        pl.semaphore_signal(barrier, inc=1, device_id=(z - 1, e), device_id_type=MESH)
+
+    @pl.when(z < nz - 1)
+    def _():
+        pl.semaphore_signal(barrier, inc=1, device_id=(z + 1, e), device_id_type=MESH)
+
+    ends = (z > 0).astype(jnp.int32) + (z < nz - 1).astype(jnp.int32)
+    pl.semaphore_wait(barrier, 3 + ends)
+
+
+class Gather:
+    Z, XA, XB, XF, YB, YA, YF, P0, PXA, PXB, PYB, PYA, PDB, PDA = range(14)
+
+    def __init__(self, nz, shards, outs, send, recv, local):
+        self.nz, self.shards, self.outs = nz, shards, outs
+        self.send, self.recv, self.local = send, recv, local
+        self.z, self.e = place()
+        self.x, self.y, self.p = self.e ^ 2, self.e ^ 4, self.e ^ 1
+        self.d = self.e ^ 6
+
+    def at(self, i, zz, ee, half):
+        ref = self.outs[i].at[zz, ee]
+        return ref if half is None else ref.at[half]
+
+    def own(self, i, half):
+        ref = self.shards[i]
+        return ref if half is None else ref.at[half]
+
+    def copy(self, i, kind, zz, ee, half, dev, mine=False):
+        dst = self.at(i, zz, ee, half)
+        return pltpu.make_async_remote_copy(
+            src_ref=self.own(i, half) if mine else dst,
+            dst_ref=dst,
+            send_sem=self.send.at[i, zz, kind],
+            recv_sem=self.recv.at[i, zz, kind],
+            device_id=dev,
+            device_id_type=MESH,
+        )
+
+    def start(self, kind, zz, ee, half, dev, mine=False):
+        for i in range(len(self.outs)):
+            self.copy(i, kind, zz, ee, half, dev, mine).start()
+
+    def arrived(self, kind, zz, ee, half):
+        for i in range(len(self.outs)):
+            self.copy(i, kind, zz, ee, half, (self.z, self.e)).wait_recv()
+
+    def sent(self, kind, zz, ee, half, mine=False):
+        for i in range(len(self.outs)):
+            self.copy(i, kind, zz, ee, half, (self.z, self.e), mine).wait_send()
+
+    def zz(self, j):
+        return line_order(self.z, self.nz, j)
+
+    def launch(self, j):
+        z, e, nz = self.z, self.e, self.nz
+        zz = self.zz(j)
+        mine = j == 0
+        if mine:
+            for i in range(len(self.outs)):
+                pltpu.make_async_copy(self.shards[i], self.at(i, z, e, None), self.local.at[i]).start()
+        else:
+            self.arrived(self.Z, zz, e, None)
+
+        @pl.when(jnp.logical_and(zz <= z, z < nz - 1))
+        def _():
+            self.start(self.Z, zz, e, None, (z + 1, e), mine)
+
+        if mine:
+            @pl.when(z > 0)
+            def _():
+                for i in range(len(self.outs)):
+                    pltpu.make_async_remote_copy(
+                        src_ref=self.own(i, None), dst_ref=self.at(i, z, e, None),
+                        send_sem=self.local.at[len(self.outs) + i],
+                        recv_sem=self.recv.at[i, z, self.Z],
+                        device_id=(z - 1, e), device_id_type=MESH).start()
+        else:
+            @pl.when(jnp.logical_and(zz > z, z > 0))
+            def _():
+                self.start(self.Z, zz, e, None, (z - 1, e))
+
+        self.start(self.XA, zz, e, 0, (z, self.x), mine)
+        self.start(self.YB, zz, e, 1, (z, self.y), mine)
+        self.start(self.XB, zz, e, 1, (z, self.x), mine)
+        self.start(self.YA, zz, e, 0, (z, self.y), mine)
+        self.start(self.P0, zz, e, None, (z, self.p), mine)
+
+    def relay(self, j):
+        z = self.z
+        zz = self.zz(j)
+        self.arrived(self.XA, zz, self.x, 0)
+        self.start(self.YF, zz, self.x, 0, (z, self.y))
+        self.start(self.PXA, zz, self.x, 0, (z, self.p))
+        self.arrived(self.YB, zz, self.y, 1)
+        self.start(self.XF, zz, self.y, 1, (z, self.x))
+        self.start(self.PYB, zz, self.y, 1, (z, self.p))
+
+    def finish(self, j):
+        z = self.z
+        zz = self.zz(j)
+        self.arrived(self.XB, zz, self.x, 1)
+        self.start(self.PXB, zz, self.x, 1, (z, self.p))
+        self.arrived(self.YA, zz, self.y, 0)
+        self.start(self.PYA, zz, self.y, 0, (z, self.p))
+        self.arrived(self.XF, zz, self.d, 1)
+        self.start(self.PDB, zz, self.d, 1, (z, self.p))
+        self.arrived(self.YF, zz, self.d, 0)
+        self.start(self.PDA, zz, self.d, 0, (z, self.p))
+
+    def shared(self, j):
+        zz = self.zz(j)
+        p = self.p
+        self.arrived(self.P0, zz, p, None)
+        self.arrived(self.PXA, zz, p ^ 2, 0)
+        self.arrived(self.PXB, zz, p ^ 2, 1)
+        self.arrived(self.PYA, zz, p ^ 4, 0)
+        self.arrived(self.PYB, zz, p ^ 4, 1)
+        self.arrived(self.PDA, zz, p ^ 6, 0)
+        self.arrived(self.PDB, zz, p ^ 6, 1)
+
+    def drain(self, j):
+        z, e, nz = self.z, self.e, self.nz
+        zz = self.zz(j)
+        mine = j == 0
+
+        @pl.when(jnp.logical_and(zz <= z, z < nz - 1))
+        def _():
+            self.sent(self.Z, zz, e, None, mine)
+
+        if mine:
+            for i in range(len(self.outs)):
+                pltpu.make_async_copy(self.shards[i], self.at(i, z, e, None), self.local.at[i]).wait()
+
+            @pl.when(z > 0)
+            def _():
+                for i in range(len(self.outs)):
+                    pltpu.make_async_remote_copy(
+                        src_ref=self.own(i, None), dst_ref=self.at(i, z, e, None),
+                        send_sem=self.local.at[len(self.outs) + i],
+                        recv_sem=self.recv.at[i, z, self.Z],
+                        device_id=(z, e), device_id_type=MESH).wait_send()
+        else:
+            @pl.when(jnp.logical_and(zz > z, z > 0))
+            def _():
+                self.sent(self.Z, zz, e, None)
+
+        self.sent(self.XA, zz, e, 0, mine)
+        self.sent(self.XB, zz, e, 1, mine)
+        self.sent(self.YA, zz, e, 0, mine)
+        self.sent(self.YB, zz, e, 1, mine)
+        self.sent(self.P0, zz, e, None, mine)
+        self.sent(self.YF, zz, self.x, 0)
+        self.sent(self.XF, zz, self.y, 1)
+        self.sent(self.PXA, zz, self.x, 0)
+        self.sent(self.PXB, zz, self.x, 1)
+        self.sent(self.PYA, zz, self.y, 0)
+        self.sent(self.PYB, zz, self.y, 1)
+        self.sent(self.PDA, zz, self.d, 0)
+        self.sent(self.PDB, zz, self.d, 1)
+
+
+def gather_kernel(nz, count, *refs):
+    shards, outs = refs[:count], refs[count : 2 * count]
+    send, recv, local = refs[2 * count :]
+    z, e = place()
+    greet(z, e, nz)
+    g = Gather(nz, shards, outs, send, recv, local)
+    for j in range(nz):
+        g.launch(j)
+        g.relay(j)
+        if j > 0:
+            g.finish(j - 1)
+    g.finish(nz - 1)
+    for j in range(nz):
+        g.shared(j)
+    for j in range(nz):
+        g.drain(j)
+
+
+def gather_scratch(nz, count):
+    return [
+        pltpu.SemaphoreType.DMA((count, nz, 14)),
+        pltpu.SemaphoreType.DMA((count, nz, 14)),
+        pltpu.SemaphoreType.DMA((2 * count,)),
+    ]
+
+
+def gather_all(arrays, collective_id):
+    nz, width = lax.axis_size("dp"), lax.axis_size("expert")
+    count = len(arrays)
+    halves = [a.reshape((2, a.shape[0] // 2) + a.shape[1:]) for a in arrays]
+    outs = pl.pallas_call(
+        functools.partial(gather_kernel, nz, count),
+        out_shape=[jax.ShapeDtypeStruct((nz, width) + h.shape, h.dtype) for h in halves],
+        in_specs=[pl.BlockSpec(memory_space=pltpu.VMEM)] * count,
+        out_specs=[pl.BlockSpec(memory_space=pl.ANY)] * count,
+        scratch_shapes=gather_scratch(nz, count),
+        compiler_params=pltpu.CompilerParams(
+            collective_id=collective_id, has_side_effects=True, vmem_limit_bytes=VMEM_LIMIT
+        ),
+        name="gather_all",
+    )(*halves)
+    return [
+        o.reshape((nz * width * a.shape[0],) + a.shape[1:]) for o, a in zip(outs, arrays)
+    ]
+
+
+def accumulate(dst, src):
+    rows = dst.shape[0]
+    block = 32 if rows % 32 == 0 else rows
+
+    def body(r, _):
+        at = pl.ds(pl.multiple_of(r * block, block), block)
+        dst[at, :] = dst[at, :] + src[at, :]
+        return 0
+
+    lax.fori_loop(0, rows // block, body, 0)
+
+
+class Scatter:
+    YD, YO, XD, XO, XA, YB, Z, ZB = range(4, 12)
+
+    def __init__(self, nz, terms, outs, sums, temps, from_y, from_x, last_x, last_y, from_z, send, recv, local):
+        self.nz, self.terms, self.outs = nz, terms, outs
+        self.sums, self.temps = sums, temps
+        self.from_y, self.from_x, self.last_x, self.last_y, self.from_z = from_y, from_x, last_x, last_y, from_z
+        self.send, self.recv, self.local = send, recv, local
+        self.count = len(terms)
+        self.z, self.e = place()
+        self.core = self.e % 2
+        self.chip = self.e // 2
+        self.x, self.y, self.p = self.e ^ 2, self.e ^ 4, self.e ^ 1
+        self.chips = (self.chip ^ 3, self.chip ^ 1, self.chip ^ 2, self.chip)
+
+    def zz(self, j):
+        return line_order(self.z, self.nz, self.nz - 1 - j)
+
+    def remote(self, i, kind, zz, src, dst, dev):
+        return pltpu.make_async_remote_copy(
+            src_ref=src, dst_ref=dst, send_sem=self.send.at[i, zz, kind], recv_sem=self.recv.at[i, zz, kind],
+            device_id=dev, device_id_type=MESH)
+
+    def pair(self, i, j, q):
+        zz, chip = self.zz(j), self.chips[q]
+        return self.remote(i, q, zz, self.terms[i].at[zz, chip * 2 + (1 - self.core)], self.sums[i].at[zz, q],
+                           (self.z, self.p))
+
+    def load(self, i, j, q):
+        slot = q % 2
+        return pltpu.make_async_copy(
+            self.terms[i].at[self.zz(j), self.chips[q] * 2 + self.core], self.temps[i].at[slot], self.local.at[i, slot])
+
+    def begin(self):
+        for j in range(self.nz):
+            for q in range(4):
+                for i in range(self.count):
+                    self.pair(i, j, q).start()
+        for i in range(self.count):
+            self.load(i, 0, 0).start()
+
+    def yd(self, i, zz):
+        return self.remote(i, self.YD, zz, self.sums[i].at[zz, 0, 0], self.from_y[i].at[zz, 0], (self.z, self.y))
+
+    def yo(self, i, zz):
+        return self.remote(i, self.YO, zz, self.sums[i].at[zz, 2, 0], self.from_y[i].at[zz, 1], (self.z, self.y))
+
+    def xd(self, i, zz):
+        return self.remote(i, self.XD, zz, self.sums[i].at[zz, 0, 1], self.from_x[i].at[zz, 0], (self.z, self.x))
+
+    def xo(self, i, zz):
+        return self.remote(i, self.XO, zz, self.sums[i].at[zz, 1, 1], self.from_x[i].at[zz, 1], (self.z, self.x))
+
+    def xa(self, i, zz):
+        return self.remote(i, self.XA, zz, self.sums[i].at[zz, 1, 0], self.last_x[i].at[zz], (self.z, self.x))
+
+    def yb(self, i, zz):
+        return self.remote(i, self.YB, zz, self.sums[i].at[zz, 2, 1], self.last_y[i].at[zz], (self.z, self.y))
+
+    def up(self, i, zz):
+        return self.remote(i, self.Z, zz, self.sums[i].at[zz, 3], self.from_z[i].at[zz], (self.z + 1, self.e))
+
+    def down(self, i, zz):
+        return self.remote(i, self.Z, zz, self.sums[i].at[zz, 3], self.from_z[i].at[zz], (self.z - 1, self.e))
+
+    def down_last(self, i, zz):
+        return self.remote(i, self.ZB, zz, self.sums[i].at[zz, 3], self.from_z[i].at[self.nz], (self.z - 1, self.e))
+
+    def first(self, j):
+        zz = self.zz(j)
+        for q in range(4):
+            for i in range(self.count):
+                if q < 3:
+                    self.load(i, j, q + 1).start()
+                elif j < self.nz - 1:
+                    self.load(i, j + 1, 0).start()
+                self.pair(i, j, q).wait_recv()
+                self.load(i, j, q).wait()
+                for h in range(2):
+                    accumulate(self.sums[i].at[zz, q, h], self.temps[i].at[q % 2, h])
+                if q == 0:
+                    self.yd(i, zz).start()
+                    self.xd(i, zz).start()
+                if q == 1:
+                    self.xo(i, zz).start()
+                if q == 2:
+                    self.yo(i, zz).start()
+
+    def second(self, j):
+        zz = self.zz(j)
+        for i in range(self.count):
+            self.yd(i, zz).wait_recv()
+            accumulate(self.sums[i].at[zz, 1, 0], self.from_y[i].at[zz, 0])
+            self.xa(i, zz).start()
+            self.xd(i, zz).wait_recv()
+            accumulate(self.sums[i].at[zz, 2, 1], self.from_x[i].at[zz, 0])
+            self.yb(i, zz).start()
+
+    def third(self, j):
+        z, nz = self.z, self.nz
+        zz = self.zz(j)
+        for i in range(self.count):
+            self.yo(i, zz).wait_recv()
+            accumulate(self.sums[i].at[zz, 3, 0], self.from_y[i].at[zz, 1])
+            self.xo(i, zz).wait_recv()
+            accumulate(self.sums[i].at[zz, 3, 1], self.from_x[i].at[zz, 1])
+            self.xa(i, zz).wait_recv()
+            accumulate(self.sums[i].at[zz, 3, 0], self.last_x[i].at[zz])
+            self.yb(i, zz).wait_recv()
+            accumulate(self.sums[i].at[zz, 3, 1], self.last_y[i].at[zz])
+            if j < nz - 1:
+                @pl.when(jnp.logical_or(jnp.logical_and(zz > z, z > 0), jnp.logical_and(zz < z, z < nz - 1)))
+                def _():
+                    self.up(i, zz).wait_recv()
+                    for h in range(2):
+                        accumulate(self.sums[i].at[zz, 3, h], self.from_z[i].at[zz, h])
+
+                @pl.when(zz > z)
+                def _():
+                    self.up(i, zz).start()
+
+                @pl.when(zz < z - 1)
+                def _():
+                    self.down(i, zz).start()
+
+                @pl.when(zz == z - 1)
+                def _():
+                    self.down_last(i, zz).start()
+            else:
+                @pl.when(z > 0)
+                def _():
+                    self.up(i, z).wait_recv()
+                    for h in range(2):
+                        accumulate(self.sums[i].at[z, 3, h], self.from_z[i].at[z, h])
+
+                @pl.when(z < nz - 1)
+                def _():
+                    self.down_last(i, z).wait_recv()
+                    for h in range(2):
+                        accumulate(self.sums[i].at[z, 3, h], self.from_z[i].at[nz, h])
+
+                self.outs[i][...] = self.sums[i][z, 3].astype(self.outs[i].dtype)
+
+    def drain(self, j):
+        z, nz = self.z, self.nz
+        zz = self.zz(j)
+        for i in range(self.count):
+            for q in range(4):
+                self.pair(i, j, q).wait_send()
+            for c in (self.yd, self.yo, self.xd, self.xo, self.xa, self.yb):
+                c(i, zz).wait_send()
+            if j < nz - 1:
+                @pl.when(zz > z)
+                def _():
+                    self.up(i, zz).wait_send()
+
+                @pl.when(zz < z - 1)
+                def _():
+                    self.down(i, zz).wait_send()
+
+                @pl.when(zz == z - 1)
+                def _():
+                    self.down_last(i, zz).wait_send()
+
+
+def scatter_kernel(nz, count, *refs):
+    groups = [refs[k * count : (k + 1) * count] for k in range(9)]
+    send, recv, local = refs[9 * count :]
+    z, e = place()
+    greet(z, e, nz)
+    s = Scatter(nz, *groups, send, recv, local)
+    s.begin()
+    for j in range(nz):
+        s.first(j)
+        if j > 0:
+            s.second(j - 1)
+        if j > 1:
+            s.third(j - 2)
+    s.second(nz - 1)
+    if nz > 1:
+        s.third(nz - 2)
+    s.third(nz - 1)
+    for j in range(nz):
+        s.drain(j)
+
+
+def scatter_sum(arrays, collective_id):
+    nz, width = lax.axis_size("dp"), lax.axis_size("expert")
+    count = len(arrays)
+    devices = nz * width
+    terms = [a.reshape(nz, width, 2, a.shape[0] // (2 * devices), a.shape[1]) for a in arrays]
+    chips = width // 2
+    scratch = []
+    shapes = [t.shape[3:] for t in terms]
+    kinds = [a.dtype for a in arrays]
+    for lead in ((nz, chips, 2), (2, 2), (nz, 2), (nz, 2), (nz,), (nz,), (nz + 1, 2)):
+        scratch += [pltpu.VMEM(lead + s, k) for s, k in zip(shapes, kinds)]
+    outs = pl.pallas_call(
+        functools.partial(scatter_kernel, nz, count),
+        out_shape=[jax.ShapeDtypeStruct((2,) + s, jnp.float32) for s in shapes],
+        in_specs=[pl.BlockSpec(memory_space=pl.ANY)] * count,
+        out_specs=[pl.BlockSpec(memory_space=pltpu.VMEM)] * count,
+        scratch_shapes=scratch
+        + [
+            pltpu.SemaphoreType.DMA((count, nz, 12)),
+            pltpu.SemaphoreType.DMA((count, nz, 12)),
+            pltpu.SemaphoreType.DMA((count, 2)),
+        ],
+        compiler_params=pltpu.CompilerParams(
+            collective_id=collective_id, has_side_effects=True, vmem_limit_bytes=VMEM_LIMIT
+        ),
+        name="scatter_sum",
+    )(*terms)
+    return [o.reshape(2 * s[0], s[1]) for o, s in zip(outs, shapes)]
+
+
+def mm(a, b, da=1, db=0):
+    return lax.dot_general(a, b, (((da,), (db,)), ((), ())), preferred_element_type=F32)
+
+
+def expert_kernel(group, cap, x_ref, g_ref, gate_ref, rank_ref, wg_ref, wu_ref, wd_ref,
+                  y_ref, r_ref, gg_ref, rows_ref, down_ref, act_ref, gp_ref, up_ref, cot_ref):
+    length, width = x_ref.shape[1:]
+    slot = lax.broadcasted_iota(jnp.int32, (cap, length), 0).astype(F32)
+    picks, gates = [], []
+    for s in range(group):
+        hit = slot == rank_ref[s]
+        pick = hit.astype(BF16)
+        picks.append(pick)
+        gate = jnp.sum(jnp.where(hit, gate_ref[s], 0.0), 1, keepdims=True)
+        gates.append(gate)
+        at = pl.ds(s * cap, cap)
+        rows_ref[at, :] = mm(pick, x_ref[s]).astype(BF16)
+        cot = mm(pick, g_ref[s])
+        cot_ref[at, :] = cot.astype(BF16)
+        down_ref[at, :] = (gate * cot).astype(BF16)
+    gate_all = jnp.concatenate(gates, 0)
+    rows = rows_ref[...]
+    pre_gate = mm(rows, wg_ref[...])
+    pre_up = mm(rows, wu_ref[...])
+    sig = jax.nn.sigmoid(pre_gate)
+    silu = pre_gate * sig
+    act_ref[...] = (silu * pre_up).astype(BF16)
+    act_grad = mm(down_ref[...], wd_ref[...], 1, 1)
+    gp_ref[...] = (act_grad * pre_up * sig * (1.0 + pre_gate * (1.0 - sig))).astype(BF16)
+    up_ref[...] = (act_grad * silu).astype(BF16)
+    tile = 512
+    gg = jnp.zeros((group * cap, 1), F32)
+    for n in range(width // tile):
+        cols = pl.ds(n * tile, tile)
+        out = mm(act_ref[...], wd_ref[:, cols]).astype(BF16).astype(F32)
+        gg = gg + jnp.sum(out * cot_ref[:, cols].astype(F32), 1, keepdims=True)
+        out = (out * gate_all).astype(BF16)
+        back = (mm(gp_ref[...], wg_ref[cols, :], 1, 1) + mm(up_ref[...], wu_ref[cols, :], 1, 1)).astype(BF16)
+        for s in range(group):
+            part = slice(s * cap, (s + 1) * cap)
+            y_ref[s, :, cols] = mm(picks[s], out[part], 0, 0).astype(BF16)
+            r_ref[s, :, cols] = mm(picks[s], back[part], 0, 0).astype(BF16)
+    for s in range(group):
+        gg_ref[s] = jnp.sum(picks[s].astype(F32) * gg[s * cap : (s + 1) * cap], 0, keepdims=True)
+
+
+def experts(x, g, gate, rank, wg, wu, wd, cap, group):
+    devices, length, width = x.shape
+    ff = wg.shape[1]
+    rows = devices * cap
+    step = group * cap
+    block = lambda *tail: pl.BlockSpec((group,) + tail, lambda i: (i,) + (0,) * len(tail))
+    flat = lambda n: pl.BlockSpec((step, n), lambda i: (i, 0))
+    whole = lambda a: pl.BlockSpec(a.shape, lambda i: (0, 0), pipeline_mode=pl.Buffered(1))
+    return pl.pallas_call(
+        functools.partial(expert_kernel, group, cap),
+        grid=(devices // group,),
+        in_specs=[block(length, width), block(length, width), block(1, length), block(1, length),
+                  whole(wg), whole(wu), whole(wd)],
+        out_specs=[block(length, width), block(length, width), block(1, length),
+                   flat(width), flat(width), flat(ff), flat(ff), flat(ff)],
+        out_shape=[
+            jax.ShapeDtypeStruct((devices, length, width), BF16),
+            jax.ShapeDtypeStruct((devices, length, width), BF16),
+            jax.ShapeDtypeStruct((devices, 1, length), F32),
+            jax.ShapeDtypeStruct((rows, width), BF16),
+            jax.ShapeDtypeStruct((rows, width), BF16),
+            jax.ShapeDtypeStruct((rows, ff), BF16),
+            jax.ShapeDtypeStruct((rows, ff), BF16),
+            jax.ShapeDtypeStruct((rows, ff), BF16),
+        ],
+        scratch_shapes=[pltpu.VMEM((step, width), BF16)],
+        compiler_params=pltpu.CompilerParams(vmem_limit_bytes=VMEM_LIMIT, dimension_semantics=("arbitrary",)),
+        name="experts",
+    )(x, g, gate, rank, wg, wu, wd)
+
+
+def pack_columns(columns, rows, lanes, dtype):
+    parts = [c.astype(dtype) for c in columns]
+    used = sum(c.shape[1] for c in parts)
+    return jnp.concatenate(parts + [jnp.zeros((rows, lanes - used), dtype)], 1)
+
+
+def spread(vector, devices, rows):
+    blocks = vector.reshape(devices, -1)
+    return jnp.pad(blocks, ((0, 0), (0, rows - blocks.shape[1]))).reshape(devices * rows, 1)
+
+
+def per_device_gather(
+    hidden_in,
+    segment_ids,
+    expert_ids,
+    attn_gain,
+    query_gain,
+    key_gain,
+    w_query,
+    w_key,
+    w_value,
+    w_output,
+    mlp_gain,
+    w_router,
+    w_gate,
+    w_up,
+    w_down,
+    out_grad,
+):
+    devices = lax.axis_size(("dp", "expert"))
+    me = lax.axis_index(("dp", "expert"))
+    length, choices = expert_ids.shape
+    width = hidden_in.shape[1]
+    experts_total = devices
+    capacity = 5 * length * choices // (4 * experts_total)
+    query_cols, key_cols = w_query.shape[1], w_key.shape[1]
+    rows = w_query.shape[0]
+    head_rows = query_gain.shape[0]
+
+    column = lambda v: jnp.pad(v, (0, rows - v.shape[0]))[:, None]
+    lanes = 128 * pl.cdiv(experts_total + 4, 128)
+    small = pack_columns(
+        [w_router, column(attn_gain), column(mlp_gain), column(query_gain), column(key_gain)], rows, lanes, BF16
+    )
+    w_mixed = jnp.concatenate([w_query, w_key, w_value], 1)
+    w_mixed, w_out, small = gather_all([w_mixed, w_output, small], 1)
+    router = small[:, :experts_total]
+    attn_gain, mlp_gain = small[:, experts_total], small[:, experts_total + 1]
+    heads_of = small.reshape(devices, rows, lanes)[:, :head_rows]
+    query_gain = heads_of[:, :, experts_total + 2].reshape(-1)
+    key_gain = heads_of[:, :, experts_total + 3].reshape(-1)
+
+    group_size = HEADS // KV_HEADS
+    plain_in = hidden_in.astype(F32)
+    inv_attn = rms_scale(plain_in)
+    normed_attn = (plain_in * inv_attn * attn_gain).astype(BF16)
+    mixed = jnp.dot(normed_attn, w_mixed, preferred_element_type=F32)
+    query_raw = mixed[:, :query_cols].reshape(length, HEADS, HEAD_DIM)
+    key_raw = mixed[:, query_cols : query_cols + key_cols].reshape(length, KV_HEADS, HEAD_DIM)
+    value_rows = mixed[:, query_cols + key_cols :].astype(BF16).reshape(length, KV_HEADS, HEAD_DIM)
+    query_scale = rms_scale(query_raw)
+    key_scale = rms_scale(key_raw)
+    cosine_table, sine_table = rope_tables(jnp.arange(length) % TOK_DEV, HEAD_DIM)
+    query_rot = rotate(query_raw * query_scale * query_gain, cosine_table, sine_table).astype(BF16)
+    query_rot = query_rot.reshape(length, KV_HEADS, group_size, HEAD_DIM)
+    key_rot = rotate(key_raw * key_scale * key_gain, cosine_table, sine_table).astype(BF16)
+    position = jnp.arange(length)
+    allowed = (segment_ids[:, None] == segment_ids[None, :]) & (position[None, :] <= position[:, None])
+    attended, log_totals = attend(query_rot, key_rot, value_rows, allowed)
+    attended = attended.reshape(length, HEADS * HEAD_DIM)
+    residual = plain_in + jnp.dot(attended, w_out, preferred_element_type=F32)
+
+    inv_mlp = rms_scale(residual)
+    normed_mlp = (residual * inv_mlp * mlp_gain).astype(BF16)
+    logits = jnp.dot(normed_mlp, router, preferred_element_type=F32)
+    chosen = jnp.any(expert_ids[:, :, None] == jnp.arange(experts_total)[None, None, :], 1)
+    raised = jnp.where(chosen, jnp.exp(logits), 0.0)
+    gate = raised / jnp.sum(raised, -1, keepdims=True)
+    not_after = (position[None, :] <= position[:, None]).astype(BF16)
+    rank = jnp.dot(not_after, chosen.astype(BF16), preferred_element_type=F32) - 1.0
+    rank = jnp.where(chosen, rank, -1.0)
+    gate_high = lax.reduce_precision(gate, 8, 7)
+    table = jnp.concatenate([gate_high, gate - gate_high, rank], 1).T.astype(BF16)
+
+    all_rows, all_tables = gather_all([normed_mlp, table], 2)
+    (all_grads,) = gather_all([out_grad], 3)
+    mine = lax.dynamic_index_in_dim(
+        all_tables.reshape(devices, 3, experts_total, length), me, 2, keepdims=False
+    ).astype(F32)
+    cube = (devices, length, width)
+    y_terms, r_terms, gate_terms, rows_in, down_in, act, gate_pre_grad, up_pre_grad = experts(
+        all_rows.reshape(cube), all_grads.reshape(cube), mine[:, :1] + mine[:, 1:2], mine[:, 2:],
+        w_gate[0], w_up[0], w_down[0], capacity, 4,
+    )
+    is_me = (jnp.arange(experts_total) == me).astype(F32)
+    gate_terms = (gate_terms * is_me[None, :, None]).reshape(devices * experts_total, length)
+    row_grad_sum, gate_grad = scatter_sum([r_terms.reshape(devices * length, width), gate_terms], 4)
+    (mixed_out,) = scatter_sum([y_terms.reshape(devices * length, width)], 5)
+    block_out = residual + mixed_out
+    grad_w_down = jnp.dot(act.T, down_in, preferred_element_type=F32)[None]
+    grad_w_gate = jnp.dot(rows_in.T, gate_pre_grad, preferred_element_type=F32)[None]
+    grad_w_up = jnp.dot(rows_in.T, up_pre_grad, preferred_element_type=F32)[None]
+
+    gate_grad = gate_grad.T
+    sel_grad = gate * (gate_grad - jnp.sum(gate * gate_grad, -1, keepdims=True))
+    logit_grad = jnp.where(chosen, sel_grad, 0.0).astype(BF16)
+    grad_w_router = jnp.dot(normed_mlp.T, logit_grad, preferred_element_type=F32)
+    normed_mlp_grad = row_grad_sum + jnp.dot(logit_grad, router.T, preferred_element_type=F32)
+    grad_mlp_gain = jnp.sum(normed_mlp_grad * residual * inv_mlp, 0)
+    residual_grad = out_grad.astype(F32) + norm_grad(normed_mlp_grad, residual, inv_mlp, mlp_gain)
+
+    branch_grad = residual_grad.astype(BF16)
+    grad_w_output = jnp.dot(attended.T, branch_grad, preferred_element_type=F32).astype(BF16)
+    attended_grad = jnp.dot(branch_grad, w_out.T, preferred_element_type=F32).astype(BF16)
+    attended_grad = attended_grad.reshape(length, KV_HEADS, group_size, HEAD_DIM)
+    query_rot_grad, key_rot_grad, value_sum_grad = attend_grad(
+        query_rot, key_rot, value_rows, allowed, log_totals, attended_grad
+    )
+    query_normed_grad = unrotate(query_rot_grad.reshape(length, HEADS, HEAD_DIM), cosine_table, sine_table)
+    key_normed_grad = unrotate(key_rot_grad, cosine_table, sine_table)
+    grad_query_gain = jnp.sum(query_normed_grad * query_raw * query_scale, (0, 1))
+    grad_key_gain = jnp.sum(key_normed_grad * key_raw * key_scale, (0, 1))
+    query_grad = norm_grad(query_normed_grad, query_raw, query_scale, query_gain).astype(BF16)
+    key_grad = norm_grad(key_normed_grad, key_raw, key_scale, key_gain).astype(BF16)
+    mixed_grad = jnp.concatenate(
+        [
+            query_grad.reshape(length, query_cols),
+            key_grad.reshape(length, key_cols),
+            value_sum_grad.astype(BF16).reshape(length, key_cols),
+        ],
+        1,
+    )
+    grad_w_mixed = jnp.dot(normed_attn.T, mixed_grad, preferred_element_type=F32).astype(BF16)
+    normed_attn_grad = jnp.dot(mixed_grad, w_mixed.T, preferred_element_type=F32)
+    grad_attn_gain = jnp.sum(normed_attn_grad * plain_in * inv_attn, 0)
+    grad_in = residual_grad + norm_grad(normed_attn_grad, plain_in, inv_attn, attn_gain)
+
+    small_grads = pack_columns(
+        [
+            grad_w_router,
+            grad_attn_gain[:, None],
+            grad_mlp_gain[:, None],
+            spread(grad_query_gain, devices, rows),
+            spread(grad_key_gain, devices, rows),
+        ],
+        width,
+        lanes,
+        F32,
+    )
+    share_mixed, share_w_output, share_small = scatter_sum([grad_w_mixed, grad_w_output, small_grads], 6)
+    return (
+        block_out,
+        grad_in,
+        share_small[:, experts_total],
+        share_small[:head_rows, experts_total + 2],
+        share_small[:head_rows, experts_total + 3],
+        share_mixed[:, :query_cols],
+        share_mixed[:, query_cols : query_cols + key_cols],
+        share_mixed[:, query_cols + key_cols :],
+        share_w_output,
+        share_small[:, experts_total + 1],
+        share_small[:, :experts_total],
+        grad_w_gate,
+        grad_w_up,
+        grad_w_down,
+    )
+
+
+def per_device(*arguments):
+    expert_ids, w_gate = arguments[2], arguments[12]
+    devices, width = lax.axis_size(("dp", "expert")), lax.axis_size("expert")
+    length, choices = expert_ids.shape
+    capacity = 5 * length * choices // (4 * devices)
+    dense = devices <= 4 * choices and w_gate.shape[0] == 1 and width == 8
+    if dense and capacity % 16 == 0 and devices % 4 == 0:
+        return per_device_gather(*arguments)
+    return per_device_exchange(*arguments)
+
+
 def solution(mesh):
     in_specs = (
         P(("dp", "expert"), None),

time: 2530 us -> 1350 us (0.53)
  waiting for transfers between devices: 1600 us -> 0 us
  Pallas kernels: 0 us -> 1050 us
  blocking collectives: 353 us -> 0 us
  matrix products: 248 us -> 141 us
  local copies, waits for them, and re-layouts: 172 us -> 79.9 us
  other arithmetic: 120 us -> 69.2 us
    pallas_call x0 -> x7, Pallas kernels: none -> 1050 us  [the longest x3 491 us: scatter_sum(): pl.pallas_call(functools.partial(scatter_kernel, nz, count), out_shape=[j...]
    reduce_scatter x4 -> x0, waiting for transfers between devices: 809 us -> none  [the longest x1 365 us: per_device(): lax.psum_scatter(grad_w_query, ('dp', 'expert'), scatter_dimension=0, til...]
    all_to_all x3 -> x0, waiting for transfers between devices: 624 us -> none  [move_rows(): lax.all_to_all(row_block, ('dp', 'expert'), split_axis=0, concat_axis=0,...]
    all_to_all x1 -> x0, blocking collectives: 231 us -> none  [move_rows(): lax.all_to_all(row_block, ('dp', 'expert'), split_axis=0, concat_axis=0,...]
    all_gather x4 -> x0, waiting for transfers between devices: 161 us -> none  [the longest x1 86.8 us: per_device(): lax.all_gather(w_output, ('dp', 'expert'), axis=0, tiled=True)]
    dot_general x23 -> x13, matrix products: 222 us -> 115 us  [the longest x1 18.3 us: per_device_gather(): jnp.dot(branch_grad, w_out.T, preferred_element_type=F32).astype(BF16)]
    gather x4 -> x0, local copies, waits for them, and re-layouts: 89.8 us -> none  [the longest x1 24.6 us: per_device(): send_grad = down_in[pair_ids] * filled[:, None]]
    unnamed x2 -> x0, blocking collectives: 80.1 us -> none
  transfers between devices with their start and end apart: 12 -> 0, of which waited for: 8 -> 0; matrix products, arithmetic and copies ran while one was open for 16% -> 0% of each run, Pallas kernels for 0% -> 0%
where the time goes in v1:
time: 1350 us; the launch traced here: 1340 us
  Pallas kernels  1050 us (78%)
  matrix products  141 us (10%)
  local copies, waits for them, and re-layouts  79.9 us (6%)
  other arithmetic  69.2 us (5%)
    pallas_call x3, Pallas kernels, scatter_sum(): pl.pallas_call(functools.partial(scatter_kernel, nz, count), out_shape=[j...  491 us
    pallas_call x3, Pallas kernels, gather_all(): pl.pallas_call(functools.partial(gather_kernel, nz, count), out_shape=[ja...  467 us
    pallas_call x1, Pallas kernels, experts(): pl.pallas_call(functools.partial(expert_kernel, group, cap), grid=(device...  93.2 us
    unnamed x126, local copies, waits for them, and re-layouts  34.2 us

profile of v1, /device:TPU:0, one launch (start us, length us, event | category | flops | bytes accessed | tf_op | source)
XLA Modules:
  0.0 1342.7 jit_solution(2391478376250726488)
XLA Ops:
  7.4 167.7 %gather_all.3 = (bf16[4,8,2,32,5120]{4,3,2,1,0:T(8,128)(2,1)}, bf16[4,8,2,64,2048]{4,3,2,1,0:T(8,128)(2,1)}, bf16[4,8,2,32,128]{4,3,2,1,0:T(8,128)(2,1)}) custom-call(bf16[2,32,5120]{2,1,0:T(8,128)(2,1)} %bitcast.274, bf16[2,64,2048]{2,1,0:T(8,128)(2,1)} %bitcast.285, bf16[2,32,128]{2,1,0:T(8,128)(2,1)} %concatenate.67.refs_2_), custom_call_target="tpu_custom_call" | custom-call | tf_op jit(solution)/shard_map/gather_all/pallas_call | solution.py:647
  179.0 10.1 fusion.45
  217.2 5.5 fusion.25
  222.7 9.1 multiply_reduce_fusion.4
  236.7 153.5 %gather_all.4 = (bf16[4,8,2,128,2048]{4,3,2,1,0:T(8,128)(2,1)}, bf16[4,8,2,48,256]{4,3,2,1,0:T(8,128)(2,1)}) custom-call(bf16[2,128,2048]{2,1,0:T(8,128)(2,1)} %bitcast.255, bf16[2,48,256]{2,1,0:T(8,128)(2,1)} %bitcast.293), custom_call_target="tpu_custom_call" | custom-call | tf_op jit(solution)/shard_map/gather_all/pallas_call | solution.py:647
  392.0 145.7 %gather_all.5 = bf16[4,8,2,128,2048]{4,3,2,1,0:T(8,128)(2,1)} custom-call(bf16[2,128,2048]{2,1,0:T(8,128)(2,1)} %bitcast.269), custom_call_target="tpu_custom_call" | custom-call | tf_op jit(solution)/shard_map/gather_all/pallas_call | solution.py:647
  537.7 93.2 %experts.1 = (bf16[32,256,2048]{2,1,0:T(8,128)(2,1)}, bf16[32,256,2048]{2,1,0:T(8,128)(2,1)}, f32[32,1,256]{2,1,0:T(1,128)}, bf16[2560,2048]{1,0:T(8,128)(2,1)},...) custom-call(bf16[32,256,2048]{2,1,0:T(8,128)(2,1)} %bitcast.244, ...), custom_call_target="tpu_custom_call" | custom-call | tf_op jit(solution)/shard_map/experts/pallas_call | solution.py:945
  630.9 14.3 %convolution_bitcast_fusion = f32[1,768,2048]{2,1,0:T(8,128)} fusion(bf16[2560,768]{1,0:T(8,128)(2,1)} %get-tuple-element.48, bf16[2560,2048]{1,0:T(8,128)(2,1)} %get-tuple-element.49), kind=kOutput, calls=%fused_computation.40 | convolution fusion | flops 8053063680 | bytes 20709376 | tf_op jit(solution)/shard_map/dot_general | solution.py:1067
  645.2 11.0 convolution_bitcast_fusion.1
  656.2 11.1 convolution_bitcast_fusion.2
  668.5 161.3 %scatter_sum.4 = (f32[2,128,2048]{2,1,0:T(8,128)}, f32[2,16,256]{2,1,0:T(8,128)}) custom-call(bf16[4,8,2,128,2048]{4,3,2,1,0:T(8,128)(2,1)} %bitcast.246, f32[4,8,2,16,256]{4,3,2,1,0:T(8,128)} %broadcast_multiply_fusion.refs_1_), custom_call_target="tpu_custom_call" | custom-call | tf_op jit(solution)/shard_map/scatter_sum/pallas_call | solution.py:872
  838.3 156.7 %scatter_sum.3 = f32[2,128,2048]{2,1,0:T(8,128)} custom-call(bf16[4,8,2,128,2048]{4,3,2,1,0:T(8,128)(2,1)} %bitcast.245), custom_call_target="tpu_custom_call" | custom-call | tf_op jit(solution)/shard_map/scatter_sum/pallas_call | solution.py:872
  1001.6 18.3 %fusion.26 = bf16[32,8,32,128]{3,1,2,0:T(8,128)(2,1)} fusion(bf16[4096,2048]{1,0:T(8,128)(2,1)} %bitcast.248, f32[256,2048]{1,0:T(8,128)S(1)} %get-tuple-element.70), kind=kOutput, calls=%fused_computation.66 | convolution fusion | flops 4296540160 | bytes 20971520 | tf_op jit(solution)/shard_map/dot_general | solution.py:1081
  1022.0 6.3 fusion
  1037.0 5.5 copy.301
  1042.6 6.0 copy.302
  1048.7 8.4 multiply_add_fusion
  1057.0 5.8 multiply_reduce_fusion
  1066.4 19.3 %fusion.12 = (f32[4096]{0:T(1024)S(1)}, bf16[256,4096]{1,0:T(8,128)(2,1)}) fusion(f32[32,8,32,128]{3,2,1,0:T(8,128)S(1)} %bitcast.253, f32[32,8,32,128]{3,2,1,0:T(8,128)S(1)} %bitcast.257, f32[256,5120]{1,0:T(8,128)S(1)} %bitcast.252, f32[32,8,32,128]{3,2,1,0:T(8,128)S(1)} %bitcast.256, f32[32,8,32,128]{3,2,1,0:T(8,128)S(1)} %bitcast.258, ...), kind=kLoop, calls=%fused_computation.30 | loop fusion | flops 9433088 | bytes 23101440 | tf_op jit(solution)/shard_map/reduce_sum | solution.py:1088
  1095.3 7.9 copy.265
  1108.2 11.9 fusion.22
  1133.0 12.1 convolution_convert_fusion
  1145.1 9.8 convolution_convert_fusion.1
  1154.9 173.0 %scatter_sum.5 = (f32[2,32,5120]{2,1,0:T(8,128)}, f32[2,64,2048]{2,1,0:T(8,128)}, f32[2,32,128]{2,1,0:T(8,128)}) custom-call(bf16[4,8,2,32,5120]{4,3,2,1,0:T(8,128)(2,1)} %bitcast.238, bf16[4,8,2,64,2048]{4,3,2,1,0:T(8,128)(2,1)} %bitcast.239, f32[4,8,2,32,128]{4,3,2,1,0:T(8,128)} %concatenate.83.refs_2_), custom_call_target="tpu_custom_call" | custom-call | tf_op jit(solution)/shard_map/scatter_sum/pallas_call | solution.py:872
  (219 shorter events, 117.2 us)
Async XLA Ops:
  178.1 11.0 copy-start.32
  179.0 10.1 copy-start.34
  191.6 6.7 copy-start.17
  195.3 11.9 copy-start.20
  195.3 11.9 copy-start.22
  195.6 15.1 %copy-start.26 = (bf16[256,4,64]{2,0,1:T(8,128)(2,1)}, bf16[256,4,64]{2,0,1:T(8,128)(2,1)S(1)}, u32[]{:S(2)}) copy-start(bf16[256,4,64]{2,0,1:T(8,128)(2,1)S(1)} %get-tuple-element.78) | copy-start | bytes 393220
  195.6 15.1 %copy-start.28 = (bf16[256,4,64]{2,0,1:T(8,128)(2,1)}, bf16[256,4,64]{2,0,1:T(8,128)(2,1)S(1)}, u32[]{:S(2)}) copy-start(bf16[256,4,64]{2,0,1:T(8,128)(2,1)S(1)} %get-tuple-element.79) | copy-start | bytes 393220
  222.7 9.1 copy-start.12
  630.9 14.3 %copy-start.47 = (bf16[2560,2048]{1,0:T(8,128)(2,1)S(1)}, bf16[2560,2048]{1,0:T(8,128)(2,1)}, u32[]{:S(2)}) copy-start(bf16[2560,2048]{1,0:T(8,128)(2,1)} %get-tuple-element.45) | copy-start | bytes 31457284
  630.9 14.3 %copy-start.49 = (bf16[2560,768]{1,0:T(8,128)(2,1)S(1)}, bf16[2560,768]{1,0:T(8,128)(2,1)}, u32[]{:S(2)}) copy-start(bf16[2560,768]{1,0:T(8,128)(2,1)} %get-tuple-element.47) | copy-start | bytes 11796484
  645.2 11.0 copy-start.48
  656.2 11.2 copy-start.38
  1022.0 6.4 slice-start
  1048.6 8.4 copy-start.1
  1048.6 8.4 copy-start.41
  1048.6 17.7 %slice-start.2 = ((s8[5242880]{0:T(1024)(128)(4,1)}), s8[4194304]{0:T(1024)(128)(4,1)S(1)}, s32[]{:S(2)}) async-start(s8[5242880]{0:T(1024)(128)(4,1)} %bitcast.251), calls=%async_computation.2 | async-start | bytes 8388608
  1057.0 9.3 slice-start.3
  1066.4 19.3 %copy-start.3 = (bf16[4,8,256,256]{2,3,1,0:T(8,128)(2,1)S(1)}, bf16[4,8,256,256]{2,3,1,0:T(8,128)(2,1)}, u32[]{:S(2)}) copy-start(bf16[4,8,256,256]{2,3,1,0:T(8,128)(2,1)} %copy-done.2) | copy-start | bytes 12582916
  1066.4 19.3 %copy-start.15 = (bf16[256,32,64]{2,0,1:T(8,128)(2,1)S(1)}, bf16[256,32,64]{2,0,1:T(8,128)(2,1)}, u32[]{:S(2)}) copy-start(bf16[256,32,64]{2,0,1:T(8,128)(2,1)} %copy-done.14) | copy-start | bytes 3145732
  1120.2 8.1 copy-start.19
  1133.0 12.1 copy-start.8
  1154.9 182.8 %copy-start.45 = (f32[256]{0:T(256)S(1)}, f32[256]{0:T(256)}, u32[]{:S(2)}) copy-start(f32[256]{0:T(256)} %get-tuple-element.98) | copy-start | bytes 3076
  1327.9 9.8 copy-start.9
  1330.4 11.1 copy-start.30
  (30 other events, 102.7 us)

commit v2 on v1

--- a/solution.py
+++ b/solution.py
@@ -463,155 +463,138 @@
 
 
 class Gather:
-    Z, XA, XB, XF, YB, YA, YF, P0, PXA, PXB, PYB, PYA, PDB, PDA = range(14)
+    Z, ZX, ZY, X3, X2, XQ, Y3, Y2, YQ, P0, PX3, PXQ, PY3, PYQ, PDX, PDY = range(16)
+    KINDS = 16
+    WHOLE, LOW, HIGH, LOW3, HIGH3, Q0, Q3 = (0, 4), (0, 2), (2, 2), (0, 3), (1, 3), (0, 1), (3, 1)
 
     def __init__(self, nz, shards, outs, send, recv, local):
         self.nz, self.shards, self.outs = nz, shards, outs
         self.send, self.recv, self.local = send, recv, local
         self.z, self.e = place()
-        self.x, self.y, self.p = self.e ^ 2, self.e ^ 4, self.e ^ 1
-        self.d = self.e ^ 6
-
-    def at(self, i, zz, ee, half):
-        ref = self.outs[i].at[zz, ee]
-        return ref if half is None else ref.at[half]
-
-    def own(self, i, half):
-        ref = self.shards[i]
-        return ref if half is None else ref.at[half]
-
-    def copy(self, i, kind, zz, ee, half, dev, mine=False):
-        dst = self.at(i, zz, ee, half)
+        self.p, self.x, self.y, self.d = self.e ^ 1, self.e ^ 2, self.e ^ 4, self.e ^ 6
+
+    def zz(self, j):
+        return line_order(self.z, self.nz, j)
+
+    def part(self, ref, piece):
+        return ref.at[pl.ds(piece[0], piece[1])]
+
+    def copy(self, i, kind, zz, ee, piece, dev, mine=False, sem=None):
+        dst = self.part(self.outs[i].at[zz, ee], piece)
         return pltpu.make_async_remote_copy(
-            src_ref=self.own(i, half) if mine else dst,
+            src_ref=self.part(self.shards[i], piece) if mine else dst,
             dst_ref=dst,
-            send_sem=self.send.at[i, zz, kind],
+            send_sem=self.send.at[i, zz, kind] if sem is None else sem,
             recv_sem=self.recv.at[i, zz, kind],
             device_id=dev,
             device_id_type=MESH,
         )
 
-    def start(self, kind, zz, ee, half, dev, mine=False):
+    def start(self, kind, zz, ee, piece, dev, mine=False):
         for i in range(len(self.outs)):
-            self.copy(i, kind, zz, ee, half, dev, mine).start()
-
-    def arrived(self, kind, zz, ee, half):
+            self.copy(i, kind, zz, ee, piece, dev, mine).start()
+
+    def arrived(self, kind, zz, ee, piece):
         for i in range(len(self.outs)):
-            self.copy(i, kind, zz, ee, half, (self.z, self.e)).wait_recv()
-
-    def sent(self, kind, zz, ee, half, mine=False):
+            self.copy(i, kind, zz, ee, piece, (self.z, self.e)).wait_recv()
+
+    def sent(self, kind, zz, ee, piece, mine=False):
         for i in range(len(self.outs)):
-            self.copy(i, kind, zz, ee, half, (self.z, self.e), mine).wait_send()
-
-    def zz(self, j):
-        return line_order(self.z, self.nz, j)
+            self.copy(i, kind, zz, ee, piece, (self.z, self.e), mine).wait_send()
+
+    def along(self, j, kind, ee, piece, act):
+        z, e, nz = self.z, self.e, self.nz
+        zz, mine = self.zz(j), j == 0 and kind == self.Z
+        for i in range(len(self.outs)):
+            @pl.when(jnp.logical_and(zz <= z, z < nz - 1))
+            def _():
+                act(self.copy(i, kind, zz, ee, piece, (z + 1, e), mine))
+
+            @pl.when(jnp.logical_and(zz >= z, z > 0))
+            def _():
+                sem = self.local.at[1 + kind, i] if j == 0 else None
+                act(self.copy(i, kind, zz, ee, piece, (z - 1, e), mine, sem))
+
+    def keep(self, i):
+        return pltpu.make_async_copy(self.shards[i], self.outs[i].at[self.z, self.e], self.local.at[0, i])
 
     def launch(self, j):
-        z, e, nz = self.z, self.e, self.nz
-        zz = self.zz(j)
-        mine = j == 0
+        z, e, zz, mine = self.z, self.e, self.zz(j), j == 0
+        if not mine:
+            self.arrived(self.Z, zz, e, self.WHOLE)
+        else:
+            self.start(self.XQ, zz, e, self.Q3, (z, self.x), mine)
+            self.start(self.YQ, zz, e, self.Q0, (z, self.y), mine)
+        self.along(j, self.Z, e, self.WHOLE, lambda c: c.start())
+        self.start(self.X3, zz, e, self.LOW3, (z, self.x), mine)
+        self.start(self.Y3, zz, e, self.HIGH3, (z, self.y), mine)
+        self.start(self.P0, zz, e, self.WHOLE, (z, self.p), mine)
         if mine:
             for i in range(len(self.outs)):
-                pltpu.make_async_copy(self.shards[i], self.at(i, z, e, None), self.local.at[i]).start()
-        else:
-            self.arrived(self.Z, zz, e, None)
-
-        @pl.when(jnp.logical_and(zz <= z, z < nz - 1))
-        def _():
-            self.start(self.Z, zz, e, None, (z + 1, e), mine)
-
+                self.keep(i).start()
+
+    def mates(self, j):
+        zz, mine = self.zz(j), j == 0
+        self.arrived(self.XQ if mine else self.ZX, zz, self.x, self.Q3)
+        self.along(j, self.ZX, self.x, self.Q3, lambda c: c.start())
+        self.start(self.PXQ, zz, self.x, self.Q3, (self.z, self.p))
+        self.arrived(self.YQ if mine else self.ZY, zz, self.y, self.Q0)
+        self.along(j, self.ZY, self.y, self.Q0, lambda c: c.start())
+        self.start(self.PYQ, zz, self.y, self.Q0, (self.z, self.p))
+
+    def relay(self, j):
+        zz = self.zz(j)
+        self.arrived(self.X3, zz, self.x, self.LOW3)
+        self.start(self.Y2, zz, self.x, self.HIGH, (self.z, self.y))
+        self.start(self.PX3, zz, self.x, self.LOW3, (self.z, self.p))
+        self.arrived(self.Y3, zz, self.y, self.HIGH3)
+        self.start(self.X2, zz, self.y, self.LOW, (self.z, self.x))
+        self.start(self.PY3, zz, self.y, self.HIGH3, (self.z, self.p))
+
+    def finish(self, j):
+        zz = self.zz(j)
+        self.arrived(self.X2, zz, self.d, self.LOW)
+        self.start(self.PDX, zz, self.d, self.LOW, (self.z, self.p))
+        self.arrived(self.Y2, zz, self.d, self.HIGH)
+        self.start(self.PDY, zz, self.d, self.HIGH, (self.z, self.p))
+
+    def shared(self, j):
+        zz, p = self.zz(j), self.p
+        self.arrived(self.P0, zz, p, self.WHOLE)
+        self.arrived(self.PXQ, zz, p ^ 2, self.Q3)
+        self.arrived(self.PYQ, zz, p ^ 4, self.Q0)
+        self.arrived(self.PX3, zz, p ^ 2, self.LOW3)
+        self.arrived(self.PY3, zz, p ^ 4, self.HIGH3)
+        self.arrived(self.PDX, zz, p ^ 6, self.LOW)
+        self.arrived(self.PDY, zz, p ^ 6, self.HIGH)
+
+    def drain(self, j):
+        zz, e, mine = self.zz(j), self.e, j == 0
         if mine:
-            @pl.when(z > 0)
-            def _():
-                for i in range(len(self.outs)):
-                    pltpu.make_async_remote_copy(
-                        src_ref=self.own(i, None), dst_ref=self.at(i, z, e, None),
-                        send_sem=self.local.at[len(self.outs) + i],
-                        recv_sem=self.recv.at[i, z, self.Z],
-                        device_id=(z - 1, e), device_id_type=MESH).start()
-        else:
-            @pl.when(jnp.logical_and(zz > z, z > 0))
-            def _():
-                self.start(self.Z, zz, e, None, (z - 1, e))
-
-        self.start(self.XA, zz, e, 0, (z, self.x), mine)
-        self.start(self.YB, zz, e, 1, (z, self.y), mine)
-        self.start(self.XB, zz, e, 1, (z, self.x), mine)
-        self.start(self.YA, zz, e, 0, (z, self.y), mine)
-        self.start(self.P0, zz, e, None, (z, self.p), mine)
-
-    def relay(self, j):
-        z = self.z
-        zz = self.zz(j)
-        self.arrived(self.XA, zz, self.x, 0)
-        self.start(self.YF, zz, self.x, 0, (z, self.y))
-        self.start(self.PXA, zz, self.x, 0, (z, self.p))
-        self.arrived(self.YB, zz, self.y, 1)
-        self.start(self.XF, zz, self.y, 1, (z, self.x))
-        self.start(self.PYB, zz, self.y, 1, (z, self.p))
-
-    def finish(self, j):
-        z = self.z
-        zz = self.zz(j)
-        self.arrived(self.XB, zz, self.x, 1)
-        self.start(self.PXB, zz, self.x, 1, (z, self.p))
-        self.arrived(self.YA, zz, self.y, 0)
-        self.start(self.PYA, zz, self.y, 0, (z, self.p))
-        self.arrived(self.XF, zz, self.d, 1)
-        self.start(self.PDB, zz, self.d, 1, (z, self.p))
-        self.arrived(self.YF, zz, self.d, 0)
-        self.start(self.PDA, zz, self.d, 0, (z, self.p))
-
-    def shared(self, j):
-        zz = self.zz(j)
-        p = self.p
-        self.arrived(self.P0, zz, p, None)
-        self.arrived(self.PXA, zz, p ^ 2, 0)
-        self.arrived(self.PXB, zz, p ^ 2, 1)
-        self.arrived(self.PYA, zz, p ^ 4, 0)
-        self.arrived(self.PYB, zz, p ^ 4, 1)
-        self.arrived(self.PDA, zz, p ^ 6, 0)
-        self.arrived(self.PDB, zz, p ^ 6, 1)
-
-    def drain(self, j):
-        z, e, nz = self.z, self.e, self.nz
-        zz = self.zz(j)
-        mine = j == 0
-
-        @pl.when(jnp.logical_and(zz <= z, z < nz - 1))
-        def _():
-            self.sent(self.Z, zz, e, None, mine)
-
-        if mine:
+            self.sent(self.XQ, zz, e, self.Q3, mine)
+            self.sent(self.YQ, zz, e, self.Q0, mine)
             for i in range(len(self.outs)):
-                pltpu.make_async_copy(self.shards[i], self.at(i, z, e, None), self.local.at[i]).wait()
-
-            @pl.when(z > 0)
-            def _():
-                for i in range(len(self.outs)):
-                    pltpu.make_async_remote_copy(
-                        src_ref=self.own(i, None), dst_ref=self.at(i, z, e, None),
-                        send_sem=self.local.at[len(self.outs) + i],
-                        recv_sem=self.recv.at[i, z, self.Z],
-                        device_id=(z, e), device_id_type=MESH).wait_send()
-        else:
-            @pl.when(jnp.logical_and(zz > z, z > 0))
-            def _():
-                self.sent(self.Z, zz, e, None)
-
-        self.sent(self.XA, zz, e, 0, mine)
-        self.sent(self.XB, zz, e, 1, mine)
-        self.sent(self.YA, zz, e, 0, mine)
-        self.sent(self.YB, zz, e, 1, mine)
-        self.sent(self.P0, zz, e, None, mine)
-        self.sent(self.YF, zz, self.x, 0)
-        self.sent(self.XF, zz, self.y, 1)
-        self.sent(self.PXA, zz, self.x, 0)
-        self.sent(self.PXB, zz, self.x, 1)
-        self.sent(self.PYA, zz, self.y, 0)
-        self.sent(self.PYB, zz, self.y, 1)
-        self.sent(self.PDA, zz, self.d, 0)
-        self.sent(self.PDB, zz, self.d, 1)
+                self.keep(i).wait()
+        for kind, ee, piece in ((self.Z, e, self.WHOLE), (self.ZX, self.x, self.Q3), (self.ZY, self.y, self.Q0)):
+            self.along(j, kind, ee, piece, lambda c: c.wait_send())
+        self.sent(self.X3, zz, e, self.LOW3, mine)
+        self.sent(self.Y3, zz, e, self.HIGH3, mine)
+        self.sent(self.P0, zz, e, self.WHOLE, mine)
+        self.sent(self.PXQ, zz, self.x, self.Q3)
+        self.sent(self.PYQ, zz, self.y, self.Q0)
+        self.sent(self.Y2, zz, self.x, self.HIGH)
+        self.sent(self.X2, zz, self.y, self.LOW)
+        self.sent(self.PX3, zz, self.x, self.LOW3)
+        self.sent(self.PY3, zz, self.y, self.HIGH3)
+        self.sent(self.PDX, zz, self.d, self.LOW)
+        self.sent(self.PDY, zz, self.d, self.HIGH)
+
+    def steps(self):
+        n = self.nz
+        todo = [(self.launch, 0), (self.mates, 0)]
+        for j in range(1, n + 2):
+            todo += [(self.launch, j), (self.mates, j - 1) if j > 1 else None, (self.relay, j - 1), (self.finish, j - 2)]
+        return [functools.partial(f, j) for f, j in filter(None, todo) if 0 <= j < n]
 
 
 def gather_kernel(nz, count, *refs):
@@ -620,12 +603,8 @@
     z, e = place()
     greet(z, e, nz)
     g = Gather(nz, shards, outs, send, recv, local)
-    for j in range(nz):
-        g.launch(j)
-        g.relay(j)
-        if j > 0:
-            g.finish(j - 1)
-    g.finish(nz - 1)
+    for step in g.steps():
+        step()
     for j in range(nz):
         g.shared(j)
     for j in range(nz):
@@ -634,19 +613,19 @@
 
 def gather_scratch(nz, count):
     return [
-        pltpu.SemaphoreType.DMA((count, nz, 14)),
-        pltpu.SemaphoreType.DMA((count, nz, 14)),
-        pltpu.SemaphoreType.DMA((2 * count,)),
+        pltpu.SemaphoreType.DMA((count, nz, Gather.KINDS)),
+        pltpu.SemaphoreType.DMA((count, nz, Gather.KINDS)),
+        pltpu.SemaphoreType.DMA((4, count)),
     ]
 
 
 def gather_all(arrays, collective_id):
     nz, width = lax.axis_size("dp"), lax.axis_size("expert")
     count = len(arrays)
-    halves = [a.reshape((2, a.shape[0] // 2) + a.shape[1:]) for a in arrays]
+    parts = [a.reshape((4, a.shape[0] // 4) + a.shape[1:]) for a in arrays]
     outs = pl.pallas_call(
         functools.partial(gather_kernel, nz, count),
-        out_shape=[jax.ShapeDtypeStruct((nz, width) + h.shape, h.dtype) for h in halves],
+        out_shape=[jax.ShapeDtypeStruct((nz, width) + h.shape, h.dtype) for h in parts],
         in_specs=[pl.BlockSpec(memory_space=pltpu.VMEM)] * count,
         out_specs=[pl.BlockSpec(memory_space=pl.ANY)] * count,
         scratch_shapes=gather_scratch(nz, count),
@@ -654,10 +633,8 @@
             collective_id=collective_id, has_side_effects=True, vmem_limit_bytes=VMEM_LIMIT
         ),
         name="gather_all",
-    )(*halves)
-    return [
-        o.reshape((nz * width * a.shape[0],) + a.shape[1:]) for o, a in zip(outs, arrays)
-    ]
+    )(*parts)
+    return [o.reshape((nz * width * a.shape[0],) + a.shape[1:]) for o, a in zip(outs, arrays)]
 
 
 def accumulate(dst, src):
@@ -673,18 +650,20 @@
 
 
 class Scatter:
-    YD, YO, XD, XO, XA, YB, Z, ZB = range(4, 12)
-
-    def __init__(self, nz, terms, outs, sums, temps, from_y, from_x, last_x, last_y, from_z, send, recv, local):
+    X2, Y2, X3, Y3, Z, ZB, ZX, ZXB, ZY, ZYB, XQ, YQ = range(4, 16)
+    KINDS = 16
+    BUFFERS = 9
+
+    def __init__(self, nz, terms, outs, sums, temps, from_x2, from_y2, from_x3, from_y3, from_z, from_zm, from_q, send, recv, local):
         self.nz, self.terms, self.outs = nz, terms, outs
         self.sums, self.temps = sums, temps
-        self.from_y, self.from_x, self.last_x, self.last_y, self.from_z = from_y, from_x, last_x, last_y, from_z
+        self.from_x2, self.from_y2, self.from_x3, self.from_y3 = from_x2, from_y2, from_x3, from_y3
+        self.from_z, self.from_zm, self.from_q = from_z, from_zm, from_q
         self.send, self.recv, self.local = send, recv, local
         self.count = len(terms)
         self.z, self.e = place()
-        self.core = self.e % 2
-        self.chip = self.e // 2
-        self.x, self.y, self.p = self.e ^ 2, self.e ^ 4, self.e ^ 1
+        self.core, self.chip = self.e % 2, self.e // 2
+        self.p, self.x, self.y = self.e ^ 1, self.e ^ 2, self.e ^ 4
         self.chips = (self.chip ^ 3, self.chip ^ 1, self.chip ^ 2, self.chip)
 
     def zz(self, j):
@@ -695,6 +674,9 @@
             src_ref=src, dst_ref=dst, send_sem=self.send.at[i, zz, kind], recv_sem=self.recv.at[i, zz, kind],
             device_id=dev, device_id_type=MESH)
 
+    def quarters(self, i, zz, q, first, n):
+        return self.sums[i].at[zz, q, pl.ds(first, n)]
+
     def pair(self, i, j, q):
         zz, chip = self.zz(j), self.chips[q]
         return self.remote(i, q, zz, self.terms[i].at[zz, chip * 2 + (1 - self.core)], self.sums[i].at[zz, q],
@@ -704,6 +686,35 @@
         slot = q % 2
         return pltpu.make_async_copy(
             self.terms[i].at[self.zz(j), self.chips[q] * 2 + self.core], self.temps[i].at[slot], self.local.at[i, slot])
+
+    def x2(self, i, zz):
+        return self.remote(i, self.X2, zz, self.quarters(i, zz, 0, 0, 2), self.from_x2[i].at[zz], (self.z, self.x))
+
+    def y2(self, i, zz):
+        return self.remote(i, self.Y2, zz, self.quarters(i, zz, 0, 2, 2), self.from_y2[i].at[zz], (self.z, self.y))
+
+    def x3(self, i, zz):
+        return self.remote(i, self.X3, zz, self.quarters(i, zz, 1, 0, 3), self.from_x3[i].at[zz], (self.z, self.x))
+
+    def y3(self, i, zz):
+        return self.remote(i, self.Y3, zz, self.quarters(i, zz, 2, 1, 3), self.from_y3[i].at[zz], (self.z, self.y))
+
+    def xq(self, i):
+        return self.remote(i, self.XQ, self.z, self.quarters(i, self.z, 1, 3, 1), self.from_q[i].at[pl.ds(0, 1)], (self.z, self.x))
+
+    def yq(self, i):
+        return self.remote(i, self.YQ, self.z, self.quarters(i, self.z, 2, 0, 1), self.from_q[i].at[pl.ds(1, 1)], (self.z, self.y))
+
+    def line(self, i, zz, which, dz, last=False):
+        slot = self.nz if last else zz
+        kind = (self.Z, self.ZX, self.ZY)[which] + int(last)
+        src = (self.sums[i].at[zz, 3], self.quarters(i, zz, 1, 3, 1), self.quarters(i, zz, 2, 0, 1))[which]
+        dst = self.from_z[i].at[slot] if which == 0 else self.from_zm[i].at[slot, pl.ds(which - 1, 1)]
+        return self.remote(i, kind, zz, src, dst, (self.z + dz, self.e))
+
+    def add(self, i, zz, q, first, n, src):
+        for k in range(n):
+            accumulate(self.sums[i].at[zz, q, first + k], src.at[k])
 
     def begin(self):
         for j in range(self.nz):
@@ -712,33 +723,6 @@
                     self.pair(i, j, q).start()
         for i in range(self.count):
             self.load(i, 0, 0).start()
-
-    def yd(self, i, zz):
-        return self.remote(i, self.YD, zz, self.sums[i].at[zz, 0, 0], self.from_y[i].at[zz, 0], (self.z, self.y))
-
-    def yo(self, i, zz):
-        return self.remote(i, self.YO, zz, self.sums[i].at[zz, 2, 0], self.from_y[i].at[zz, 1], (self.z, self.y))
-
-    def xd(self, i, zz):
-        return self.remote(i, self.XD, zz, self.sums[i].at[zz, 0, 1], self.from_x[i].at[zz, 0], (self.z, self.x))
-
-    def xo(self, i, zz):
-        return self.remote(i, self.XO, zz, self.sums[i].at[zz, 1, 1], self.from_x[i].at[zz, 1], (self.z, self.x))
-
-    def xa(self, i, zz):
-        return self.remote(i, self.XA, zz, self.sums[i].at[zz, 1, 0], self.last_x[i].at[zz], (self.z, self.x))
-
-    def yb(self, i, zz):
-        return self.remote(i, self.YB, zz, self.sums[i].at[zz, 2, 1], self.last_y[i].at[zz], (self.z, self.y))
-
-    def up(self, i, zz):
-        return self.remote(i, self.Z, zz, self.sums[i].at[zz, 3], self.from_z[i].at[zz], (self.z + 1, self.e))
-
-    def down(self, i, zz):
-        return self.remote(i, self.Z, zz, self.sums[i].at[zz, 3], self.from_z[i].at[zz], (self.z - 1, self.e))
-
-    def down_last(self, i, zz):
-        return self.remote(i, self.ZB, zz, self.sums[i].at[zz, 3], self.from_z[i].at[self.nz], (self.z - 1, self.e))
 
     def first(self, j):
         zz = self.zz(j)
@@ -750,70 +734,80 @@
                     self.load(i, j + 1, 0).start()
                 self.pair(i, j, q).wait_recv()
                 self.load(i, j, q).wait()
-                for h in range(2):
-                    accumulate(self.sums[i].at[zz, q, h], self.temps[i].at[q % 2, h])
+                self.add(i, zz, q, 0, 4, self.temps[i].at[q % 2])
                 if q == 0:
-                    self.yd(i, zz).start()
-                    self.xd(i, zz).start()
-                if q == 1:
-                    self.xo(i, zz).start()
-                if q == 2:
-                    self.yo(i, zz).start()
+                    self.x2(i, zz).start()
+                    self.y2(i, zz).start()
 
     def second(self, j):
         zz = self.zz(j)
         for i in range(self.count):
-            self.yd(i, zz).wait_recv()
-            accumulate(self.sums[i].at[zz, 1, 0], self.from_y[i].at[zz, 0])
-            self.xa(i, zz).start()
-            self.xd(i, zz).wait_recv()
-            accumulate(self.sums[i].at[zz, 2, 1], self.from_x[i].at[zz, 0])
-            self.yb(i, zz).start()
+            self.y2(i, zz).wait_recv()
+            self.add(i, zz, 1, 2, 2, self.from_y2[i].at[zz])
+            self.x3(i, zz).start()
+            self.x2(i, zz).wait_recv()
+            self.add(i, zz, 2, 0, 2, self.from_x2[i].at[zz])
+            self.y3(i, zz).start()
+            for which in (1, 2):
+                self.flow(i, j, which)
+
+    def flow(self, i, j, which):
+        z, nz, zz = self.z, self.nz, self.zz(j)
+        q, first, n = ((3, 0, 4), (1, 3, 1), (2, 0, 1))[which]
+
+        def came(slot):
+            ref = self.from_z[i].at[slot] if which == 0 else self.from_zm[i].at[slot, pl.ds(which - 1, 1)]
+            self.add(i, zz, q, first, n, ref)
+
+        if j < nz - 1:
+            @pl.when(jnp.logical_or(jnp.logical_and(zz > z, z > 0), jnp.logical_and(zz < z, z < nz - 1)))
+            def _():
+                self.line(i, zz, which, 1).wait_recv()
+                came(zz)
+
+            @pl.when(zz > z)
+            def _():
+                self.line(i, zz, which, 1).start()
+
+            @pl.when(zz < z - 1)
+            def _():
+                self.line(i, zz, which, -1).start()
+
+            @pl.when(zz == z - 1)
+            def _():
+                self.line(i, zz, which, -1, True).start()
+        else:
+            @pl.when(z > 0)
+            def _():
+                self.line(i, zz, which, 1).wait_recv()
+                came(zz)
+
+            @pl.when(z < nz - 1)
+            def _():
+                self.line(i, zz, which, -1, True).wait_recv()
+                came(nz)
+
+            if which == 1:
+                self.xq(i).start()
+            if which == 2:
+                self.yq(i).start()
 
     def third(self, j):
-        z, nz = self.z, self.nz
         zz = self.zz(j)
         for i in range(self.count):
-            self.yo(i, zz).wait_recv()
-            accumulate(self.sums[i].at[zz, 3, 0], self.from_y[i].at[zz, 1])
-            self.xo(i, zz).wait_recv()
-            accumulate(self.sums[i].at[zz, 3, 1], self.from_x[i].at[zz, 1])
-            self.xa(i, zz).wait_recv()
-            accumulate(self.sums[i].at[zz, 3, 0], self.last_x[i].at[zz])
-            self.yb(i, zz).wait_recv()
-            accumulate(self.sums[i].at[zz, 3, 1], self.last_y[i].at[zz])
-            if j < nz - 1:
-                @pl.when(jnp.logical_or(jnp.logical_and(zz > z, z > 0), jnp.logical_and(zz < z, z < nz - 1)))
-                def _():
-                    self.up(i, zz).wait_recv()
-                    for h in range(2):
-                        accumulate(self.sums[i].at[zz, 3, h], self.from_z[i].at[zz, h])
-
-                @pl.when(zz > z)
-                def _():
-                    self.up(i, zz).start()
-
-                @pl.when(zz < z - 1)
-                def _():
-                    self.down(i, zz).start()
-
-                @pl.when(zz == z - 1)
-                def _():
-                    self.down_last(i, zz).start()
-            else:
-                @pl.when(z > 0)
-                def _():
-                    self.up(i, z).wait_recv()
-                    for h in range(2):
-                        accumulate(self.sums[i].at[z, 3, h], self.from_z[i].at[z, h])
-
-                @pl.when(z < nz - 1)
-                def _():
-                    self.down_last(i, z).wait_recv()
-                    for h in range(2):
-                        accumulate(self.sums[i].at[z, 3, h], self.from_z[i].at[nz, h])
-
-                self.outs[i][...] = self.sums[i][z, 3].astype(self.outs[i].dtype)
+            self.x3(i, zz).wait_recv()
+            self.add(i, zz, 3, 0, 3, self.from_x3[i].at[zz])
+            self.y3(i, zz).wait_recv()
+            self.add(i, zz, 3, 1, 3, self.from_y3[i].at[zz])
+            self.flow(i, j, 0)
+
+    def result(self):
+        for i in range(self.count):
+            self.xq(i).wait_recv()
+            self.add(i, self.z, 3, 3, 1, self.from_q[i].at[pl.ds(0, 1)])
+            self.yq(i).wait_recv()
+            self.add(i, self.z, 3, 0, 1, self.from_q[i].at[pl.ds(1, 1)])
+            self.outs[i][...] = self.sums[i][self.z, 3].astype(self.outs[i].dtype)
 
     def drain(self, j):
         z, nz = self.z, self.nz
@@ -821,39 +815,41 @@
         for i in range(self.count):
             for q in range(4):
                 self.pair(i, j, q).wait_send()
-            for c in (self.yd, self.yo, self.xd, self.xo, self.xa, self.yb):
+            for c in (self.x2, self.y2, self.x3, self.y3):
                 c(i, zz).wait_send()
             if j < nz - 1:
-                @pl.when(zz > z)
-                def _():
-                    self.up(i, zz).wait_send()
-
-                @pl.when(zz < z - 1)
-                def _():
-                    self.down(i, zz).wait_send()
-
-                @pl.when(zz == z - 1)
-                def _():
-                    self.down_last(i, zz).wait_send()
+                for which in range(3):
+                    @pl.when(zz > z)
+                    def _():
+                        self.line(i, zz, which, 1).wait_send()
+
+                    @pl.when(zz < z - 1)
+                    def _():
+                        self.line(i, zz, which, -1).wait_send()
+
+                    @pl.when(zz == z - 1)
+                    def _():
+                        self.line(i, zz, which, -1, True).wait_send()
+            else:
+                self.xq(i).wait_send()
+                self.yq(i).wait_send()
+
+    def steps(self):
+        todo = []
+        for j in range(self.nz + 2):
+            todo += [(self.first, j), (self.second, j - 1), (self.third, j - 2)]
+        return [functools.partial(f, j) for f, j in todo if 0 <= j < self.nz] + [self.result]
 
 
 def scatter_kernel(nz, count, *refs):
-    groups = [refs[k * count : (k + 1) * count] for k in range(9)]
-    send, recv, local = refs[9 * count :]
+    groups = [refs[k * count : (k + 1) * count] for k in range(2 + Scatter.BUFFERS)]
+    send, recv, local = refs[(2 + Scatter.BUFFERS) * count :]
     z, e = place()
     greet(z, e, nz)
     s = Scatter(nz, *groups, send, recv, local)
     s.begin()
-    for j in range(nz):
-        s.first(j)
-        if j > 0:
-            s.second(j - 1)
-        if j > 1:
-            s.third(j - 2)
-    s.second(nz - 1)
-    if nz > 1:
-        s.third(nz - 2)
-    s.third(nz - 1)
+    for step in s.steps():
+        step()
     for j in range(nz):
         s.drain(j)
 
@@ -862,22 +858,21 @@
     nz, width = lax.axis_size("dp"), lax.axis_size("expert")
     count = len(arrays)
     devices = nz * width
-    terms = [a.reshape(nz, width, 2, a.shape[0] // (2 * devices), a.shape[1]) for a in arrays]
-    chips = width // 2
+    terms = [a.reshape(nz, width, 4, a.shape[0] // (4 * devices), a.shape[1]) for a in arrays]
     scratch = []
     shapes = [t.shape[3:] for t in terms]
-    kinds = [a.dtype for a in arrays]
-    for lead in ((nz, chips, 2), (2, 2), (nz, 2), (nz, 2), (nz,), (nz,), (nz + 1, 2)):
-        scratch += [pltpu.VMEM(lead + s, k) for s, k in zip(shapes, kinds)]
+    leads = ((nz, width // 2, 4), (2, 4), (nz, 2), (nz, 2), (nz, 3), (nz, 3), (nz + 1, 4), (nz + 1, 2), (2,))
+    for lead in leads:
+        scratch += [pltpu.VMEM(lead + s, a.dtype) for s, a in zip(shapes, arrays)]
     outs = pl.pallas_call(
         functools.partial(scatter_kernel, nz, count),
-        out_shape=[jax.ShapeDtypeStruct((2,) + s, jnp.float32) for s in shapes],
+        out_shape=[jax.ShapeDtypeStruct((4,) + s, jnp.float32) for s in shapes],
         in_specs=[pl.BlockSpec(memory_space=pl.ANY)] * count,
         out_specs=[pl.BlockSpec(memory_space=pltpu.VMEM)] * count,
         scratch_shapes=scratch
         + [
-            pltpu.SemaphoreType.DMA((count, nz, 12)),
-            pltpu.SemaphoreType.DMA((count, nz, 12)),
+            pltpu.SemaphoreType.DMA((count, nz, Scatter.KINDS)),
+            pltpu.SemaphoreType.DMA((count, nz, Scatter.KINDS)),
             pltpu.SemaphoreType.DMA((count, 2)),
         ],
         compiler_params=pltpu.CompilerParams(
@@ -885,7 +880,7 @@
         ),
         name="scatter_sum",
     )(*terms)
-    return [o.reshape(2 * s[0], s[1]) for o, s in zip(outs, shapes)]
+    return [o.reshape(4 * s[0], s[1]) for o, s in zip(outs, shapes)]
 
 
 def mm(a, b, da=1, db=0):

time: 1350 us -> 1250 us (0.926)
  Pallas kernels: 1050 us -> 951 us
    pallas_call x3, Pallas kernels: 491 us -> 420 us  [scatter_sum(): pl.pallas_call(functools.partial(scatter_kernel, nz, count), out_shape=[j...]
    pallas_call x3, Pallas kernels: 467 us -> 438 us  [gather_all(): pl.pallas_call(functools.partial(gather_kernel, nz, count), out_shape=[ja...]
where the time goes in v2:
time: 1250 us; the launch traced here: 1240 us
  Pallas kernels  951 us (76%)
  matrix products  140 us (11%)
  local copies, waits for them, and re-layouts  79.6 us (6%)
  other arithmetic  69.2 us (6%)
    pallas_call x3, Pallas kernels, gather_all(): pl.pallas_call(functools.partial(gather_kernel, nz, count), out_shape=[ja...  438 us
    pallas_call x3, Pallas kernels, scatter_sum(): pl.pallas_call(functools.partial(scatter_kernel, nz, count), out_shape=[j...  420 us
    pallas_call x1, Pallas kernels, experts(): pl.pallas_call(functools.partial(expert_kernel, group, cap), grid=(device...  93.2 us
    unnamed x126, local copies, waits for them, and re-layouts  33.9 us

profile of v2, /device:TPU:0, one launch (start us, length us, event | category | flops | bytes accessed | tf_op | source)
XLA Modules:
  0.0 1242.0 jit_solution(17418336842500481521)
XLA Ops:
  7.4 155.4 %gather_all.3 = (bf16[4,8,4,16,5120]{4,3,2,1,0:T(8,128)(2,1)}, bf16[4,8,4,32,2048]{4,3,2,1,0:T(8,128)(2,1)}, bf16[4,8,4,16,128]{4,3,2,1,0:T(8,128)(2,1)}) custom-call(bf16[4,16,5120]{2,1,0:T(8,128)(2,1)} %bitcast.274, bf16[4,32,2048]{2,1,0:T(8,128)(2,1)} %bitcast.285, bf16[4,16,128]{2,1,0:T(8,128)(2,1)} %concatenate.67.refs_2_), custom_call_target="tpu_custom_call" | custom-call | tf_op jit(solution)/shard_map/gather_all/pallas_call | solution.py:626
  166.6 10.0 fusion.45
  204.8 5.5 fusion.25
  210.3 9.1 multiply_reduce_fusion.4
  224.3 142.9 %gather_all.4 = (bf16[4,8,4,64,2048]{4,3,2,1,0:T(8,128)(2,1)}, bf16[4,8,4,24,256]{4,3,2,1,0:T(8,128)(2,1)}) custom-call(bf16[4,64,2048]{2,1,0:T(8,128)(2,1)} %bitcast.255, bf16[4,24,256]{2,1,0:T(8,128)(2,1)} %bitcast.293), custom_call_target="tpu_custom_call" | custom-call | tf_op jit(solution)/shard_map/gather_all/pallas_call | solution.py:626
  369.1 139.9 %gather_all.5 = bf16[4,8,4,64,2048]{4,3,2,1,0:T(8,128)(2,1)} custom-call(bf16[4,64,2048]{2,1,0:T(8,128)(2,1)} %bitcast.269), custom_call_target="tpu_custom_call" | custom-call | tf_op jit(solution)/shard_map/gather_all/pallas_call | solution.py:626
  509.0 93.2 %experts.1 = (bf16[32,256,2048]{2,1,0:T(8,128)(2,1)}, bf16[32,256,2048]{2,1,0:T(8,128)(2,1)}, f32[32,1,256]{2,1,0:T(1,128)}, bf16[2560,2048]{1,0:T(8,128)(2,1)},...) custom-call(bf16[32,256,2048]{2,1,0:T(8,128)(2,1)} %bitcast.244, ...), custom_call_target="tpu_custom_call" | custom-call | tf_op jit(solution)/shard_map/experts/pallas_call | solution.py:940
  602.3 14.3 %convolution_bitcast_fusion = f32[1,768,2048]{2,1,0:T(8,128)} fusion(bf16[2560,768]{1,0:T(8,128)(2,1)} %get-tuple-element.48, bf16[2560,2048]{1,0:T(8,128)(2,1)} %get-tuple-element.49), kind=kOutput, calls=%fused_computation.40 | convolution fusion | flops 8053063680 | bytes 20709376 | tf_op jit(solution)/shard_map/dot_general | solution.py:1062
  616.5 11.0 convolution_bitcast_fusion.1
  627.5 11.1 convolution_bitcast_fusion.2
  639.9 142.6 %scatter_sum.4 = (f32[4,64,2048]{2,1,0:T(8,128)}, f32[4,8,256]{2,1,0:T(8,128)}) custom-call(bf16[4,8,4,64,2048]{4,3,2,1,0:T(8,128)(2,1)} %bitcast.246, f32[4,8,4,8,256]{4,3,2,1,0:T(8,128)} %broadcast_multiply_fusion.refs_1_), custom_call_target="tpu_custom_call" | custom-call | tf_op jit(solution)/shard_map/scatter_sum/pallas_call | solution.py:867
  791.0 129.8 %scatter_sum.3 = f32[4,64,2048]{2,1,0:T(8,128)} custom-call(bf16[4,8,4,64,2048]{4,3,2,1,0:T(8,128)(2,1)} %bitcast.245), custom_call_target="tpu_custom_call" | custom-call | tf_op jit(solution)/shard_map/scatter_sum/pallas_call | solution.py:867
  927.4 18.1 %fusion.26 = bf16[32,8,32,128]{3,1,2,0:T(8,128)(2,1)} fusion(bf16[4096,2048]{1,0:T(8,128)(2,1)} %bitcast.248, f32[256,2048]{1,0:T(8,128)S(1)} %get-tuple-element.70), kind=kOutput, calls=%fused_computation.66 | convolution fusion | flops 4296540160 | bytes 20971520 | tf_op jit(solution)/shard_map/dot_general | solution.py:1076
  947.6 6.3 fusion
  962.6 5.5 copy.301
  968.1 5.7 copy.302
  973.9 8.4 multiply_add_fusion
  982.3 5.8 multiply_reduce_fusion
  991.7 19.3 %fusion.12 = (f32[4096]{0:T(1024)S(1)}, bf16[256,4096]{1,0:T(8,128)(2,1)}) fusion(f32[32,8,32,128]{3,2,1,0:T(8,128)S(1)} %bitcast.253, f32[32,8,32,128]{3,2,1,0:T(8,128)S(1)} %bitcast.257, f32[256,5120]{1,0:T(8,128)S(1)} %bitcast.252, f32[32,8,32,128]{3,2,1,0:T(8,128)S(1)} %bitcast.256, f32[32,8,32,128]{3,2,1,0:T(8,128)S(1)} %bitcast.258, ...), kind=kLoop, calls=%fused_computation.30 | loop fusion | flops 9433088 | bytes 23101440 | tf_op jit(solution)/shard_map/reduce_sum | solution.py:1083
  1020.6 7.9 copy.265
  1033.5 11.9 fusion.22
  1058.3 12.0 convolution_convert_fusion
  1070.3 9.8 convolution_convert_fusion.1
  1080.1 147.2 %scatter_sum.5 = (f32[4,16,5120]{2,1,0:T(8,128)}, f32[4,32,2048]{2,1,0:T(8,128)}, f32[4,16,128]{2,1,0:T(8,128)}) custom-call(bf16[4,8,4,16,5120]{4,3,2,1,0:T(8,128)(2,1)} %bitcast.238, bf16[4,8,4,32,2048]{4,3,2,1,0:T(8,128)(2,1)} %bitcast.239, f32[4,8,4,16,128]{4,3,2,1,0:T(8,128)} %concatenate.83.refs_2_), custom_call_target="tpu_custom_call" | custom-call | tf_op jit(solution)/shard_map/scatter_sum/pallas_call | solution.py:867
  (219 shorter events, 117.2 us)
Async XLA Ops:
  165.7 10.9 copy-start.32
  166.6 10.1 copy-start.34
  179.2 6.7 copy-start.17
  182.9 11.9 copy-start.20
  183.0 11.9 copy-start.22
  183.2 15.1 %copy-start.26 = (bf16[256,4,64]{2,0,1:T(8,128)(2,1)}, bf16[256,4,64]{2,0,1:T(8,128)(2,1)S(1)}, u32[]{:S(2)}) copy-start(bf16[256,4,64]{2,0,1:T(8,128)(2,1)S(1)} %get-tuple-element.78) | copy-start | bytes 393220
  183.2 15.1 %copy-start.28 = (bf16[256,4,64]{2,0,1:T(8,128)(2,1)}, bf16[256,4,64]{2,0,1:T(8,128)(2,1)S(1)}, u32[]{:S(2)}) copy-start(bf16[256,4,64]{2,0,1:T(8,128)(2,1)S(1)} %get-tuple-element.79) | copy-start | bytes 393220
  210.3 9.1 copy-start.12
  602.2 14.3 %copy-start.47 = (bf16[2560,2048]{1,0:T(8,128)(2,1)S(1)}, bf16[2560,2048]{1,0:T(8,128)(2,1)}, u32[]{:S(2)}) copy-start(bf16[2560,2048]{1,0:T(8,128)(2,1)} %get-tuple-element.45) | copy-start | bytes 31457284
  602.2 14.3 %copy-start.49 = (bf16[2560,768]{1,0:T(8,128)(2,1)S(1)}, bf16[2560,768]{1,0:T(8,128)(2,1)}, u32[]{:S(2)}) copy-start(bf16[2560,768]{1,0:T(8,128)(2,1)} %get-tuple-element.47) | copy-start | bytes 11796484
  616.5 11.0 copy-start.48
  627.5 11.2 copy-start.38
  947.5 6.4 slice-start
  973.9 8.4 copy-start.1
  973.9 8.4 copy-start.41
  973.9 17.7 %slice-start.2 = ((s8[5242880]{0:T(1024)(128)(4,1)}), s8[4194304]{0:T(1024)(128)(4,1)S(1)}, s32[]{:S(2)}) async-start(s8[5242880]{0:T(1024)(128)(4,1)} %bitcast.251), calls=%async_computation.2 | async-start | bytes 8388608
  982.3 9.3 slice-start.3
  991.6 19.4 %copy-start.3 = (bf16[4,8,256,256]{2,3,1,0:T(8,128)(2,1)S(1)}, bf16[4,8,256,256]{2,3,1,0:T(8,128)(2,1)}, u32[]{:S(2)}) copy-start(bf16[4,8,256,256]{2,3,1,0:T(8,128)(2,1)} %copy-done.2) | copy-start | bytes 12582916
  991.6 19.4 %copy-start.15 = (bf16[256,32,64]{2,0,1:T(8,128)(2,1)S(1)}, bf16[256,32,64]{2,0,1:T(8,128)(2,1)}, u32[]{:S(2)}) copy-start(bf16[256,32,64]{2,0,1:T(8,128)(2,1)} %copy-done.14) | copy-start | bytes 3145732
  1045.5 8.1 copy-start.19
  1058.3 12.0 copy-start.8
  1080.1 157.0 %copy-start.45 = (f32[256]{0:T(256)S(1)}, f32[256]{0:T(256)}, u32[]{:S(2)}) copy-start(f32[256]{0:T(256)} %get-tuple-element.98) | copy-start | bytes 3076
  1227.3 9.8 copy-start.9
  1229.7 11.1 copy-start.30
  (30 other events, 102.1 us)

commit v3 on v2

--- a/solution.py
+++ b/solution.py
@@ -854,27 +854,27 @@
         s.drain(j)
 
 
+def scatter_buffers(nz, width, kinds):
+    leads = ((nz, width // 2, 4), (2, 4), (nz, 2), (nz, 2), (nz, 3), (nz, 3), (nz + 1, 4), (nz + 1, 2), (2,))
+    return [pltpu.VMEM(lead + shape, dtype) for lead in leads for shape, dtype in kinds] + [
+        pltpu.SemaphoreType.DMA((len(kinds), nz, Scatter.KINDS)),
+        pltpu.SemaphoreType.DMA((len(kinds), nz, Scatter.KINDS)),
+        pltpu.SemaphoreType.DMA((len(kinds), 2)),
+    ]
+
+
 def scatter_sum(arrays, collective_id):
     nz, width = lax.axis_size("dp"), lax.axis_size("expert")
     count = len(arrays)
     devices = nz * width
     terms = [a.reshape(nz, width, 4, a.shape[0] // (4 * devices), a.shape[1]) for a in arrays]
-    scratch = []
     shapes = [t.shape[3:] for t in terms]
-    leads = ((nz, width // 2, 4), (2, 4), (nz, 2), (nz, 2), (nz, 3), (nz, 3), (nz + 1, 4), (nz + 1, 2), (2,))
-    for lead in leads:
-        scratch += [pltpu.VMEM(lead + s, a.dtype) for s, a in zip(shapes, arrays)]
     outs = pl.pallas_call(
         functools.partial(scatter_kernel, nz, count),
         out_shape=[jax.ShapeDtypeStruct((4,) + s, jnp.float32) for s in shapes],
         in_specs=[pl.BlockSpec(memory_space=pl.ANY)] * count,
         out_specs=[pl.BlockSpec(memory_space=pltpu.VMEM)] * count,
-        scratch_shapes=scratch
-        + [
-            pltpu.SemaphoreType.DMA((count, nz, Scatter.KINDS)),
-            pltpu.SemaphoreType.DMA((count, nz, Scatter.KINDS)),
-            pltpu.SemaphoreType.DMA((count, 2)),
-        ],
+        scratch_shapes=scatter_buffers(nz, width, [(s, a.dtype) for s, a in zip(shapes, arrays)]),
         compiler_params=pltpu.CompilerParams(
             collective_id=collective_id, has_side_effects=True, vmem_limit_bytes=VMEM_LIMIT
         ),
@@ -960,6 +960,191 @@
     )(x, g, gate, rank, wg, wu, wd)
 
 
+def rope(values, cosine, sine):
+    return values * cosine + pltpu.roll(values, values.shape[1] // 2, 1) * sine
+
+
+class AttentionGrad:
+    def __init__(self, branch, w_out, raw, tables, gains, seg_col, seg_row, grads, gain_grads,
+                 w_buf, q_buf, k_buf, v_buf, mask, k_rot, v_low, dk, dv, sems):
+        self.branch, self.w_out, self.raw, self.tables, self.gains = branch, w_out, raw, tables, gains
+        self.seg_col, self.seg_row, self.grads, self.gain_grads = seg_col, seg_row, grads, gain_grads
+        self.w_buf, self.q_buf, self.k_buf, self.v_buf, self.mask = w_buf, q_buf, k_buf, v_buf, mask
+        self.k_rot, self.v_low, self.dk, self.dv, self.sems = k_rot, v_low, dk, dv, sems
+        self.cols = w_buf.shape[1]
+        self.query_cols = w_out.shape[0]
+        self.key_cols = k_buf.shape[1]
+        self.count = self.query_cols // self.cols
+        self.per_key = self.count // (self.key_cols // HEAD_DIM)
+
+    def fetch(self, t, slot):
+        at = pl.ds(pl.multiple_of(t * self.cols, self.cols), self.cols)
+        return (
+            pltpu.make_async_copy(self.w_out.at[at, :], self.w_buf.at[slot], self.sems.at[0, slot]),
+            pltpu.make_async_copy(self.raw.at[:, at], self.q_buf.at[slot], self.sems.at[1, slot]),
+        )
+
+    def prepare(self):
+        q, k = self.query_cols, self.key_cols
+        key = pltpu.make_async_copy(self.raw.at[:, pl.ds(q, k)], self.k_buf, self.sems.at[2, 0])
+        value = pltpu.make_async_copy(self.raw.at[:, pl.ds(q + k, k)], self.v_buf, self.sems.at[2, 1])
+        key.start()
+        value.start()
+        for c in self.fetch(0, 0):
+            c.start()
+        length = self.seg_col.shape[0]
+        row = lax.broadcasted_iota(jnp.int32, (length, length), 0)
+        col = lax.broadcasted_iota(jnp.int32, (length, length), 1)
+        same = self.seg_col[...] == self.seg_row[...]
+        self.mask[...] = jnp.where(jnp.logical_and(same, col <= row), 1.0, 0.0)
+        self.gain_grads[...] = jnp.zeros_like(self.gain_grads)
+        key.wait()
+        value.wait()
+
+    def normed(self, raw, which):
+        scale = lax.rsqrt(jnp.mean(raw * raw, 1, keepdims=True) + EPS)
+        return scale, (raw * scale) * self.gains[which : which + 1, :]
+
+    def back(self, rot_grad, raw, scale, which):
+        cosine, sine = self.tables[0], self.tables[1]
+        grad = rope(rot_grad, cosine, -sine)
+        part = jnp.sum(grad * raw * scale, 0, keepdims=True)
+        self.gain_grads[which : which + 1, :] = self.gain_grads[which : which + 1, :] + part
+        weighted = grad * self.gains[which : which + 1, :]
+        mean = jnp.mean(weighted * raw, 1, keepdims=True)
+        return scale * weighted - raw * (scale * scale * scale) * mean
+
+    def step(self, t):
+        slot = lax.rem(t, 2)
+        last = t + 1 < self.count
+
+        @pl.when(last)
+        def _():
+            for c in self.fetch(t + 1, 1 - slot):
+                c.start()
+
+        for c in self.fetch(t, slot):
+            c.wait()
+        cosine, sine = self.tables[0], self.tables[1]
+        at_key = pl.ds(pl.multiple_of(t // self.per_key * HEAD_DIM, HEAD_DIM), HEAD_DIM)
+
+        @pl.when(lax.rem(t, self.per_key) == 0)
+        def _():
+            _, key = self.normed(self.k_buf[:, at_key], 1)
+            self.k_rot[...] = rope(key, cosine, sine).astype(BF16)
+            self.v_low[...] = self.v_buf[:, at_key].astype(BF16)
+            self.dk[...] = jnp.zeros_like(self.dk)
+            self.dv[...] = jnp.zeros_like(self.dv)
+
+        score_scale = 1.0 / math.sqrt(HEAD_DIM)
+        out_grad = mm(self.branch[...], self.w_buf[slot], 1, 1).astype(BF16)
+        mask = self.mask[...] > 0.0
+        k_rot, v_low = self.k_rot[...], self.v_low[...]
+        for h in range(self.cols // HEAD_DIM):
+            here = slice(h * HEAD_DIM, (h + 1) * HEAD_DIM)
+            raw = self.q_buf[slot, :, here]
+            scale, query = self.normed(raw, 0)
+            q_rot = rope(query, cosine, sine).astype(BF16)
+            d_out = out_grad[:, here]
+            scores = mm(q_rot, k_rot, 1, 1) * score_scale
+            raised = jnp.where(mask, jnp.exp(scores), 0.0)
+            probs = raised / jnp.sum(raised, 1, keepdims=True)
+            self.dv[...] += mm(probs.astype(BF16), d_out, 0, 0)
+            d_probs = mm(d_out, v_low, 1, 1)
+            d_scores = (probs * (d_probs - jnp.sum(probs * d_probs, 1, keepdims=True))).astype(BF16)
+            dq = mm(d_scores, k_rot) * score_scale
+            self.dk[...] += mm(d_scores, q_rot, 0, 0)
+            at = pl.ds(pl.multiple_of(t * self.cols + h * HEAD_DIM, HEAD_DIM), HEAD_DIM)
+            self.grads[:, at] = self.back(dq, raw, scale, 0).astype(BF16)
+
+        @pl.when(lax.rem(t, self.per_key) == self.per_key - 1)
+        def _():
+            raw = self.k_buf[:, at_key]
+            scale, _ = self.normed(raw, 1)
+            shift = pl.multiple_of(t // self.per_key * HEAD_DIM, HEAD_DIM)
+            self.grads[:, pl.ds(self.query_cols + shift, HEAD_DIM)] = self.back(
+                self.dk[...] * score_scale, raw, scale, 1
+            ).astype(BF16)
+            self.grads[:, pl.ds(self.query_cols + self.key_cols + shift, HEAD_DIM)] = self.dv[...].astype(BF16)
+
+
+def scatter_attention_kernel(nz, plan, term, branch, w_out, raw, tables, gains, seg_col, seg_row,
+                             total, grads, gain_grads, *scratch):
+    buffers, rest = scratch[: Scatter.BUFFERS], scratch[Scatter.BUFFERS :]
+    send, recv, local = rest[:3]
+    z, e = place()
+    greet(z, e, nz)
+    s = Scatter(nz, [term], [total], *[[b] for b in buffers], send, recv, local)
+    a = AttentionGrad(branch, w_out, raw, tables, gains, seg_col, seg_row, grads, gain_grads, *rest[3:])
+    s.begin()
+    a.prepare()
+    steps = s.steps()
+    run_beside(a.count, a.step, steps, plan)
+    for j in range(nz):
+        s.drain(j)
+
+
+def run_beside(count, work, steps, plan):
+    bounds = [sum(plan[:t]) for t in range(len(plan) + 1)]
+
+    def body(t, _):
+        for k in range(count):
+            todo = steps[bounds[k] : bounds[k + 1]]
+            if todo:
+                @pl.when(t == k)
+                def _():
+                    for step in todo:
+                        step()
+        work(t)
+        return 0
+
+    lax.fori_loop(0, count, body, 0)
+    for step in steps[bounds[count] :]:
+        step()
+
+
+def scatter_with_attention(terms, branch, w_out, raw, tables, gains, segments, collective_id):
+    nz, width = lax.axis_size("dp"), lax.axis_size("expert")
+    devices = nz * width
+    length = branch.shape[0]
+    shape = (terms.shape[0] // (4 * devices), terms.shape[1])
+    term = terms.reshape((nz, width, 4) + shape)
+    heads = 4
+    cols = heads * HEAD_DIM
+    key_cols = (raw.shape[1] - w_out.shape[0]) // 2
+    vmem = pl.BlockSpec(memory_space=pltpu.VMEM)
+    hbm = pl.BlockSpec(memory_space=pl.ANY)
+    plan = [3, 1, 1, 1, 1, 1, 1, 1]
+    total, grads, gain_grads = pl.pallas_call(
+        functools.partial(scatter_attention_kernel, nz, plan),
+        out_shape=[
+            jax.ShapeDtypeStruct((4,) + shape, F32),
+            jax.ShapeDtypeStruct(raw.shape, BF16),
+            jax.ShapeDtypeStruct((2, HEAD_DIM), F32),
+        ],
+        in_specs=[hbm, vmem, hbm, hbm, vmem, vmem, vmem, vmem],
+        out_specs=[vmem, vmem, vmem],
+        scratch_shapes=scatter_buffers(nz, width, [(shape, terms.dtype)])
+        + [
+            pltpu.VMEM((2, cols, w_out.shape[1]), BF16),
+            pltpu.VMEM((2, length, cols), F32),
+            pltpu.VMEM((length, key_cols), F32),
+            pltpu.VMEM((length, key_cols), F32),
+            pltpu.VMEM((length, length), F32),
+            pltpu.VMEM((length, HEAD_DIM), BF16),
+            pltpu.VMEM((length, HEAD_DIM), BF16),
+            pltpu.VMEM((length, HEAD_DIM), F32),
+            pltpu.VMEM((length, HEAD_DIM), F32),
+            pltpu.SemaphoreType.DMA((3, 2)),
+        ],
+        compiler_params=pltpu.CompilerParams(
+            collective_id=collective_id, has_side_effects=True, vmem_limit_bytes=VMEM_LIMIT
+        ),
+        name="scatter_attention",
+    )(term, branch, w_out, raw, tables, gains, segments[:, None], segments[None, :])
+    return total.reshape(4 * shape[0], shape[1]), grads, gain_grads
+
+
 def pack_columns(columns, rows, lanes, dtype):
     parts = [c.astype(dtype) for c in columns]
     used = sum(c.shape[1] for c in parts)
@@ -1057,8 +1242,6 @@
     is_me = (jnp.arange(experts_total) == me).astype(F32)
     gate_terms = (gate_terms * is_me[None, :, None]).reshape(devices * experts_total, length)
     row_grad_sum, gate_grad = scatter_sum([r_terms.reshape(devices * length, width), gate_terms], 4)
-    (mixed_out,) = scatter_sum([y_terms.reshape(devices * length, width)], 5)
-    block_out = residual + mixed_out
     grad_w_down = jnp.dot(act.T, down_in, preferred_element_type=F32)[None]
     grad_w_gate = jnp.dot(rows_in.T, gate_pre_grad, preferred_element_type=F32)[None]
     grad_w_up = jnp.dot(rows_in.T, up_pre_grad, preferred_element_type=F32)[None]
@@ -1073,25 +1256,14 @@
 
     branch_grad = residual_grad.astype(BF16)
     grad_w_output = jnp.dot(attended.T, branch_grad, preferred_element_type=F32).astype(BF16)
-    attended_grad = jnp.dot(branch_grad, w_out.T, preferred_element_type=F32).astype(BF16)
-    attended_grad = attended_grad.reshape(length, KV_HEADS, group_size, HEAD_DIM)
-    query_rot_grad, key_rot_grad, value_sum_grad = attend_grad(
-        query_rot, key_rot, value_rows, allowed, log_totals, attended_grad
-    )
-    query_normed_grad = unrotate(query_rot_grad.reshape(length, HEADS, HEAD_DIM), cosine_table, sine_table)
-    key_normed_grad = unrotate(key_rot_grad, cosine_table, sine_table)
-    grad_query_gain = jnp.sum(query_normed_grad * query_raw * query_scale, (0, 1))
-    grad_key_gain = jnp.sum(key_normed_grad * key_raw * key_scale, (0, 1))
-    query_grad = norm_grad(query_normed_grad, query_raw, query_scale, query_gain).astype(BF16)
-    key_grad = norm_grad(key_normed_grad, key_raw, key_scale, key_gain).astype(BF16)
-    mixed_grad = jnp.concatenate(
-        [
-            query_grad.reshape(length, query_cols),
-            key_grad.reshape(length, key_cols),
-            value_sum_grad.astype(BF16).reshape(length, key_cols),
-        ],
-        1,
-    )
+    cosine, sine = cosine_table[:, 0], sine_table[:, 0]
+    tables = jnp.stack([jnp.concatenate([cosine, cosine], 1), jnp.concatenate([-sine, sine], 1)])
+    head_gains = jnp.stack([query_gain, key_gain]).astype(F32)
+    mixed_out, mixed_grad, gain_grads = scatter_with_attention(
+        y_terms.reshape(devices * length, width), branch_grad, w_out, mixed, tables, head_gains, segment_ids, 5
+    )
+    block_out = residual + mixed_out
+    grad_query_gain, grad_key_gain = gain_grads[0], gain_grads[1]
     grad_w_mixed = jnp.dot(normed_attn.T, mixed_grad, preferred_element_type=F32).astype(BF16)
     normed_attn_grad = jnp.dot(mixed_grad, w_mixed.T, preferred_element_type=F32)
     grad_attn_gain = jnp.sum(normed_attn_grad * plain_in * inv_attn, 0)

time: 1250 us -> 1150 us (0.920)
  other arithmetic: 69.2 us -> 29.2 us
  matrix products: 140 us -> 102 us
  local copies, waits for them, and re-layouts: 79.6 us -> 48.3 us
    pallas_call x0 -> x1, Pallas kernels: none -> 141 us  [scatter_with_attention(): pl.pallas_call(functools.partial(scatter_attention_kernel, nz, plan), out...]
    pallas_call x3 -> x2, Pallas kernels: 420 us -> 290 us  [scatter_sum(): pl.pallas_call(functools.partial(scatter_kernel, nz, count), out_shape=[j...]
    dot_general x5 -> x0, matrix products: 32.6 us -> none  [the longest x1 18.1 us: per_device_gather(): jnp.dot(branch_grad, w_out.T, preferred_element_type=F32).astype(BF16)]
    reduce_sum x5 -> x0, other arithmetic: 27.6 us -> none  [the longest x2 19.4 us: per_device_gather(): jnp.sum(query_normed_grad * query_raw * query_scale, (0, 1))]
    unnamed x126 -> x106, local copies, waits for them, and re-layouts: 33.9 us -> 19.5 us
where the time goes in v3:
time: 1150 us; the launch traced here: 1140 us
  Pallas kernels  962 us (84%)
  matrix products  102 us (9%)
  local copies, waits for them, and re-layouts  48.3 us (4%)
  other arithmetic  29.2 us (3%)
    pallas_call x3, Pallas kernels, gather_all(): pl.pallas_call(functools.partial(gather_kernel, nz, count), out_shape=[ja...  438 us
    pallas_call x2, Pallas kernels, scatter_sum(): pl.pallas_call(functools.partial(scatter_kernel, nz, count), out_shape=[j...  290 us
    pallas_call x1, Pallas kernels, scatter_with_attention(): pl.pallas_call(functools.partial(scatter_attention_kernel, nz, plan), out...  141 us
    pallas_call x1, Pallas kernels, experts(): pl.pallas_call(functools.partial(expert_kernel, group, cap), grid=(device...  93.2 us

profile of v3, /device:TPU:0, one launch (start us, length us, event | category | flops | bytes accessed | tf_op | source)
XLA Modules:
  0.0 1143.5 jit_solution(6374075102426562458)
XLA Ops:
  7.4 155.4 %gather_all.3 = (bf16[4,8,4,16,5120]{4,3,2,1,0:T(8,128)(2,1)}, bf16[4,8,4,32,2048]{4,3,2,1,0:T(8,128)(2,1)}, bf16[4,8,4,16,128]{4,3,2,1,0:T(8,128)(2,1)}) custom-call(bf16[4,16,5120]{2,1,0:T(8,128)(2,1)} %bitcast.156, bf16[4,32,2048]{2,1,0:T(8,128)(2,1)} %bitcast.163, bf16[4,16,128]{2,1,0:T(8,128)(2,1)} %concatenate.60.refs_2_), custom_call_target="tpu_custom_call" | custom-call | tf_op jit(solution)/shard_map/gather_all/pallas_call | solution.py:626
  162.8 2.6 slice_convert_fusion
  167.2 10.1 fusion.23.raw
  183.7 2.5 slice_bitcast_fusion
  189.4 3.9 multiply_multiply_fusion
  196.8 6.0 fusion
  204.0 5.7 fusion.15
  213.0 4.6 multiply_reduce_fusion.3
  223.0 142.9 %gather_all.4 = (bf16[4,8,4,64,2048]{4,3,2,1,0:T(8,128)(2,1)}, bf16[4,8,4,24,256]{4,3,2,1,0:T(8,128)(2,1)}) custom-call(bf16[4,64,2048]{2,1,0:T(8,128)(2,1)} %bitcast.144, bf16[4,24,256]{2,1,0:T(8,128)(2,1)} %bitcast.172), custom_call_target="tpu_custom_call" | custom-call | tf_op jit(solution)/shard_map/gather_all/pallas_call | solution.py:626
  367.7 139.9 %gather_all.5 = bf16[4,8,4,64,2048]{4,3,2,1,0:T(8,128)(2,1)} custom-call(bf16[4,64,2048]{2,1,0:T(8,128)(2,1)} %bitcast.152), custom_call_target="tpu_custom_call" | custom-call | tf_op jit(solution)/shard_map/gather_all/pallas_call | solution.py:626
  507.6 93.2 %experts.1 = (bf16[32,256,2048]{2,1,0:T(8,128)(2,1)}, bf16[32,256,2048]{2,1,0:T(8,128)(2,1)}, f32[32,1,256]{2,1,0:T(1,128)}, bf16[2560,2048]{1,0:T(8,128)(2,1)},...) custom-call(bf16[32,256,2048]{2,1,0:T(8,128)(2,1)} %bitcast.142, ...), custom_call_target="tpu_custom_call" | custom-call | tf_op jit(solution)/shard_map/experts/pallas_call | solution.py:940
  600.9 14.3 %convolution_bitcast_fusion = f32[1,768,2048]{2,1,0:T(8,128)} fusion(bf16[2560,768]{1,0:T(8,128)(2,1)} %get-tuple-element.54, bf16[2560,2048]{1,0:T(8,128)(2,1)} %get-tuple-element.55), kind=kOutput, calls=%fused_computation.17 | convolution fusion | flops 8053063680 | bytes 20709376 | tf_op jit(solution)/shard_map/dot_general | solution.py:1245
  615.1 11.0 convolution_bitcast_fusion.1
  626.1 11.3 convolution_bitcast_fusion.2
  638.6 142.7 %scatter_sum.2 = (f32[4,64,2048]{2,1,0:T(8,128)}, f32[4,8,256]{2,1,0:T(8,128)}) custom-call(bf16[4,8,4,64,2048]{4,3,2,1,0:T(8,128)(2,1)} %bitcast.143, f32[4,8,4,8,256]{4,3,2,1,0:T(8,128)} %broadcast_multiply_fusion.refs_1_), custom_call_target="tpu_custom_call" | custom-call | tf_op jit(solution)/shard_map/scatter_sum/pallas_call | solution.py:872
  783.1 2.7 fusion.49
  785.8 2.5 multiply_reduce_fusion.1
  793.2 141.3 %scatter_attention.1 = (f32[4,64,2048]{2,1,0:T(8,128)}, bf16[256,5120]{1,0:T(8,128)(2,1)}, f32[2,128]{1,0:T(2,128)}) custom-call(bf16[4,8,4,64,2048]{4,3,2,1,0:T(8,128)(2,1)} %bitcast.141, bf16[256,2048]{1,0:T(8,128)(2,1)} %get-tuple-element.62.branch, bf16[4096,2048]{1,0:T(8,128)(2,1)} %bitcast.136, f32[256,5120]{1,0:T(8,128)} %copy-done.4, ...), custom_call_target="tpu_custom_call" | custom-call | tf_op jit(solution)/shard_map/scatter_attention/pallas_call | solution.py:1118
  934.5 12.2 %fusion.10 = (f32[2048]{0:T(1024)S(1)}, f32[256]{0:T(256)S(1)}, f32[256,2048]{1,0:T(8,128)}) fusion(bf16[256,2048]{1,0:T(8,128)(2,1)} %param.16, f32[256]{0:T(256)S(1)} %copy-done.28, f32[2048]{0:T(1024)S(1)} %bitcast.169, bf16[256,5120]{1,0:T(8,128)(2,1)} %get-tuple-element.46, bf16[2048,5120]{1,0:T(8,128)(2,1)} %bitcast.186), kind=kOutput, calls=%fused_computation.29 | convolution fusion | flops 5372377088 | bytes 26757120 | tf_op jit(solution)/shard_map/dot_general | solution.py:1268
  955.9 5.0 concatenate.73.refs_2_
  960.9 9.5 convolution_convert_fusion.1
  970.4 11.8 %convolution_convert_fusion = bf16[2048,5120]{1,0:T(8,128)(2,1)} fusion(bf16[256,5120]{1,0:T(8,128)(2,1)} %get-tuple-element.46, bf16[256,2048]{1,0:T(8,128)(2,1)S(1)} %copy-done.6, f32[2048]{0:T(1024)S(1)} %bitcast.170, f32[256]{0:T(256)S(1)} %copy-done.28), kind=kOutput, calls=%fused_computation | convolution fusion | flops 5381292032 | bytes 24650752 | tf_op jit(solution)/shard_map/dot_general | solution.py:1267
  982.2 146.9 %scatter_sum.3 = (f32[4,16,5120]{2,1,0:T(8,128)}, f32[4,32,2048]{2,1,0:T(8,128)}, f32[4,16,128]{2,1,0:T(8,128)}) custom-call(bf16[4,8,4,16,5120]{4,3,2,1,0:T(8,128)(2,1)} %bitcast.134, bf16[4,8,4,32,2048]{4,3,2,1,0:T(8,128)(2,1)} %bitcast.135, f32[4,8,4,16,128]{4,3,2,1,0:T(8,128)} %concatenate.73.refs_2_), custom_call_target="tpu_custom_call" | custom-call | tf_op jit(solution)/shard_map/scatter_sum/pallas_call | solution.py:872
  1136.4 4.3 fusion.7
  (176 shorter events, 60.0 us)
Async XLA Ops:
  181.8 4.4 copy-start.21
  196.8 6.0 copy-start.25
  204.0 5.7 slice-start
  204.0 5.9 slice-start.1
  204.0 7.8 slice-start.2
  204.0 9.0 slice-start.3
  209.7 7.9 copy-start.9
  600.8 14.3 %copy-start.39 = (bf16[2560,2048]{1,0:T(8,128)(2,1)S(1)}, bf16[2560,2048]{1,0:T(8,128)(2,1)}, u32[]{:S(2)}) copy-start(bf16[2560,2048]{1,0:T(8,128)(2,1)} %get-tuple-element.51) | copy-start | bytes 31457284
  600.8 14.3 %copy-start.41 = (bf16[2560,768]{1,0:T(8,128)(2,1)S(1)}, bf16[2560,768]{1,0:T(8,128)(2,1)}, u32[]{:S(2)}) copy-start(bf16[2560,768]{1,0:T(8,128)(2,1)} %get-tuple-element.53) | copy-start | bytes 11796484
  615.1 11.0 copy-start.40
  626.1 11.3 copy-start.26
  638.6 142.7 %copy-start.34 = (f32[256]{0:T(256)S(1)}, f32[256]{0:T(256)}, u32[]{:S(2)}) copy-start(f32[256]{0:T(256)} %copy-done.33) | copy-start | bytes 3076
  638.6 147.1 %copy-start.12 = (bf16[4,8,4,16,128]{4,3,2,1,0:T(8,128)(2,1)S(1)}, bf16[4,8,4,16,128]{4,3,2,1,0:T(8,128)(2,1)}, u32[]{:S(2)}) copy-start(bf16[4,8,4,16,128]{4,3,2,1,0:T(8,128)(2,1)} %get-tuple-element.35) | copy-start | bytes 1572868
  781.3 4.4 copy-start.1
  781.4 4.4 copy-start.30
  793.2 141.3 %copy-start.28 = (f32[256]{0:T(256)S(1)}, f32[256]{0:T(256)}, u32[]{:S(2)}) copy-start(f32[256]{0:T(256)} %copy-done.27) | copy-start | bytes 3076
  934.5 14.0 %copy-start.38 = (f32[2,128]{1,0:T(2,128)S(1)}, f32[2,128]{1,0:T(2,128)}, u32[]{:S(2)}) copy-start(f32[2,128]{1,0:T(2,128)} %get-tuple-element.47) | copy-start | bytes 3076
  948.7 7.2 copy-start.13
  955.9 5.0 copy-start.10
  960.9 9.5 copy-start.6
  1129.1 7.3 copy-start.7
  1129.1 7.3 copy-start.36
  1136.4 4.3 copy-start.2
  1136.4 4.3 copy-start.15
  (22 other events, 47.9 us)

commit v4 on v3

--- a/solution.py
+++ b/solution.py
@@ -518,6 +518,10 @@
     def keep(self, i):
         return pltpu.make_async_copy(self.shards[i], self.outs[i].at[self.z, self.e], self.local.at[0, i])
 
+    def kept(self):
+        for i in range(len(self.outs)):
+            self.keep(i).wait()
+
     def launch(self, j):
         z, e, zz, mine = self.z, self.e, self.zz(j), j == 0
         if not mine:
@@ -558,23 +562,26 @@
         self.arrived(self.Y2, zz, self.d, self.HIGH)
         self.start(self.PDY, zz, self.d, self.HIGH, (self.z, self.p))
 
-    def shared(self, j):
+    def shared_near(self, j):
         zz, p = self.zz(j), self.p
         self.arrived(self.P0, zz, p, self.WHOLE)
         self.arrived(self.PXQ, zz, p ^ 2, self.Q3)
+        self.arrived(self.PX3, zz, p ^ 2, self.LOW3)
+
+    def shared_far(self, j):
+        zz, p = self.zz(j), self.p
         self.arrived(self.PYQ, zz, p ^ 4, self.Q0)
-        self.arrived(self.PX3, zz, p ^ 2, self.LOW3)
         self.arrived(self.PY3, zz, p ^ 4, self.HIGH3)
         self.arrived(self.PDX, zz, p ^ 6, self.LOW)
         self.arrived(self.PDY, zz, p ^ 6, self.HIGH)
 
-    def drain(self, j):
+    def drain(self, j, kept=False):
         zz, e, mine = self.zz(j), self.e, j == 0
         if mine:
             self.sent(self.XQ, zz, e, self.Q3, mine)
             self.sent(self.YQ, zz, e, self.Q0, mine)
-            for i in range(len(self.outs)):
-                self.keep(i).wait()
+            if not kept:
+                self.kept()
         for kind, ee, piece in ((self.Z, e, self.WHOLE), (self.ZX, self.x, self.Q3), (self.ZY, self.y, self.Q0)):
             self.along(j, kind, ee, piece, lambda c: c.wait_send())
         self.sent(self.X3, zz, e, self.LOW3, mine)
@@ -606,7 +613,8 @@
     for step in g.steps():
         step()
     for j in range(nz):
-        g.shared(j)
+        g.shared_near(j)
+        g.shared_far(j)
     for j in range(nz):
         g.drain(j)
 
@@ -887,79 +895,6 @@
     return lax.dot_general(a, b, (((da,), (db,)), ((), ())), preferred_element_type=F32)
 
 
-def expert_kernel(group, cap, x_ref, g_ref, gate_ref, rank_ref, wg_ref, wu_ref, wd_ref,
-                  y_ref, r_ref, gg_ref, rows_ref, down_ref, act_ref, gp_ref, up_ref, cot_ref):
-    length, width = x_ref.shape[1:]
-    slot = lax.broadcasted_iota(jnp.int32, (cap, length), 0).astype(F32)
-    picks, gates = [], []
-    for s in range(group):
-        hit = slot == rank_ref[s]
-        pick = hit.astype(BF16)
-        picks.append(pick)
-        gate = jnp.sum(jnp.where(hit, gate_ref[s], 0.0), 1, keepdims=True)
-        gates.append(gate)
-        at = pl.ds(s * cap, cap)
-        rows_ref[at, :] = mm(pick, x_ref[s]).astype(BF16)
-        cot = mm(pick, g_ref[s])
-        cot_ref[at, :] = cot.astype(BF16)
-        down_ref[at, :] = (gate * cot).astype(BF16)
-    gate_all = jnp.concatenate(gates, 0)
-    rows = rows_ref[...]
-    pre_gate = mm(rows, wg_ref[...])
-    pre_up = mm(rows, wu_ref[...])
-    sig = jax.nn.sigmoid(pre_gate)
-    silu = pre_gate * sig
-    act_ref[...] = (silu * pre_up).astype(BF16)
-    act_grad = mm(down_ref[...], wd_ref[...], 1, 1)
-    gp_ref[...] = (act_grad * pre_up * sig * (1.0 + pre_gate * (1.0 - sig))).astype(BF16)
-    up_ref[...] = (act_grad * silu).astype(BF16)
-    tile = 512
-    gg = jnp.zeros((group * cap, 1), F32)
-    for n in range(width // tile):
-        cols = pl.ds(n * tile, tile)
-        out = mm(act_ref[...], wd_ref[:, cols]).astype(BF16).astype(F32)
-        gg = gg + jnp.sum(out * cot_ref[:, cols].astype(F32), 1, keepdims=True)
-        out = (out * gate_all).astype(BF16)
-        back = (mm(gp_ref[...], wg_ref[cols, :], 1, 1) + mm(up_ref[...], wu_ref[cols, :], 1, 1)).astype(BF16)
-        for s in range(group):
-            part = slice(s * cap, (s + 1) * cap)
-            y_ref[s, :, cols] = mm(picks[s], out[part], 0, 0).astype(BF16)
-            r_ref[s, :, cols] = mm(picks[s], back[part], 0, 0).astype(BF16)
-    for s in range(group):
-        gg_ref[s] = jnp.sum(picks[s].astype(F32) * gg[s * cap : (s + 1) * cap], 0, keepdims=True)
-
-
-def experts(x, g, gate, rank, wg, wu, wd, cap, group):
-    devices, length, width = x.shape
-    ff = wg.shape[1]
-    rows = devices * cap
-    step = group * cap
-    block = lambda *tail: pl.BlockSpec((group,) + tail, lambda i: (i,) + (0,) * len(tail))
-    flat = lambda n: pl.BlockSpec((step, n), lambda i: (i, 0))
-    whole = lambda a: pl.BlockSpec(a.shape, lambda i: (0, 0), pipeline_mode=pl.Buffered(1))
-    return pl.pallas_call(
-        functools.partial(expert_kernel, group, cap),
-        grid=(devices // group,),
-        in_specs=[block(length, width), block(length, width), block(1, length), block(1, length),
-                  whole(wg), whole(wu), whole(wd)],
-        out_specs=[block(length, width), block(length, width), block(1, length),
-                   flat(width), flat(width), flat(ff), flat(ff), flat(ff)],
-        out_shape=[
-            jax.ShapeDtypeStruct((devices, length, width), BF16),
-            jax.ShapeDtypeStruct((devices, length, width), BF16),
-            jax.ShapeDtypeStruct((devices, 1, length), F32),
-            jax.ShapeDtypeStruct((rows, width), BF16),
-            jax.ShapeDtypeStruct((rows, width), BF16),
-            jax.ShapeDtypeStruct((rows, ff), BF16),
-            jax.ShapeDtypeStruct((rows, ff), BF16),
-            jax.ShapeDtypeStruct((rows, ff), BF16),
-        ],
-        scratch_shapes=[pltpu.VMEM((step, width), BF16)],
-        compiler_params=pltpu.CompilerParams(vmem_limit_bytes=VMEM_LIMIT, dimension_semantics=("arbitrary",)),
-        name="experts",
-    )(x, g, gate, rank, wg, wu, wd)
-
-
 def rope(values, cosine, sine):
     return values * cosine + pltpu.roll(values, values.shape[1] // 2, 1) * sine
 
@@ -992,11 +927,7 @@
         value.start()
         for c in self.fetch(0, 0):
             c.start()
-        length = self.seg_col.shape[0]
-        row = lax.broadcasted_iota(jnp.int32, (length, length), 0)
-        col = lax.broadcasted_iota(jnp.int32, (length, length), 1)
-        same = self.seg_col[...] == self.seg_row[...]
-        self.mask[...] = jnp.where(jnp.logical_and(same, col <= row), 1.0, 0.0)
+        self.mask[...] = allowed_mask(self.seg_col, self.seg_row)
         self.gain_grads[...] = jnp.zeros_like(self.gain_grads)
         key.wait()
         value.wait()
@@ -1145,6 +1076,411 @@
     return total.reshape(4 * shape[0], shape[1]), grads, gain_grads
 
 
+TILE = 512
+
+
+class ExpertWork:
+    def __init__(self, nz, cap, group, all_rows, all_tables, all_grads, weights, outs, bufs, sems):
+        self.nz, self.cap, self.group = nz, cap, group
+        self.all_rows, self.all_tables, self.all_grads = all_rows, all_tables, all_grads
+        self.weights, self.outs, self.bufs, self.sems = weights, outs, bufs, sems
+        self.z, self.e = place()
+        self.width = all_rows.shape[1]
+        self.per = self.width // group
+
+    def weight_copies(self):
+        return [pltpu.make_async_copy(w, b, self.sems.at[0, i]) for i, (w, b) in enumerate(zip(self.weights, self.bufs[:3]))]
+
+    def inputs(self, t, slot):
+        j, part = t // self.per, lax.rem(t, self.per)
+        at = self.block(part)
+        zz = line_place(self.z, self.nz, j)
+        x, tab, g = self.bufs[3:6]
+        return (
+            pltpu.make_async_copy(self.all_rows.at[zz, at], x.at[slot], self.sems.at[1 + slot, 0]),
+            pltpu.make_async_copy(self.all_tables.at[zz, at], tab.at[slot], self.sems.at[1 + slot, 1]),
+            pltpu.make_async_copy(self.all_grads.at[zz, at], g.at[slot], self.sems.at[1 + slot, 2]),
+        )
+
+    def flat(self, t):
+        step = self.group * self.cap
+        return pl.ds(pl.multiple_of(t * step, step), step)
+
+    def row_results(self, t):
+        pairs = zip(self.bufs[8:10], self.outs[3:5])
+        return [pltpu.make_async_copy(b, o.at[self.flat(t)], self.sems.at[3, i]) for i, (b, o) in enumerate(pairs)]
+
+    def hidden_results(self, t):
+        pairs = zip(self.bufs[10:13], self.outs[5:8])
+        return [pltpu.make_async_copy(b, o.at[self.flat(t)], self.sems.at[3, 2 + i]) for i, (b, o) in enumerate(pairs)]
+
+    def term_results(self, t, n, cols):
+        at = self.block(lax.rem(t, self.per))
+        zz = line_place(self.z, self.nz, t // self.per)
+        pairs = zip(self.bufs[6:8], self.outs[:2])
+        return [
+            pltpu.make_async_copy(b.at[:, :, cols], o.at[zz, at, :, cols], self.sems.at[4 + i, n])
+            for i, (b, o) in enumerate(pairs)
+        ]
+
+    def begin(self):
+        for c in self.weight_copies():
+            c.start()
+
+    def block(self, part):
+        near = self.e // self.group
+        return pl.ds(jnp.where(part == 0, near, 1 - near) * self.group, self.group)
+
+    def ready(self, j, part):
+        for c in self.inputs(jnp.int32(j * self.per + part), part):
+            c.start()
+
+    def step(self, t, hook):
+        slot = lax.rem(t, 2)
+        hook(0)
+        cap, group = self.cap, self.group
+        wg, wu, wd, xb, tb, gb, yb, rb, rowb, downb, actb, gpb, upb, cotb = self.bufs
+        for c in self.inputs(t, slot):
+            c.wait()
+
+        @pl.when(t == 0)
+        def _():
+            for c in self.weight_copies():
+                c.wait()
+
+        self.free(t, self.row_results)
+        length, width = xb.shape[2] * xb.shape[3], xb.shape[4]
+        lanes = tb.shape[4]
+        me = self.z * self.width + self.e
+        total = self.nz * self.width
+        lane = lax.broadcasted_iota(jnp.int32, (8, lanes), 1)
+        row = lax.broadcasted_iota(jnp.int32, (8, lanes), 0)
+        gate_lanes = jnp.logical_and(row == 0, jnp.logical_or(lane == me, lane == total + me))
+        rank_lane = jnp.logical_and(row == 1, lane == 2 * total + me)
+        select = jnp.where(jnp.logical_or(gate_lanes, rank_lane), 1.0, 0.0).astype(BF16)
+        slots = lax.broadcasted_iota(jnp.int32, (cap, length), 0).astype(F32)
+        picks, gates = [], []
+        for s in range(group):
+            info = mm(select, tb[slot, s].reshape(length, lanes), 1, 1)
+            hit = slots == info[1:2]
+            pick = hit.astype(BF16)
+            picks.append(pick)
+            gate = jnp.sum(jnp.where(hit, info[0:1], 0.0), 1, keepdims=True)
+            gates.append(gate)
+            at = pl.ds(s * cap, cap)
+            rowb[at, :] = mm(pick, xb[slot, s].reshape(length, width)).astype(BF16)
+            cot = mm(pick, gb[slot, s].reshape(length, width))
+            cotb[at, :] = cot.astype(BF16)
+            downb[at, :] = (gate * cot).astype(BF16)
+        for c in self.row_results(t):
+            c.start()
+        hook(1)
+        gate_all = jnp.concatenate(gates, 0)
+        rows = rowb[...]
+        pre_gate = mm(rows, wg[...])
+        pre_up = mm(rows, wu[...])
+        sig = jax.nn.sigmoid(pre_gate)
+        silu = pre_gate * sig
+        self.free(t, self.hidden_results)
+        actb[...] = (silu * pre_up).astype(BF16)
+        hook(2)
+        act_grad = mm(downb[...], wd[...], 1, 1)
+        gpb[...] = (act_grad * pre_up * sig * (1.0 + pre_gate * (1.0 - sig))).astype(BF16)
+        upb[...] = (act_grad * silu).astype(BF16)
+        for c in self.hidden_results(t):
+            c.start()
+        gg = jnp.zeros((group * cap, 1), F32)
+        for n in range(width // TILE):
+            hook(3 + n)
+            cols = pl.ds(n * TILE, TILE)
+            self.free(t, lambda s: self.term_results(s, n, cols))
+            out = mm(actb[...], wd[:, cols]).astype(BF16).astype(F32)
+            gg = gg + jnp.sum(out * cotb[:, cols].astype(F32), 1, keepdims=True)
+            out = (out * gate_all).astype(BF16)
+            back = (mm(gpb[...], wg[cols, :], 1, 1) + mm(upb[...], wu[cols, :], 1, 1)).astype(BF16)
+            for s in range(group):
+                part = slice(s * cap, (s + 1) * cap)
+                yb[s, :, cols] = mm(picks[s], out[part], 0, 0).astype(BF16)
+                rb[s, :, cols] = mm(picks[s], back[part], 0, 0).astype(BF16)
+            for c in self.term_results(t, n, cols):
+                c.start()
+        near = self.e // group
+        block = jnp.where(lax.rem(t, self.per) == 0, near, 1 - near)
+        first = line_place(self.z, self.nz, t // self.per) * self.width + block * group
+        for s in range(group):
+            self.outs[2][first + s] = jnp.sum(
+                picks[s].astype(F32) * gg[s * cap : (s + 1) * cap], 0, keepdims=True
+            )
+
+    def free(self, t, copies):
+        @pl.when(t > 0)
+        def _():
+            for c in copies(t - 1):
+                c.wait()
+
+    def end(self):
+        t = jnp.int32(self.nz * self.per - 1)
+        for c in self.row_results(t) + self.hidden_results(t):
+            c.wait()
+        for n in range(self.bufs[13].shape[1] // TILE):
+            for c in self.term_results(t, n, pl.ds(n * TILE, TILE)):
+                c.wait()
+
+
+def line_place(z, nz, j):
+    near = jnp.minimum(z, nz - 1 - z)
+    step = (j + 1) // 2
+    zigzag = jnp.where(lax.rem(j, 2) == 0, z + step, z - step)
+    tail = jnp.where(z < nz - 1 - z, j, nz - 1 - j)
+    return jnp.where(j <= 2 * near, zigzag, tail)
+
+
+def gather_expert_kernel(nz, cap, group, *refs):
+    shards, all_grads, weights = refs[:2], refs[2], refs[3:6]
+    gathered, outs = refs[6:8], refs[8:16]
+    send, recv, local = refs[16:19]
+    bufs, sems = refs[19:33], refs[33]
+    z, e = place()
+    greet(z, e, nz)
+    g = Gather(nz, shards, gathered, send, recv, local)
+    w = ExpertWork(nz, cap, group, gathered[0], gathered[1], all_grads, weights, outs, bufs, sems)
+    w.begin()
+    edge = jnp.logical_or(z == 0, z == nz - 1)
+    plans = RELAYS.get(nz) or (relays_first(g, nz),) * 2
+
+    def run(name):
+        kind, j = name[0], int(name[1:])
+        if kind == "N":
+            g.shared_near(j)
+            if j == 0:
+                g.kept()
+            w.ready(j, 0)
+        elif kind == "A":
+            g.shared_far(j)
+            w.ready(j, 1)
+        else:
+            {"L": g.launch, "M": g.mates, "R": g.relay, "F": g.finish}[kind](j)
+
+    def body(t, _):
+        def hook(k):
+            for plan, here in zip(plans, (edge, jnp.logical_not(edge))):
+                for piece, part, names in plan:
+                    if part == k:
+                        @pl.when(jnp.logical_and(t == piece, here))
+                        def _():
+                            for name in names.split():
+                                run(name)
+
+        w.step(t, hook)
+        return 0
+
+    lax.fori_loop(0, nz * w.per, body, 0)
+    w.end()
+    for j in range(nz):
+        g.drain(j, True)
+
+
+def relays_first(g, nz):
+    names = [{"launch": "L", "mates": "M", "relay": "R", "finish": "F"}[f.func.__name__] + str(f.args[0]) for f in g.steps()]
+    head = [(0, 0, n) for n in names]
+    return head + [(2 * j, 0, "N%d" % j) for j in range(nz)] + [(2 * j + 1, 0, "A%d" % j) for j in range(nz)]
+
+
+RELAYS = {
+    4: (
+        (
+            (0, 0, "L0 M0 L1"), (0, 0, "R0 N0"), (0, 2, "M1"), (0, 6, "R1"), (1, 0, "N1 F0 A0 L2"), (1, 2, "F1"), (1, 5, "M2 A1"),
+            (2, 6, "R2"), (3, 1, "N2"), (3, 5, "L3"), (4, 0, "F2"), (4, 2, "A2"), (4, 4, "M3"), (5, 2, "R3"), (5, 5, "N3"),
+            (6, 3, "F3"), (6, 6, "A3"),
+        ),
+        (
+            (0, 0, "L0 M0 L1"), (0, 0, "R0 L2 N0"), (0, 2, "M1 M2"), (0, 6, "R1"), (1, 0, "N1 F0 A0 L3"), (1, 6, "M3 R2"), (2, 2, "N2"),
+            (2, 6, "F1"), (3, 0, "A1"), (3, 6, "R3"), (4, 1, "N3"), (4, 6, "F2"), (5, 0, "A2"), (5, 2, "F3"), (5, 5, "A3"),
+        ),
+    )
+}
+
+
+def gather_with_experts(rows, table, all_grads, w_gate, w_up, w_down, cap, collective_id):
+    nz, width = lax.axis_size("dp"), lax.axis_size("expert")
+    devices, group = nz * width, 4
+    length, model = rows.shape
+    ff = w_gate.shape[1]
+    quarter = length // 4
+    shards = [a.reshape(4, quarter, a.shape[1]) for a in (rows, table)]
+    step, picked = group * cap, devices * cap
+    vmem = pl.BlockSpec(memory_space=pltpu.VMEM)
+    hbm = pl.BlockSpec(memory_space=pl.ANY)
+    block = lambda a: pltpu.VMEM((2, group) + a.shape, a.dtype)
+    shape = lambda *dims: jax.ShapeDtypeStruct(dims, BF16)
+    outs = pl.pallas_call(
+        functools.partial(gather_expert_kernel, nz, cap, group),
+        out_shape=[shape(nz, width, *s.shape) for s in shards]
+        + [
+            shape(nz, width, length, model),
+            shape(nz, width, length, model),
+            jax.ShapeDtypeStruct((devices, 1, length), F32),
+            shape(picked, model),
+            shape(picked, model),
+            shape(picked, ff),
+            shape(picked, ff),
+            shape(picked, ff),
+        ],
+        in_specs=[vmem, vmem, hbm, hbm, hbm, hbm],
+        out_specs=[hbm, hbm, hbm, hbm, vmem, hbm, hbm, hbm, hbm, hbm],
+        scratch_shapes=gather_scratch(nz, 2)
+        + [pltpu.VMEM(w.shape, BF16) for w in (w_gate, w_up, w_down)]
+        + [block(shards[0]), block(shards[1]), block(shards[0])]
+        + [pltpu.VMEM((group, length, model), BF16)] * 2
+        + [pltpu.VMEM((step, n), BF16) for n in (model, model, ff, ff, ff, model)]
+        + [pltpu.SemaphoreType.DMA((6, max(5, model // TILE)))],
+        compiler_params=pltpu.CompilerParams(
+            collective_id=collective_id, has_side_effects=True, vmem_limit_bytes=VMEM_LIMIT
+        ),
+        name="gather_experts",
+    )(*shards, all_grads.reshape((nz, width) + shards[0].shape), w_gate, w_up, w_down)
+    return outs[2:]
+
+
+class Attention:
+    def __init__(self, hidden, gain, w_mixed, w_out, tables, gains, seg_col, seg_row, raw, normed, attended, branch,
+                 w_buf, o_buf, kv_buf, mask, k_rot, v_low, sems):
+        self.hidden, self.gain, self.w_mixed, self.w_out = hidden, gain, w_mixed, w_out
+        self.tables, self.gains, self.seg_col, self.seg_row = tables, gains, seg_col, seg_row
+        self.raw, self.normed, self.attended, self.branch = raw, normed, attended, branch
+        self.w_buf, self.o_buf, self.kv_buf, self.mask = w_buf, o_buf, kv_buf, mask
+        self.k_rot, self.v_low, self.sems = k_rot, v_low, sems
+        self.cols = o_buf.shape[1]
+        self.query_cols = w_out.shape[0]
+        self.key_cols = kv_buf.shape[1] // 2
+        self.count = self.query_cols // self.cols
+        self.per_key = self.count // (self.key_cols // HEAD_DIM)
+
+    def fetch(self, t, slot):
+        at = pl.ds(pl.multiple_of(t * self.cols, self.cols), self.cols)
+        return (
+            pltpu.make_async_copy(self.w_mixed.at[:, at], self.w_buf.at[slot], self.sems.at[0, slot]),
+            pltpu.make_async_copy(self.w_out.at[at, :], self.o_buf.at[slot], self.sems.at[1, slot]),
+        )
+
+    def prepare(self):
+        kv = pltpu.make_async_copy(
+            self.w_mixed.at[:, pl.ds(self.query_cols, 2 * self.key_cols)], self.kv_buf, self.sems.at[2, 0]
+        )
+        kv.start()
+        for c in self.fetch(0, 0):
+            c.start()
+        values = self.hidden[...].astype(F32)
+        scale = lax.rsqrt(jnp.mean(values * values, 1, keepdims=True) + EPS)
+        self.normed[...] = (values * scale * self.gain[...]).astype(BF16)
+        self.branch[...] = jnp.zeros_like(self.branch)
+        self.mask[...] = allowed_mask(self.seg_col, self.seg_row)
+        kv.wait()
+        self.raw[:, self.query_cols :] = mm(self.normed[...], self.kv_buf[...])
+
+    def step(self, t):
+        slot = lax.rem(t, 2)
+
+        @pl.when(t + 1 < self.count)
+        def _():
+            for c in self.fetch(t + 1, 1 - slot):
+                c.start()
+
+        for c in self.fetch(t, slot):
+            c.wait()
+        cosine, sine = self.tables[0], self.tables[1]
+
+        @pl.when(lax.rem(t, self.per_key) == 0)
+        def _():
+            shift = pl.multiple_of(t // self.per_key * HEAD_DIM, HEAD_DIM)
+            key = head_norm(self.raw[:, pl.ds(self.query_cols + shift, HEAD_DIM)], self.gains[1:2, :])
+            self.k_rot[...] = rope(key, cosine, sine).astype(BF16)
+            self.v_low[...] = self.raw[:, pl.ds(self.query_cols + self.key_cols + shift, HEAD_DIM)].astype(BF16)
+
+        at = pl.ds(pl.multiple_of(t * self.cols, self.cols), self.cols)
+        query_raw = mm(self.normed[...], self.w_buf[slot])
+        self.raw[:, at] = query_raw
+        mask = self.mask[...] > 0.0
+        k_rot, v_low = self.k_rot[...], self.v_low[...]
+        outs = []
+        for h in range(self.cols // HEAD_DIM):
+            query = head_norm(query_raw[:, h * HEAD_DIM : (h + 1) * HEAD_DIM], self.gains[0:1, :])
+            q_rot = rope(query, cosine, sine).astype(BF16)
+            scores = mm(q_rot, k_rot, 1, 1) * (1.0 / math.sqrt(HEAD_DIM))
+            raised = jnp.where(mask, jnp.exp(scores), 0.0)
+            probs = (raised / jnp.sum(raised, 1, keepdims=True)).astype(BF16)
+            outs.append(mm(probs, v_low).astype(BF16))
+        out = jnp.concatenate(outs, 1)
+        self.attended[:, at] = out
+        self.branch[...] += mm(out, self.o_buf[slot])
+
+
+def head_norm(raw, gain):
+    return raw * lax.rsqrt(jnp.mean(raw * raw, 1, keepdims=True) + EPS) * gain
+
+
+def allowed_mask(seg_col, seg_row):
+    length = seg_col.shape[0]
+    row = lax.broadcasted_iota(jnp.int32, (length, length), 0)
+    col = lax.broadcasted_iota(jnp.int32, (length, length), 1)
+    same = seg_col[...] == seg_row[...]
+    return jnp.where(jnp.logical_and(same, col <= row), 1.0, 0.0)
+
+
+def gather_attention_kernel(nz, plan, shard, hidden, gain, w_mixed, w_out, tables, gains, seg_col, seg_row,
+                            gathered, raw, normed, attended, branch, *scratch):
+    z, e = place()
+    greet(z, e, nz)
+    g = Gather(nz, [shard], [gathered], *scratch[:3])
+    a = Attention(hidden, gain, w_mixed, w_out, tables, gains, seg_col, seg_row, raw, normed, attended, branch, *scratch[3:])
+    steps = g.steps()
+    steps[0]()
+    a.prepare()
+    run_beside(a.count, a.step, steps[1:], plan)
+    for j in range(nz):
+        g.shared_near(j)
+        g.shared_far(j)
+    for j in range(nz):
+        g.drain(j)
+
+
+def gather_with_attention(rows, hidden, gain, w_mixed, w_out, tables, gains, segments, collective_id):
+    nz, width = lax.axis_size("dp"), lax.axis_size("expert")
+    length, model = hidden.shape
+    shard = rows.reshape(4, rows.shape[0] // 4, rows.shape[1])
+    cols = 4 * HEAD_DIM
+    mixed, query_cols = w_mixed.shape[1], w_out.shape[0]
+    vmem = pl.BlockSpec(memory_space=pltpu.VMEM)
+    hbm = pl.BlockSpec(memory_space=pl.ANY)
+    gathered, raw, normed, attended, branch = pl.pallas_call(
+        functools.partial(gather_attention_kernel, nz, [1, 0, 1, 1, 0, 1, 2, 2]),
+        out_shape=[
+            jax.ShapeDtypeStruct((nz, width) + shard.shape, shard.dtype),
+            jax.ShapeDtypeStruct((length, mixed), F32),
+            jax.ShapeDtypeStruct((length, model), BF16),
+            jax.ShapeDtypeStruct((length, query_cols), BF16),
+            jax.ShapeDtypeStruct((length, model), F32),
+        ],
+        in_specs=[vmem, vmem, vmem, hbm, hbm, vmem, vmem, vmem, vmem],
+        out_specs=[hbm, vmem, vmem, vmem, vmem],
+        scratch_shapes=gather_scratch(nz, 1)
+        + [
+            pltpu.VMEM((2, model, cols), BF16),
+            pltpu.VMEM((2, cols, model), BF16),
+            pltpu.VMEM((model, mixed - query_cols), BF16),
+            pltpu.VMEM((length, length), F32),
+            pltpu.VMEM((length, HEAD_DIM), BF16),
+            pltpu.VMEM((length, HEAD_DIM), BF16),
+            pltpu.SemaphoreType.DMA((3, 2)),
+        ],
+        compiler_params=pltpu.CompilerParams(
+            collective_id=collective_id, has_side_effects=True, vmem_limit_bytes=VMEM_LIMIT
+        ),
+        name="gather_attention",
+    )(shard, hidden, gain, w_mixed, w_out, tables, gains, segments[:, None], segments[None, :])
+    return gathered, raw, normed, attended, branch
+
+
 def pack_columns(columns, rows, lanes, dtype):
     parts = [c.astype(dtype) for c in columns]
     used = sum(c.shape[1] for c in parts)
@@ -1197,25 +1533,16 @@
     query_gain = heads_of[:, :, experts_total + 2].reshape(-1)
     key_gain = heads_of[:, :, experts_total + 3].reshape(-1)
 
-    group_size = HEADS // KV_HEADS
     plain_in = hidden_in.astype(F32)
     inv_attn = rms_scale(plain_in)
-    normed_attn = (plain_in * inv_attn * attn_gain).astype(BF16)
-    mixed = jnp.dot(normed_attn, w_mixed, preferred_element_type=F32)
-    query_raw = mixed[:, :query_cols].reshape(length, HEADS, HEAD_DIM)
-    key_raw = mixed[:, query_cols : query_cols + key_cols].reshape(length, KV_HEADS, HEAD_DIM)
-    value_rows = mixed[:, query_cols + key_cols :].astype(BF16).reshape(length, KV_HEADS, HEAD_DIM)
-    query_scale = rms_scale(query_raw)
-    key_scale = rms_scale(key_raw)
     cosine_table, sine_table = rope_tables(jnp.arange(length) % TOK_DEV, HEAD_DIM)
-    query_rot = rotate(query_raw * query_scale * query_gain, cosine_table, sine_table).astype(BF16)
-    query_rot = query_rot.reshape(length, KV_HEADS, group_size, HEAD_DIM)
-    key_rot = rotate(key_raw * key_scale * key_gain, cosine_table, sine_table).astype(BF16)
-    position = jnp.arange(length)
-    allowed = (segment_ids[:, None] == segment_ids[None, :]) & (position[None, :] <= position[:, None])
-    attended, log_totals = attend(query_rot, key_rot, value_rows, allowed)
-    attended = attended.reshape(length, HEADS * HEAD_DIM)
-    residual = plain_in + jnp.dot(attended, w_out, preferred_element_type=F32)
+    cosine, sine = cosine_table[:, 0], sine_table[:, 0]
+    tables = jnp.stack([jnp.concatenate([cosine, cosine], 1), jnp.concatenate([-sine, sine], 1)])
+    head_gains = jnp.stack([query_gain, key_gain]).astype(F32)
+    all_grads, mixed, normed_attn, attended, branch = gather_with_attention(
+        out_grad, hidden_in, attn_gain.astype(F32)[None, :], w_mixed, w_out, tables, head_gains, segment_ids, 3
+    )
+    residual = plain_in + branch
 
     inv_mlp = rms_scale(residual)
     normed_mlp = (residual * inv_mlp * mlp_gain).astype(BF16)
@@ -1223,21 +1550,15 @@
     chosen = jnp.any(expert_ids[:, :, None] == jnp.arange(experts_total)[None, None, :], 1)
     raised = jnp.where(chosen, jnp.exp(logits), 0.0)
     gate = raised / jnp.sum(raised, -1, keepdims=True)
+    position = jnp.arange(length)
     not_after = (position[None, :] <= position[:, None]).astype(BF16)
     rank = jnp.dot(not_after, chosen.astype(BF16), preferred_element_type=F32) - 1.0
     rank = jnp.where(chosen, rank, -1.0)
     gate_high = lax.reduce_precision(gate, 8, 7)
-    table = jnp.concatenate([gate_high, gate - gate_high, rank], 1).T.astype(BF16)
-
-    all_rows, all_tables = gather_all([normed_mlp, table], 2)
-    (all_grads,) = gather_all([out_grad], 3)
-    mine = lax.dynamic_index_in_dim(
-        all_tables.reshape(devices, 3, experts_total, length), me, 2, keepdims=False
-    ).astype(F32)
-    cube = (devices, length, width)
-    y_terms, r_terms, gate_terms, rows_in, down_in, act, gate_pre_grad, up_pre_grad = experts(
-        all_rows.reshape(cube), all_grads.reshape(cube), mine[:, :1] + mine[:, 1:2], mine[:, 2:],
-        w_gate[0], w_up[0], w_down[0], capacity, 4,
+    table = pack_columns([gate_high, gate - gate_high, rank], length, 128 * pl.cdiv(3 * experts_total, 128), BF16)
+
+    y_terms, r_terms, gate_terms, rows_in, down_in, act, gate_pre_grad, up_pre_grad = gather_with_experts(
+        normed_mlp, table, all_grads, w_gate[0], w_up[0], w_down[0], capacity, 2
     )
     is_me = (jnp.arange(experts_total) == me).astype(F32)
     gate_terms = (gate_terms * is_me[None, :, None]).reshape(devices * experts_total, length)
@@ -1256,9 +1577,6 @@
 
     branch_grad = residual_grad.astype(BF16)
     grad_w_output = jnp.dot(attended.T, branch_grad, preferred_element_type=F32).astype(BF16)
-    cosine, sine = cosine_table[:, 0], sine_table[:, 0]
-    tables = jnp.stack([jnp.concatenate([cosine, cosine], 1), jnp.concatenate([-sine, sine], 1)])
-    head_gains = jnp.stack([query_gain, key_gain]).astype(F32)
     mixed_out, mixed_grad, gain_grads = scatter_with_attention(
         y_terms.reshape(devices * length, width), branch_grad, w_out, mixed, tables, head_gains, segment_ids, 5
     )

time: 1150 us -> 1030 us (0.90)
  Pallas kernels: 962 us -> 899 us
  matrix products: 102 us -> 76.1 us
  local copies, waits for them, and re-layouts: 48.3 us -> 29.8 us
    pallas_call x3 -> x1, Pallas kernels: 438 us -> 155 us  [gather_all(): pl.pallas_call(functools.partial(gather_kernel, nz, count), out_shape=[ja...]
    pallas_call x1 -> x2, Pallas kernels: 93.2 us -> 309 us  [the longest x1 169 us: gather_with_experts(): pl.pallas_call(functools.partial(gather_expert_kernel, nz, cap, group), o...]
    dot_general x4 -> x0, matrix products: 26.3 us -> none  [the longest x1 10.1 us: per_device_gather(): mixed = jnp.dot(normed_attn, w_mixed, preferred_element_type=F32)]
where the time goes in v4:
time: 1030 us
  Pallas kernels  899 us (87%)
  matrix products  76.1 us (7%)
  local copies, waits for them, and re-layouts  29.8 us (3%)
  other arithmetic  20.3 us (2%)
    pallas_call x2, Pallas kernels, scatter_sum(): pl.pallas_call(functools.partial(scatter_kernel, nz, count), out_shape=[j...  294 us
    pallas_call x1, Pallas kernels, gather_with_experts(): pl.pallas_call(functools.partial(gather_expert_kernel, nz, cap, group), o...  169 us
    pallas_call x1, Pallas kernels, gather_all(): pl.pallas_call(functools.partial(gather_kernel, nz, count), out_shape=[ja...  155 us
    pallas_call x1, Pallas kernels, gather_with_attention(): pl.pallas_call(functools.partial(gather_attention_kernel, nz, [1, 0, 1, 1...  141 us
    pallas_call x1, Pallas kernels, scatter_with_attention(): pl.pallas_call(functools.partial(scatter_attention_kernel, nz, plan), out...  140 us

profile of v4, /device:TPU:0, one launch (start us, length us, event | category | flops | bytes accessed | tf_op | source)
XLA Modules:
  0.0 1026.9 jit_solution(16246268522992938310)
XLA Ops:
  2.1 2.0 pad_maximum_fusion
  5.6 155.4 %gather_all.1 = (bf16[4,8,4,16,5120]{4,3,2,1,0:T(8,128)(2,1)}, bf16[4,8,4,32,2048]{4,3,2,1,0:T(8,128)(2,1)}, bf16[4,8,4,16,128]{4,3,2,1,0:T(8,128)(2,1)}) custom-call(bf16[4,16,5120]{2,1,0:T(8,128)(2,1)} %bitcast.95, bf16[4,32,2048]{2,1,0:T(8,128)(2,1)} %bitcast.100, bf16[4,16,128]{2,1,0:T(8,128)(2,1)} %concatenate.46.refs_2_), custom_call_target="tpu_custom_call" | custom-call | tf_op jit(solution)/shard_map/gather_all/pallas_call | solution.py:634
  162.9 2.5 slice_convert_fusion
  167.1 140.6 %gather_attention.1 = (bf16[4,8,4,64,2048]{4,3,2,1,0:T(8,128)(2,1)}, f32[256,5120]{1,0:T(8,128)}, bf16[256,2048]{1,0:T(8,128)(2,1)}, bf16[256,4096]{1,0:T(8,128)(2,1)}, f32[256,2048]{1,0:T(8,128)}) custom-call(bf16[4,64,2048]{2,1,0:T(8,128)(2,1)} %bitcast.91, bf16[256,2048]{1,0:T(8,128)(2,1)} %hidden.1, f32[1,2048]{1,0:T(1,128)} %bitcast.109, ...), custom_call_target="tpu_custom_call" | custom-call | tf_op jit(solution)/shard_map/gather_attention/pallas_call | solution.py:1455
  307.8 2.4 multiply_reduce_fusion.2
  310.2 2.3 copy.102
  315.3 168.9 %gather_experts.1 = (bf16[4,8,4,64,2048]{4,3,2,1,0:T(8,128)(2,1)}, bf16[4,8,4,64,128]{4,3,2,1,0:T(8,128)(2,1)}, bf16[4,8,256,2048]{3,2,1,0:T(8,128)(2,1)}, bf16[...) custom-call(bf16[4,64,2048]{2,1,0:T(8,128)(2,1)} %bitcast.85, ...), custom_call_target="tpu_custom_call" | custom-call | tf_op jit(solution)/shard_map/gather_experts/pallas_call | solution.py:1316
  484.2 14.5 %convolution_bitcast_fusion = f32[1,768,2048]{2,1,0:T(8,128)} fusion(bf16[2560,768]{1,0:T(8,128)(2,1)} %get-tuple-element.60, bf16[2560,2048]{1,0:T(8,128)(2,1)} %get-tuple-element.61), kind=kOutput, calls=%fused_computation.7 | convolution fusion | flops 8053063680 | bytes 20709376 | tf_op jit(solution)/shard_map/dot_general | solution.py:1566
  498.7 11.0 %convolution_bitcast_fusion.1 = f32[1,2048,768]{2,1,0:T(8,128)} fusion(bf16[2560,2048]{1,0:T(8,128)(2,1)S(1)} %copy-done.21, bf16[2560,768]{1,0:T(8,128)(2,1)S(1)} %copy-done.23), kind=kOutput, calls=%fused_computation.8 | convolution fusion | flops 8053063680 | bytes 20709376 | tf_op jit(solution)/shard_map/dot_general | solution.py:1568
  509.7 11.1 %convolution_bitcast_fusion.2 = f32[1,2048,768]{2,1,0:T(8,128)} fusion(bf16[2560,2048]{1,0:T(8,128)(2,1)S(1)} %copy-done.21, bf16[2560,768]{1,0:T(8,128)(2,1)S(1)} %copy-done.22), kind=kOutput, calls=%fused_computation.9 | convolution fusion | flops 8053063680 | bytes 20709376 | tf_op jit(solution)/shard_map/dot_general | solution.py:1567
  522.0 146.9 %scatter_sum.2 = (f32[4,64,2048]{2,1,0:T(8,128)}, f32[4,8,256]{2,1,0:T(8,128)}) custom-call(bf16[4,8,4,64,2048]{4,3,2,1,0:T(8,128)(2,1)} %bitcast.82, f32[4,8,4,8,256]{4,3,2,1,0:T(8,128)} %broadcast_multiply_fusion.refs_1_), custom_call_target="tpu_custom_call" | custom-call | tf_op jit(solution)/shard_map/scatter_sum/pallas_call | solution.py:880
  670.7 2.7 fusion.26
  673.4 2.5 multiply_reduce_fusion
  675.9 2.3 fusion.21
  678.2 140.0 %scatter_attention.1 = (f32[4,64,2048]{2,1,0:T(8,128)}, bf16[256,5120]{1,0:T(8,128)(2,1)}, f32[2,128]{1,0:T(2,128)}) custom-call(bf16[4,8,4,64,2048]{4,3,2,1,0:T(8,128)(2,1)} %bitcast.81, bf16[256,2048]{1,0:T(8,128)(2,1)} %get-tuple-element.70.branch, bf16[4096,2048]{1,0:T(8,128)(2,1)} %bitcast.80, f32[256,5120]{1,0:T(8,128)} %get-tuple-element.48.raw, ...), custom_call_target="tpu_custom_call" | custom-call | tf_op jit(solution)/shard_map/scatter_attention/pallas_call | solution.py:1049
  818.2 12.1 %fusion.6 = (f32[2048]{0:T(1024)S(1)}, f32[256]{0:T(256)S(1)}, f32[256,2048]{1,0:T(8,128)}) fusion(bf16[256,2048]{1,0:T(8,128)(2,1)} %hidden.1, f32[256]{0:T(256)S(1)} %get-tuple-element.89, f32[2048]{0:T(1024)S(1)} %bitcast.110, bf16[256,5120]{1,0:T(8,128)(2,1)} %get-tuple-element.50, bf16[2048,5120]{1,0:T(8,128)(2,1)} %bitcast.84), kind=kOutput, calls=%fused_computation.17 | convolution fusion | flops 5372377088 | bytes 26757120 | tf_op jit(solution)/shard_map/dot_general | solution.py:1586
  831.3 2.0 concatenate.62
  833.5 2.0 concatenate.63
  838.5 4.8 concatenate.55.refs_2_
  843.2 10.0 convolution_convert_fusion.1
  853.2 11.6 %convolution_convert_fusion = bf16[2048,5120]{1,0:T(8,128)(2,1)} fusion(bf16[256,2048]{1,0:T(8,128)(2,1)S(1)} %copy-done.10, bf16[256,5120]{1,0:T(8,128)(2,1)} %get-tuple-element.50), kind=kOutput, calls=%fused_computation | convolution fusion | flops 5379194880 | bytes 24641536 | tf_op jit(solution)/shard_map/dot_general | solution.py:1585
  864.9 147.4 %scatter_sum.3 = (f32[4,16,5120]{2,1,0:T(8,128)}, f32[4,32,2048]{2,1,0:T(8,128)}, f32[4,16,128]{2,1,0:T(8,128)}) custom-call(bf16[4,8,4,16,5120]{4,3,2,1,0:T(8,128)(2,1)} %bitcast.77, bf16[4,8,4,32,2048]{4,3,2,1,0:T(8,128)(2,1)} %bitcast.78, f32[4,8,4,16,128]{4,3,2,1,0:T(8,128)} %concatenate.55.refs_2_), custom_call_target="tpu_custom_call" | custom-call | tf_op jit(solution)/shard_map/scatter_sum/pallas_call | solution.py:880
  1012.3 2.4 slice.71
  1019.6 4.3 fusion.3
  (108 shorter events, 23.7 us)
Async XLA Ops:
  0.6 3.5 copy-start.24
  0.7 3.6 copy-start.25
  0.7 3.8 copy-start.16
  0.7 3.9 copy-start.19
  0.7 4.0 copy-start.20
  162.9 3.4 copy-start.15
  310.1 2.6 copy-start
  310.2 2.6 copy-start.17
  310.2 3.6 copy-start.6
  484.2 14.5 %copy-start.21 = (bf16[2560,2048]{1,0:T(8,128)(2,1)S(1)}, bf16[2560,2048]{1,0:T(8,128)(2,1)}, u32[]{:S(2)}) copy-start(bf16[2560,2048]{1,0:T(8,128)(2,1)} %get-tuple-element.57) | copy-start | bytes 31457284
  484.2 14.5 %copy-start.23 = (bf16[2560,768]{1,0:T(8,128)(2,1)S(1)}, bf16[2560,768]{1,0:T(8,128)(2,1)}, u32[]{:S(2)}) copy-start(bf16[2560,768]{1,0:T(8,128)(2,1)} %get-tuple-element.59) | copy-start | bytes 11796484
  498.7 11.0 %copy-start.22 = (bf16[2560,768]{1,0:T(8,128)(2,1)S(1)}, bf16[2560,768]{1,0:T(8,128)(2,1)}, u32[]{:S(2)}) copy-start(bf16[2560,768]{1,0:T(8,128)(2,1)} %get-tuple-element.58) | copy-start | bytes 11796484
  509.7 11.1 %copy-start.14 = (f32[32,1,256]{2,1,0:T(1,128)S(1)}, f32[32,1,256]{2,1,0:T(1,128)}, u32[]{:S(2)}) copy-start(f32[32,1,256]{2,1,0:T(1,128)} %get-tuple-element.45) | copy-start | bytes 98308
  669.0 4.4 copy-start.1
  673.4 2.5 copy-start.8
  678.2 140.0 %copy-start.13 = (f32[2048,1]{0,1:T(1,128)S(1)}, f32[2048,1]{0,1:T(1,128)}, u32[]{:S(2)}) copy-start(f32[2048,1]{0,1:T(1,128)} %copy.101) | copy-start | bytes 24580
  818.2 13.0 %copy-start.18 = (f32[2,128]{1,0:T(2,128)S(1)}, f32[2,128]{1,0:T(2,128)}, u32[]{:S(2)}) copy-start(f32[2,128]{1,0:T(2,128)} %get-tuple-element.53) | copy-start | bytes 3076
  831.3 7.1 copy-start.7
  838.5 4.8 copy-start.4
  843.2 10.0 copy-start.10
  1012.3 4.1 copy-start.12
  1012.3 7.3 copy-start.5
  1019.6 4.3 copy-start.2
  1019.6 4.3 copy-start.9
  (2 other events, 2.6 us)

commit v5 on v4

--- a/solution.py
+++ b/solution.py
@@ -437,12 +437,14 @@
     return z, e
 
 
-def line_order(z, nz, j):
+def line_order(z, nz, j, inner=False):
     near = jnp.minimum(z, nz - 1 - z)
     step = (j + 1) // 2
-    zigzag = z + (step if j % 2 == 0 else -step)
+    step = step if j % 2 == 0 else -step
+    if inner:
+        step = jnp.where(z < nz - 1 - z, -step, step)
     tail = jnp.where(z < nz - 1 - z, j, nz - 1 - j)
-    return jnp.where(j <= 2 * near, zigzag, tail)
+    return jnp.where(j <= 2 * near, z + step, tail)
 
 
 def greet(z, e, nz):
@@ -523,13 +525,20 @@
             self.keep(i).wait()
 
     def launch(self, j):
-        z, e, zz, mine = self.z, self.e, self.zz(j), j == 0
+        self.launch_line(j)
+        self.launch_plane(j)
+
+    def launch_line(self, j):
+        e, zz, mine = self.e, self.zz(j), j == 0
         if not mine:
             self.arrived(self.Z, zz, e, self.WHOLE)
         else:
-            self.start(self.XQ, zz, e, self.Q3, (z, self.x), mine)
-            self.start(self.YQ, zz, e, self.Q0, (z, self.y), mine)
+            self.start(self.XQ, zz, e, self.Q3, (self.z, self.x), mine)
+            self.start(self.YQ, zz, e, self.Q0, (self.z, self.y), mine)
         self.along(j, self.Z, e, self.WHOLE, lambda c: c.start())
+
+    def launch_plane(self, j):
+        z, e, zz, mine = self.z, self.e, self.zz(j), j == 0
         self.start(self.X3, zz, e, self.LOW3, (z, self.x), mine)
         self.start(self.Y3, zz, e, self.HIGH3, (z, self.y), mine)
         self.start(self.P0, zz, e, self.WHOLE, (z, self.p), mine)
@@ -675,7 +684,7 @@
         self.chips = (self.chip ^ 3, self.chip ^ 1, self.chip ^ 2, self.chip)
 
     def zz(self, j):
-        return line_order(self.z, self.nz, self.nz - 1 - j)
+        return line_order(self.z, self.nz, self.nz - 1 - j, True)
 
     def remote(self, i, kind, zz, src, dst, dev):
         return pltpu.make_async_remote_copy(
@@ -900,24 +909,45 @@
 
 
 class AttentionGrad:
-    def __init__(self, branch, w_out, raw, tables, gains, seg_col, seg_row, grads, gain_grads,
-                 w_buf, q_buf, k_buf, v_buf, mask, k_rot, v_low, dk, dv, sems):
+    def __init__(self, branch, w_out, raw, tables, gains, seg_col, seg_row, normed, attended, w_mixed,
+                 grads, gain_grads, normed_grad, grad_out, grad_mixed,
+                 w_buf, q_buf, k_buf, v_buf, mask, k_rot, v_low, dk, dv, a_buf, m_buf, out_stage, mixed_stage, sems):
+        self.normed, self.attended, self.w_mixed = normed, attended, w_mixed
+        self.normed_grad, self.grad_out, self.grad_mixed = normed_grad, grad_out, grad_mixed
+        self.a_buf, self.m_buf, self.out_stage, self.mixed_stage = a_buf, m_buf, out_stage, mixed_stage
         self.branch, self.w_out, self.raw, self.tables, self.gains = branch, w_out, raw, tables, gains
         self.seg_col, self.seg_row, self.grads, self.gain_grads = seg_col, seg_row, grads, gain_grads
         self.w_buf, self.q_buf, self.k_buf, self.v_buf, self.mask = w_buf, q_buf, k_buf, v_buf, mask
         self.k_rot, self.v_low, self.dk, self.dv, self.sems = k_rot, v_low, dk, dv, sems
-        self.cols = w_buf.shape[1]
+        self.cols = w_buf.shape[0]
         self.query_cols = w_out.shape[0]
         self.key_cols = k_buf.shape[1]
         self.count = self.query_cols // self.cols
         self.per_key = self.count // (self.key_cols // HEAD_DIM)
+        self.total = self.count + 2 * self.key_cols // self.cols
+
+    def at(self, t):
+        return pl.ds(pl.multiple_of(t * self.cols, self.cols), self.cols)
 
     def fetch(self, t, slot):
-        at = pl.ds(pl.multiple_of(t * self.cols, self.cols), self.cols)
+        at = self.at(t)
+        return pltpu.make_async_copy(self.raw.at[:, at], self.q_buf.at[slot], self.sems.at[1, slot])
+
+    def fetch_out(self, t):
+        at = self.at(t)
         return (
-            pltpu.make_async_copy(self.w_out.at[at, :], self.w_buf.at[slot], self.sems.at[0, slot]),
-            pltpu.make_async_copy(self.raw.at[:, at], self.q_buf.at[slot], self.sems.at[1, slot]),
+            pltpu.make_async_copy(self.w_out.at[at, :], self.w_buf, self.sems.at[0, 0]),
+            pltpu.make_async_copy(self.attended.at[:, at], self.a_buf, self.sems.at[3, 0]),
         )
+
+    def fetch_mixed(self, t):
+        return pltpu.make_async_copy(self.w_mixed.at[:, self.at(t)], self.m_buf, self.sems.at[4, 0])
+
+    def put_out(self, t):
+        return pltpu.make_async_copy(self.out_stage, self.grad_out.at[self.at(t), :], self.sems.at[5, 0])
+
+    def put_mixed(self, t):
+        return pltpu.make_async_copy(self.mixed_stage, self.grad_mixed.at[:, self.at(t)], self.sems.at[5, 1])
 
     def prepare(self):
         q, k = self.query_cols, self.key_cols
@@ -925,14 +955,17 @@
         value = pltpu.make_async_copy(self.raw.at[:, pl.ds(q + k, k)], self.v_buf, self.sems.at[2, 1])
         key.start()
         value.start()
-        for c in self.fetch(0, 0):
+        for c in self.fetch_out(0):
             c.start()
+        self.fetch(0, 0).start()
+        self.fetch_mixed(0).start()
+        self.normed_grad[...] = jnp.zeros_like(self.normed_grad)
         self.mask[...] = allowed_mask(self.seg_col, self.seg_row)
         self.gain_grads[...] = jnp.zeros_like(self.gain_grads)
         key.wait()
         value.wait()
 
-    def normed(self, raw, which):
+    def scaled(self, raw, which):
         scale = lax.rsqrt(jnp.mean(raw * raw, 1, keepdims=True) + EPS)
         return scale, (raw * scale) * self.gains[which : which + 1, :]
 
@@ -947,34 +980,70 @@
 
     def step(self, t):
         slot = lax.rem(t, 2)
-        last = t + 1 < self.count
-
-        @pl.when(last)
+
+        @pl.when(t + 1 < self.count)
         def _():
-            for c in self.fetch(t + 1, 1 - slot):
-                c.start()
-
-        for c in self.fetch(t, slot):
+            self.fetch(t + 1, 1 - slot).start()
+
+        @pl.when(t < self.count)
+        def _():
+            self.heads(t, slot)
+
+        self.fetch_mixed(t).wait()
+        grads = self.grads[:, self.at(t)]
+        self.normed_grad[...] += mm(grads, self.m_buf[...], 1, 1)
+
+        @pl.when(t + 1 < self.total)
+        def _():
+            self.fetch_mixed(t + 1).start()
+
+        @pl.when(t > 0)
+        def _():
+            self.put_mixed(t - 1).wait()
+
+        self.mixed_stage[...] = mm(self.normed[...], grads, 0, 0).astype(BF16)
+        self.put_mixed(t).start()
+
+    def end(self):
+        self.put_mixed(self.total - 1).wait()
+        self.put_out(self.count - 1).wait()
+
+    def heads(self, t, slot):
+        self.fetch(t, slot).wait()
+        for c in self.fetch_out(t):
             c.wait()
+
+        @pl.when(t > 0)
+        def _():
+            self.put_out(t - 1).wait()
+
+        self.out_stage[...] = mm(self.a_buf[...], self.branch[...], 0, 0).astype(BF16)
+        self.put_out(t).start()
         cosine, sine = self.tables[0], self.tables[1]
         at_key = pl.ds(pl.multiple_of(t // self.per_key * HEAD_DIM, HEAD_DIM), HEAD_DIM)
 
         @pl.when(lax.rem(t, self.per_key) == 0)
         def _():
-            _, key = self.normed(self.k_buf[:, at_key], 1)
+            _, key = self.scaled(self.k_buf[:, at_key], 1)
             self.k_rot[...] = rope(key, cosine, sine).astype(BF16)
             self.v_low[...] = self.v_buf[:, at_key].astype(BF16)
             self.dk[...] = jnp.zeros_like(self.dk)
             self.dv[...] = jnp.zeros_like(self.dv)
 
         score_scale = 1.0 / math.sqrt(HEAD_DIM)
-        out_grad = mm(self.branch[...], self.w_buf[slot], 1, 1).astype(BF16)
+        out_grad = mm(self.branch[...], self.w_buf[...], 1, 1).astype(BF16)
+
+        @pl.when(t + 1 < self.count)
+        def _():
+            for c in self.fetch_out(t + 1):
+                c.start()
+
         mask = self.mask[...] > 0.0
         k_rot, v_low = self.k_rot[...], self.v_low[...]
         for h in range(self.cols // HEAD_DIM):
             here = slice(h * HEAD_DIM, (h + 1) * HEAD_DIM)
             raw = self.q_buf[slot, :, here]
-            scale, query = self.normed(raw, 0)
+            scale, query = self.scaled(raw, 0)
             q_rot = rope(query, cosine, sine).astype(BF16)
             d_out = out_grad[:, here]
             scores = mm(q_rot, k_rot, 1, 1) * score_scale
@@ -991,7 +1060,7 @@
         @pl.when(lax.rem(t, self.per_key) == self.per_key - 1)
         def _():
             raw = self.k_buf[:, at_key]
-            scale, _ = self.normed(raw, 1)
+            scale, _ = self.scaled(raw, 1)
             shift = pl.multiple_of(t // self.per_key * HEAD_DIM, HEAD_DIM)
             self.grads[:, pl.ds(self.query_cols + shift, HEAD_DIM)] = self.back(
                 self.dk[...] * score_scale, raw, scale, 1
@@ -999,18 +1068,19 @@
             self.grads[:, pl.ds(self.query_cols + self.key_cols + shift, HEAD_DIM)] = self.dv[...].astype(BF16)
 
 
-def scatter_attention_kernel(nz, plan, term, branch, w_out, raw, tables, gains, seg_col, seg_row,
-                             total, grads, gain_grads, *scratch):
+def scatter_attention_kernel(nz, plan, term, *refs):
+    inputs, (total, *outs), scratch = refs[:10], refs[10:16], refs[16:]
     buffers, rest = scratch[: Scatter.BUFFERS], scratch[Scatter.BUFFERS :]
     send, recv, local = rest[:3]
     z, e = place()
     greet(z, e, nz)
     s = Scatter(nz, [term], [total], *[[b] for b in buffers], send, recv, local)
-    a = AttentionGrad(branch, w_out, raw, tables, gains, seg_col, seg_row, grads, gain_grads, *rest[3:])
+    a = AttentionGrad(*inputs, *outs, *rest[3:])
     s.begin()
     a.prepare()
     steps = s.steps()
-    run_beside(a.count, a.step, steps, plan)
+    run_beside(a.total, a.step, steps, plan)
+    a.end()
     for j in range(nz):
         s.drain(j)
 
@@ -1034,10 +1104,10 @@
         step()
 
 
-def scatter_with_attention(terms, branch, w_out, raw, tables, gains, segments, collective_id):
+def scatter_with_attention(terms, branch, w_out, raw, tables, gains, segments, normed, attended, w_mixed, collective_id):
     nz, width = lax.axis_size("dp"), lax.axis_size("expert")
     devices = nz * width
-    length = branch.shape[0]
+    length, model = branch.shape
     shape = (terms.shape[0] // (4 * devices), terms.shape[1])
     term = terms.reshape((nz, width, 4) + shape)
     heads = 4
@@ -1045,19 +1115,22 @@
     key_cols = (raw.shape[1] - w_out.shape[0]) // 2
     vmem = pl.BlockSpec(memory_space=pltpu.VMEM)
     hbm = pl.BlockSpec(memory_space=pl.ANY)
-    plan = [3, 1, 1, 1, 1, 1, 1, 1]
-    total, grads, gain_grads = pl.pallas_call(
+    plan = [3, 1, 1, 1, 1, 1, 1, 1, 1, 0]
+    total, grads, gain_grads, normed_grad, grad_out, grad_mixed = pl.pallas_call(
         functools.partial(scatter_attention_kernel, nz, plan),
         out_shape=[
             jax.ShapeDtypeStruct((4,) + shape, F32),
             jax.ShapeDtypeStruct(raw.shape, BF16),
             jax.ShapeDtypeStruct((2, HEAD_DIM), F32),
+            jax.ShapeDtypeStruct((length, model), F32),
+            jax.ShapeDtypeStruct(w_out.shape, BF16),
+            jax.ShapeDtypeStruct(w_mixed.shape, BF16),
         ],
-        in_specs=[hbm, vmem, hbm, hbm, vmem, vmem, vmem, vmem],
-        out_specs=[vmem, vmem, vmem],
+        in_specs=[hbm, vmem, hbm, hbm, vmem, vmem, vmem, vmem, vmem, hbm, hbm],
+        out_specs=[vmem, vmem, vmem, vmem, hbm, hbm],
         scratch_shapes=scatter_buffers(nz, width, [(shape, terms.dtype)])
         + [
-            pltpu.VMEM((2, cols, w_out.shape[1]), BF16),
+            pltpu.VMEM((cols, model), BF16),
             pltpu.VMEM((2, length, cols), F32),
             pltpu.VMEM((length, key_cols), F32),
             pltpu.VMEM((length, key_cols), F32),
@@ -1066,35 +1139,49 @@
             pltpu.VMEM((length, HEAD_DIM), BF16),
             pltpu.VMEM((length, HEAD_DIM), F32),
             pltpu.VMEM((length, HEAD_DIM), F32),
-            pltpu.SemaphoreType.DMA((3, 2)),
+            pltpu.VMEM((length, cols), BF16),
+            pltpu.VMEM((model, cols), BF16),
+            pltpu.VMEM((cols, model), BF16),
+            pltpu.VMEM((model, cols), BF16),
+            pltpu.SemaphoreType.DMA((6, 2)),
         ],
         compiler_params=pltpu.CompilerParams(
             collective_id=collective_id, has_side_effects=True, vmem_limit_bytes=VMEM_LIMIT
         ),
         name="scatter_attention",
-    )(term, branch, w_out, raw, tables, gains, segments[:, None], segments[None, :])
-    return total.reshape(4 * shape[0], shape[1]), grads, gain_grads
+    )(term, branch, w_out, raw, tables, gains, segments[:, None], segments[None, :], normed, attended, w_mixed)
+    return total.reshape(4 * shape[0], shape[1]), gain_grads, normed_grad, grad_out, grad_mixed
 
 
 TILE = 512
 
 
 class ExpertWork:
-    def __init__(self, nz, cap, group, all_rows, all_tables, all_grads, weights, outs, bufs, sems):
+    def __init__(self, nz, cap, group, orders, all_rows, all_tables, all_grads, weights, outs, bufs, sems):
         self.nz, self.cap, self.group = nz, cap, group
         self.all_rows, self.all_tables, self.all_grads = all_rows, all_tables, all_grads
         self.weights, self.outs, self.bufs, self.sems = weights, outs, bufs, sems
         self.z, self.e = place()
         self.width = all_rows.shape[1]
-        self.per = self.width // group
+        self.orders = orders
+        self.edge = jnp.logical_or(self.z == 0, self.z == nz - 1)
 
     def weight_copies(self):
         return [pltpu.make_async_copy(w, b, self.sems.at[0, i]) for i, (w, b) in enumerate(zip(self.weights, self.bufs[:3]))]
 
+    def place_of(self, t):
+        zz, half = jnp.int32(0), jnp.int32(0)
+        for p, (ends, middle) in enumerate(zip(*self.orders)):
+            for here, (j, h) in ((self.edge, ends), (jnp.logical_not(self.edge), middle)):
+                here = jnp.logical_and(here, t == p)
+                zz = jnp.where(here, line_order(self.z, self.nz, j), zz)
+                half = jnp.where(here, h, half)
+        near = self.e // self.group
+        return zz, jnp.where(half == 0, near, 1 - near) * self.group
+
     def inputs(self, t, slot):
-        j, part = t // self.per, lax.rem(t, self.per)
-        at = self.block(part)
-        zz = line_place(self.z, self.nz, j)
+        zz, first = self.place_of(t)
+        at = pl.ds(first, self.group)
         x, tab, g = self.bufs[3:6]
         return (
             pltpu.make_async_copy(self.all_rows.at[zz, at], x.at[slot], self.sems.at[1 + slot, 0]),
@@ -1115,8 +1202,8 @@
         return [pltpu.make_async_copy(b, o.at[self.flat(t)], self.sems.at[3, 2 + i]) for i, (b, o) in enumerate(pairs)]
 
     def term_results(self, t, n, cols):
-        at = self.block(lax.rem(t, self.per))
-        zz = line_place(self.z, self.nz, t // self.per)
+        zz, first = self.place_of(t)
+        at = pl.ds(first, self.group)
         pairs = zip(self.bufs[6:8], self.outs[:2])
         return [
             pltpu.make_async_copy(b.at[:, :, cols], o.at[zz, at, :, cols], self.sems.at[4 + i, n])
@@ -1127,12 +1214,8 @@
         for c in self.weight_copies():
             c.start()
 
-    def block(self, part):
-        near = self.e // self.group
-        return pl.ds(jnp.where(part == 0, near, 1 - near) * self.group, self.group)
-
-    def ready(self, j, part):
-        for c in self.inputs(jnp.int32(j * self.per + part), part):
+    def ready(self, p):
+        for c in self.inputs(jnp.int32(p), p % 2):
             c.start()
 
     def step(self, t, hook):
@@ -1204,9 +1287,8 @@
                 rb[s, :, cols] = mm(picks[s], back[part], 0, 0).astype(BF16)
             for c in self.term_results(t, n, cols):
                 c.start()
-        near = self.e // group
-        block = jnp.where(lax.rem(t, self.per) == 0, near, 1 - near)
-        first = line_place(self.z, self.nz, t // self.per) * self.width + block * group
+        zz, first = self.place_of(t)
+        first = zz * self.width + first
         for s in range(group):
             self.outs[2][first + s] = jnp.sum(
                 picks[s].astype(F32) * gg[s * cap : (s + 1) * cap], 0, keepdims=True
@@ -1219,20 +1301,12 @@
                 c.wait()
 
     def end(self):
-        t = jnp.int32(self.nz * self.per - 1)
+        t = jnp.int32(len(self.orders[0]) - 1)
         for c in self.row_results(t) + self.hidden_results(t):
             c.wait()
         for n in range(self.bufs[13].shape[1] // TILE):
             for c in self.term_results(t, n, pl.ds(n * TILE, TILE)):
                 c.wait()
-
-
-def line_place(z, nz, j):
-    near = jnp.minimum(z, nz - 1 - z)
-    step = (j + 1) // 2
-    zigzag = jnp.where(lax.rem(j, 2) == 0, z + step, z - step)
-    tail = jnp.where(z < nz - 1 - z, j, nz - 1 - j)
-    return jnp.where(j <= 2 * near, zigzag, tail)
 
 
 def gather_expert_kernel(nz, cap, group, *refs):
@@ -1243,59 +1317,101 @@
     z, e = place()
     greet(z, e, nz)
     g = Gather(nz, shards, gathered, send, recv, local)
-    w = ExpertWork(nz, cap, group, gathered[0], gathered[1], all_grads, weights, outs, bufs, sems)
+    plain = tuple((j, h) for j in range(nz) for h in range(2))
+    orders = ORDERS.get(nz) or (plain, plain)
+    plans = RELAYS.get(nz) or (relays_first(g, orders[0]),) * 2
+    w = ExpertWork(nz, cap, group, orders, gathered[0], gathered[1], all_grads, weights, outs, bufs, sems)
     w.begin()
-    edge = jnp.logical_or(z == 0, z == nz - 1)
-    plans = RELAYS.get(nz) or (relays_first(g, nz),) * 2
-
-    def run(name):
+    relays = {"L": g.launch_line, "K": g.launch_plane, "M": g.mates, "R": g.relay, "F": g.finish}
+
+    def run(name, order):
         kind, j = name[0], int(name[1:])
-        if kind == "N":
-            g.shared_near(j)
-            if j == 0:
+        if kind == "I":
+            place, half = order[j]
+            (g.shared_far if half else g.shared_near)(place)
+            if place == 0 and half == 0:
                 g.kept()
-            w.ready(j, 0)
-        elif kind == "A":
-            g.shared_far(j)
-            w.ready(j, 1)
+            w.ready(j)
         else:
-            {"L": g.launch, "M": g.mates, "R": g.relay, "F": g.finish}[kind](j)
+            relays[kind](j)
 
     def body(t, _):
         def hook(k):
-            for plan, here in zip(plans, (edge, jnp.logical_not(edge))):
+            for plan, order, here in zip(plans, orders, (w.edge, jnp.logical_not(w.edge))):
                 for piece, part, names in plan:
                     if part == k:
                         @pl.when(jnp.logical_and(t == piece, here))
                         def _():
                             for name in names.split():
-                                run(name)
+                                run(name, order)
 
         w.step(t, hook)
         return 0
 
-    lax.fori_loop(0, nz * w.per, body, 0)
+    lax.fori_loop(0, len(orders[0]), body, 0)
     w.end()
     for j in range(nz):
         g.drain(j, True)
 
 
-def relays_first(g, nz):
-    names = [{"launch": "L", "mates": "M", "relay": "R", "finish": "F"}[f.func.__name__] + str(f.args[0]) for f in g.steps()]
-    head = [(0, 0, n) for n in names]
-    return head + [(2 * j, 0, "N%d" % j) for j in range(nz)] + [(2 * j + 1, 0, "A%d" % j) for j in range(nz)]
-
-
+def relays_first(g, order):
+    head = []
+    for f in g.steps():
+        kind, j = f.func.__name__, f.args[0]
+        names = {"launch": "L%d K%d", "mates": "M%d", "relay": "R%d", "finish": "F%d"}[kind]
+        head.append((0, 0, names.replace("%d", str(j))))
+    return head + [(p, 0, "I%d" % p) for p in range(len(order))]
+
+
+ORDERS = {
+    4: (
+        ((0, 0), (1, 0), (0, 1), (1, 1), (2, 0), (2, 1), (3, 0), (3, 1)),
+        ((0, 0), (1, 0), (0, 1), (2, 0), (1, 1), (3, 0), (2, 1), (3, 1)),
+    )
+}
 RELAYS = {
     4: (
         (
-            (0, 0, "L0 M0 L1"), (0, 0, "R0 N0"), (0, 2, "M1"), (0, 6, "R1"), (1, 0, "N1 F0 A0 L2"), (1, 2, "F1"), (1, 5, "M2 A1"),
-            (2, 6, "R2"), (3, 1, "N2"), (3, 5, "L3"), (4, 0, "F2"), (4, 2, "A2"), (4, 4, "M3"), (5, 2, "R3"), (5, 5, "N3"),
-            (6, 3, "F3"), (6, 6, "A3"),
+            (0, 0, "L0 K0 M0"),
+            (0, 0, "L1 K1 R0"),
+            (0, 0, "I0"),
+            (0, 1, "M1"),
+            (0, 5, "R1"),
+            (1, 0, "I1"),
+            (1, 2, "F0"),
+            (1, 4, "L2 K2 I2"),
+            (2, 1, "F1"),
+            (2, 2, "M2 I3"),
+            (3, 2, "R2"),
+            (3, 4, "I4"),
+            (4, 1, "L3 K3"),
+            (4, 2, "F2"),
+            (4, 5, "I5 M3"),
+            (5, 3, "R3"),
+            (5, 5, "I6"),
+            (6, 3, "F3"),
+            (6, 6, "I7"),
         ),
         (
-            (0, 0, "L0 M0 L1"), (0, 0, "R0 L2 N0"), (0, 2, "M1 M2"), (0, 6, "R1"), (1, 0, "N1 F0 A0 L3"), (1, 6, "M3 R2"), (2, 2, "N2"),
-            (2, 6, "F1"), (3, 0, "A1"), (3, 6, "R3"), (4, 1, "N3"), (4, 6, "F2"), (5, 0, "A2"), (5, 2, "F3"), (5, 5, "A3"),
+            (0, 0, "L0 K0 M0"),
+            (0, 0, "L1 L2 K1"),
+            (0, 0, "R0 K2 I0"),
+            (0, 1, "M1 M2"),
+            (0, 4, "R1"),
+            (0, 6, "I1"),
+            (1, 2, "F0"),
+            (1, 4, "L3 K3 I2"),
+            (2, 2, "M3"),
+            (2, 3, "R2"),
+            (2, 5, "I3"),
+            (3, 2, "F1"),
+            (3, 5, "I4"),
+            (4, 4, "R3"),
+            (4, 6, "I5"),
+            (5, 2, "F2"),
+            (5, 5, "I6"),
+            (6, 1, "F3"),
+            (6, 3, "I7"),
         ),
     )
 }
@@ -1576,14 +1692,12 @@
     residual_grad = out_grad.astype(F32) + norm_grad(normed_mlp_grad, residual, inv_mlp, mlp_gain)
 
     branch_grad = residual_grad.astype(BF16)
-    grad_w_output = jnp.dot(attended.T, branch_grad, preferred_element_type=F32).astype(BF16)
-    mixed_out, mixed_grad, gain_grads = scatter_with_attention(
-        y_terms.reshape(devices * length, width), branch_grad, w_out, mixed, tables, head_gains, segment_ids, 5
+    mixed_out, gain_grads, normed_attn_grad, grad_w_output, grad_w_mixed = scatter_with_attention(
+        y_terms.reshape(devices * length, width), branch_grad, w_out, mixed, tables, head_gains, segment_ids,
+        normed_attn, attended, w_mixed, 5,
     )
     block_out = residual + mixed_out
     grad_query_gain, grad_key_gain = gain_grads[0], gain_grads[1]
-    grad_w_mixed = jnp.dot(normed_attn.T, mixed_grad, preferred_element_type=F32).astype(BF16)
-    normed_attn_grad = jnp.dot(mixed_grad, w_mixed.T, preferred_element_type=F32)
     grad_attn_gain = jnp.sum(normed_attn_grad * plain_in * inv_attn, 0)
     grad_in = residual_grad + norm_grad(normed_attn_grad, plain_in, inv_attn, attn_gain)
 

time: 1030 us -> 1000 us (0.971)
  matrix products: 76.1 us -> 54.6 us
  Pallas kernels: 899 us -> 887 us
    dot_general x3 -> x0, matrix products: 33.7 us -> none  [the longest x1 12.1 us: per_device_gather(): jnp.dot(mixed_grad, w_mixed.T, preferred_element_type=F32)]
    dot_general x1, matrix products: 14.5 us -> 26.9 us  [per_device_gather(): grad_w_down = jnp.dot(act.T, down_in, preferred_element_type=F32)[None]]
where the time goes in v5:
time: 1000 us; the launch traced here: 993 us
  Pallas kernels  887 us (89%)
  matrix products  54.6 us (5%)
  local copies, waits for them, and re-layouts  27.2 us (3%)
  other arithmetic  22.9 us (2%)
    pallas_call x2, Pallas kernels, scatter_sum(): pl.pallas_call(functools.partial(scatter_kernel, nz, count), out_shape=[j...  293 us
    pallas_call x1, Pallas kernels, gather_with_experts(): pl.pallas_call(functools.partial(gather_expert_kernel, nz, cap, group), o...  165 us
    pallas_call x1, Pallas kernels, gather_all(): pl.pallas_call(functools.partial(gather_kernel, nz, count), out_shape=[ja...  155 us
    pallas_call x1, Pallas kernels, gather_with_attention(): pl.pallas_call(functools.partial(gather_attention_kernel, nz, [1, 0, 1, 1...  141 us
    pallas_call x1, Pallas kernels, scatter_with_attention(): pl.pallas_call(functools.partial(scatter_attention_kernel, nz, plan), out...  133 us
    dot_general x1, matrix products, per_device_gather(): grad_w_down = jnp.dot(act.T, down_in, preferred_element_type=F32)[None]  26.9 us

profile of v5, /device:TPU:0, one launch (start us, length us, event | category | flops | bytes accessed | tf_op | source)
XLA Modules:
  0.0 993.4 jit_solution(7614969895812450912)
XLA Ops:
  2.1 2.0 pad_maximum_fusion
  5.6 155.4 %gather_all.1 = (bf16[4,8,4,16,5120]{4,3,2,1,0:T(8,128)(2,1)}, bf16[4,8,4,32,2048]{4,3,2,1,0:T(8,128)(2,1)}, bf16[4,8,4,16,128]{4,3,2,1,0:T(8,128)(2,1)}) custom-call(bf16[4,16,5120]{2,1,0:T(8,128)(2,1)} %bitcast.89, bf16[4,32,2048]{2,1,0:T(8,128)(2,1)} %bitcast.94, bf16[4,16,128]{2,1,0:T(8,128)(2,1)} %concatenate.46.refs_2_), custom_call_target="tpu_custom_call" | custom-call | tf_op jit(solution)/shard_map/gather_all/pallas_call | solution.py:643
  163.0 2.5 slice_convert_fusion
  167.2 140.6 %gather_attention.1 = (bf16[4,8,4,64,2048]{4,3,2,1,0:T(8,128)(2,1)}, f32[256,5120]{1,0:T(8,128)}, bf16[256,2048]{1,0:T(8,128)(2,1)}, bf16[256,4096]{1,0:T(8,128)(2,1)}, f32[256,2048]{1,0:T(8,128)}) custom-call(bf16[4,64,2048]{2,1,0:T(8,128)(2,1)} %bitcast.85, bf16[256,2048]{1,0:T(8,128)(2,1)} %hidden.1, f32[1,2048]{1,0:T(1,128)} %bitcast.103, ...), custom_call_target="tpu_custom_call" | custom-call | tf_op jit(solution)/shard_map/gather_attention/pallas_call | solution.py:1571
  307.9 2.4 multiply_reduce_fusion.2
  314.2 165.3 %gather_experts.1 = (bf16[4,8,4,64,2048]{4,3,2,1,0:T(8,128)(2,1)}, bf16[4,8,4,64,128]{4,3,2,1,0:T(8,128)(2,1)}, bf16[4,8,256,2048]{3,2,1,0:T(8,128)(2,1)}, bf16[...) custom-call(bf16[4,64,2048]{2,1,0:T(8,128)(2,1)} %bitcast.79, ...), custom_call_target="tpu_custom_call" | custom-call | tf_op jit(solution)/shard_map/gather_experts/pallas_call | solution.py:1432
  479.5 26.9 %convolution_bitcast_fusion = f32[1,768,2048]{2,1,0:T(8,128)} fusion(bf16[2560,768]{1,0:T(8,128)(2,1)} %get-tuple-element.64, bf16[2560,2048]{1,0:T(8,128)(2,1)} %get-tuple-element.65), kind=kOutput, calls=%fused_computation.5 | convolution fusion | flops 8053063680 | bytes 20709376 | tf_op jit(solution)/shard_map/dot_general | solution.py:1682
  506.4 11.0 %convolution_bitcast_fusion.1 = f32[1,2048,768]{2,1,0:T(8,128)} fusion(bf16[2560,2048]{1,0:T(8,128)(2,1)S(1)} %copy-done.21, bf16[2560,768]{1,0:T(8,128)(2,1)S(1)} %copy-done.23), kind=kOutput, calls=%fused_computation.6 | convolution fusion | flops 8053063680 | bytes 20709376 | tf_op jit(solution)/shard_map/dot_general | solution.py:1684
  517.4 11.0 %convolution_bitcast_fusion.2 = f32[1,2048,768]{2,1,0:T(8,128)} fusion(bf16[2560,2048]{1,0:T(8,128)(2,1)S(1)} %copy-done.21, bf16[2560,768]{1,0:T(8,128)(2,1)S(1)} %copy-done.22), kind=kOutput, calls=%fused_computation.7 | convolution fusion | flops 8053063680 | bytes 20709376 | tf_op jit(solution)/shard_map/dot_general | solution.py:1683
  528.4 1.2 broadcast_multiply_fusion.refs_1_
  529.5 141.1 %scatter_sum.2 = (f32[4,64,2048]{2,1,0:T(8,128)}, f32[4,8,256]{2,1,0:T(8,128)}) custom-call(bf16[4,8,4,64,2048]{4,3,2,1,0:T(8,128)(2,1)} %bitcast.76, f32[4,8,4,8,256]{4,3,2,1,0:T(8,128)} %broadcast_multiply_fusion.refs_1_), custom_call_target="tpu_custom_call" | custom-call | tf_op jit(solution)/shard_map/scatter_sum/pallas_call | solution.py:889
  672.4 2.7 fusion.26
  675.0 2.5 multiply_reduce_fusion
  677.6 2.3 fusion.21
  679.9 133.0 %scatter_attention.1 = (f32[4,64,2048]{2,1,0:T(8,128)}, bf16[256,5120]{1,0:T(8,128)(2,1)}, f32[2,128]{1,0:T(2,128)}, f32[256,2048]{1,0:T(8,128)}, bf16[4096,2048...) custom-call(bf16[4,8,4,64,2048]{4,3,2,1,0:T(8,128)(2,1)} %bitcast.75, bf16[256,2048]{1,0:T(8,128)(2,1)} %get-tuple-element.74.refs_0_, ...), custom_call_target="tpu_custom_call" | custom-call | tf_op jit(solution)/shard_map/scatter_attention/pallas_call | solution.py:1119
  812.9 2.4 fusion.6
  817.5 2.0 concatenate.63
  819.5 1.8 concatenate.61
  822.5 4.5 concatenate.55.refs_2_
  827.0 152.1 %scatter_sum.3 = (f32[4,16,5120]{2,1,0:T(8,128)}, f32[4,32,2048]{2,1,0:T(8,128)}, f32[4,16,128]{2,1,0:T(8,128)}) custom-call(bf16[4,8,4,16,5120]{4,3,2,1,0:T(8,128)(2,1)} %bitcast.77, bf16[4,8,4,32,2048]{4,3,2,1,0:T(8,128)(2,1)} %bitcast.78, f32[4,8,4,16,128]{4,3,2,1,0:T(8,128)} %concatenate.55.refs_2_), custom_call_target="tpu_custom_call" | custom-call | tf_op jit(solution)/shard_map/scatter_sum/pallas_call | solution.py:889
  979.1 2.4 slice.71
  981.5 1.7 fusion.22
  986.4 4.3 fusion.3
  990.6 1.6 bitcast_add_fusion
  (106 shorter events, 19.5 us)
Async XLA Ops:
  0.6 3.5 copy-start.24
  0.7 3.6 copy-start.25
  0.7 3.8 copy-start.16
  0.7 3.9 copy-start.19
  0.7 4.0 copy-start.20
  163.0 3.5 copy-start.15
  307.9 2.5 copy-start.8
  310.3 1.3 copy-start
  310.7 1.9 copy-start.5
  479.5 26.9 %copy-start.21 = (bf16[2560,2048]{1,0:T(8,128)(2,1)S(1)}, bf16[2560,2048]{1,0:T(8,128)(2,1)}, u32[]{:S(2)}) copy-start(bf16[2560,2048]{1,0:T(8,128)(2,1)} %get-tuple-element.61) | copy-start | bytes 31457284
  479.5 26.9 %copy-start.23 = (bf16[2560,768]{1,0:T(8,128)(2,1)S(1)}, bf16[2560,768]{1,0:T(8,128)(2,1)}, u32[]{:S(2)}) copy-start(bf16[2560,768]{1,0:T(8,128)(2,1)} %get-tuple-element.63) | copy-start | bytes 11796484
  506.4 11.0 %copy-start.22 = (bf16[2560,768]{1,0:T(8,128)(2,1)S(1)}, bf16[2560,768]{1,0:T(8,128)(2,1)}, u32[]{:S(2)}) copy-start(bf16[2560,768]{1,0:T(8,128)(2,1)} %get-tuple-element.62) | copy-start | bytes 11796484
  517.4 11.0 %copy-start.14 = (f32[32,1,256]{2,1,0:T(1,128)S(1)}, f32[32,1,256]{2,1,0:T(1,128)}, u32[]{:S(2)}) copy-start(f32[32,1,256]{2,1,0:T(1,128)} %get-tuple-element.47) | copy-start | bytes 98308
  529.5 145.5 %copy-start.6 = (bf16[4,8,4,16,128]{4,3,2,1,0:T(8,128)(2,1)S(1)}, bf16[4,8,4,16,128]{4,3,2,1,0:T(8,128)(2,1)}, u32[]{:S(2)}) copy-start(bf16[4,8,4,16,128]{4,3,2,1,0:T(8,128)(2,1)} %get-tuple-element.40) | copy-start | bytes 1572868
  670.6 4.4 copy-start.1
  675.0 2.5 copy-start.9
  679.9 133.0 %copy-start.13 = (f32[2048,1]{0,1:T(1,128)S(1)}, f32[2048,1]{0,1:T(1,128)}, u32[]{:S(2)}) copy-start(f32[2048,1]{0,1:T(1,128)} %copy.101) | copy-start | bytes 24580
  812.9 3.3 copy-start.18
  816.4 6.1 copy-start.7
  979.1 4.1 copy-start.12
  979.1 7.3 copy-start.3
  986.4 4.3 copy-start.2
  986.4 4.3 copy-start.10
  990.6 1.6 copy-start.11
  (2 other events, 2.3 us)

commit v6 on v5

--- a/solution.py
+++ b/solution.py
@@ -657,6 +657,9 @@
 def accumulate(dst, src):
     rows = dst.shape[0]
     block = 32 if rows % 32 == 0 else rows
+    if rows == block:
+        dst[...] = dst[...] + src[...]
+        return
 
     def body(r, _):
         at = pl.ds(pl.multiple_of(r * block, block), block)
@@ -1597,6 +1600,137 @@
     return gathered, raw, normed, attended, branch
 
 
+class ExpertGrads:
+    TILE = 256
+
+    def __init__(self, rows, down, act, gate_pre, up_pre, grad_gate, grad_up, grad_down,
+                 tile, gate_buf, up_buf, gate_stage, up_stage, sems):
+        self.rows, self.down, self.act, self.gate_pre, self.up_pre = rows, down, act, gate_pre, up_pre
+        self.grad_gate, self.grad_up, self.grad_down = grad_gate, grad_up, grad_down
+        self.tile, self.gate_buf, self.up_buf = tile, gate_buf, up_buf
+        self.gate_stage, self.up_stage, self.sems = gate_stage, up_stage, sems
+        self.half = rows.shape[1] // self.TILE
+        self.count = 2 * self.half
+
+    def at(self, t):
+        return pl.ds(pl.multiple_of(lax.rem(t, self.half) * self.TILE, self.TILE), self.TILE)
+
+    def each(self, t, act):
+        slot = lax.rem(t, 2)
+        for source, here in ((self.rows, t < self.half), (self.down, t >= self.half)):
+            @pl.when(here)
+            def _():
+                act(pltpu.make_async_copy(source.at[:, self.at(t)], self.tile.at[slot], self.sems.at[0, slot]))
+
+    def hidden(self, source, buf, k):
+        return pltpu.make_async_copy(source, buf, self.sems.at[1, k])
+
+    def put(self, t, act):
+        for out, here in ((self.grad_gate, t < self.half), (self.grad_down, t >= self.half)):
+            @pl.when(here)
+            def _():
+                act(pltpu.make_async_copy(self.gate_stage, out.at[self.at(t), :], self.sems.at[2, 0]))
+
+    def put_up(self, t):
+        return pltpu.make_async_copy(self.up_stage, self.grad_up.at[self.at(t), :], self.sems.at[2, 1])
+
+    def prepare(self):
+        self.hidden(self.gate_pre, self.gate_buf, 0).start()
+        self.hidden(self.up_pre, self.up_buf, 1).start()
+        self.each(jnp.int32(0), lambda c: c.start())
+
+    def step(self, t):
+        slot = lax.rem(t, 2)
+
+        @pl.when(t + 1 < self.count)
+        def _():
+            self.each(t + 1, lambda c: c.start())
+
+        @pl.when(t == 0)
+        def _():
+            self.hidden(self.gate_pre, self.gate_buf, 0).wait()
+            self.hidden(self.up_pre, self.up_buf, 1).wait()
+
+        @pl.when(t == self.half)
+        def _():
+            copy = self.hidden(self.act, self.gate_buf, 0)
+            copy.start()
+            copy.wait()
+
+        self.each(t, lambda c: c.wait())
+
+        @pl.when(t > 0)
+        def _():
+            self.put(t - 1, lambda c: c.wait())
+
+        self.gate_stage[...] = mm(self.tile[slot], self.gate_buf[...], 0, 0)
+        self.put(t, lambda c: c.start())
+
+        @pl.when(t < self.half)
+        def _():
+            @pl.when(t > 0)
+            def _():
+                self.put_up(t - 1).wait()
+
+            self.up_stage[...] = mm(self.tile[slot], self.up_buf[...], 0, 0)
+            self.put_up(t).start()
+
+    def end(self):
+        self.put(jnp.int32(self.count - 1), lambda c: c.wait())
+        self.put_up(jnp.int32(self.half - 1)).wait()
+
+
+def scatter_grads_kernel(nz, plan, count, *refs):
+    terms, inputs = refs[:count], refs[count : count + 5]
+    totals, outs = refs[count + 5 : 2 * count + 5], refs[2 * count + 5 : 2 * count + 8]
+    scratch = refs[2 * count + 8 :]
+    groups = [scratch[k * count : (k + 1) * count] for k in range(Scatter.BUFFERS)]
+    rest = scratch[Scatter.BUFFERS * count :]
+    z, e = place()
+    greet(z, e, nz)
+    s = Scatter(nz, terms, totals, *groups, *rest[:3])
+    w = ExpertGrads(*inputs, *outs, *rest[3:])
+    s.begin()
+    w.prepare()
+    run_beside(w.count, w.step, s.steps(), plan)
+    w.end()
+    for j in range(nz):
+        s.drain(j)
+
+
+def scatter_with_grads(arrays, rows, down, act, gate_pre, up_pre, collective_id):
+    nz, width = lax.axis_size("dp"), lax.axis_size("expert")
+    count, devices = len(arrays), nz * width
+    terms = [a.reshape(nz, width, 4, a.shape[0] // (4 * devices), a.shape[1]) for a in arrays]
+    shapes = [t.shape[3:] for t in terms]
+    picked, model = rows.shape
+    ff = act.shape[1]
+    tile = ExpertGrads.TILE
+    vmem = pl.BlockSpec(memory_space=pltpu.VMEM)
+    hbm = pl.BlockSpec(memory_space=pl.ANY)
+    plan = [3, 1, 0, 0, 0, 0, 3, 0, 0, 0, 0, 2] + [0] * 16
+    outs = pl.pallas_call(
+        functools.partial(scatter_grads_kernel, nz, plan, count),
+        out_shape=[jax.ShapeDtypeStruct((4,) + s, F32) for s in shapes] + [jax.ShapeDtypeStruct((model, ff), F32)] * 3,
+        in_specs=[hbm] * (count + 5),
+        out_specs=[vmem] * count + [hbm] * 3,
+        scratch_shapes=scatter_buffers(nz, width, [(s, a.dtype) for s, a in zip(shapes, arrays)])
+        + [
+            pltpu.VMEM((2, picked, tile), BF16),
+            pltpu.VMEM((picked, ff), BF16),
+            pltpu.VMEM((picked, ff), BF16),
+            pltpu.VMEM((tile, ff), F32),
+            pltpu.VMEM((tile, ff), F32),
+            pltpu.SemaphoreType.DMA((3, 2)),
+        ],
+        compiler_params=pltpu.CompilerParams(
+            collective_id=collective_id, has_side_effects=True, vmem_limit_bytes=VMEM_LIMIT
+        ),
+        name="scatter_grads",
+    )(*terms, rows, down, act, gate_pre, up_pre)
+    return [o.reshape(4 * s[0], s[1]) for o, s in zip(outs, shapes)] + list(outs[count:])
+
+
 def pack_columns(columns, rows, lanes, dtype):
     parts = [c.astype(dtype) for c in columns]
     used = sum(c.shape[1] for c in parts)
@@ -1678,10 +1812,10 @@
     )
     is_me = (jnp.arange(experts_total) == me).astype(F32)
     gate_terms = (gate_terms * is_me[None, :, None]).reshape(devices * experts_total, length)
-    row_grad_sum, gate_grad = scatter_sum([r_terms.reshape(devices * length, width), gate_terms], 4)
-    grad_w_down = jnp.dot(act.T, down_in, preferred_element_type=F32)[None]
-    grad_w_gate = jnp.dot(rows_in.T, gate_pre_grad, preferred_element_type=F32)[None]
-    grad_w_up = jnp.dot(rows_in.T, up_pre_grad, preferred_element_type=F32)[None]
+    row_grad_sum, gate_grad, grad_w_gate, grad_w_up, grad_w_down = scatter_with_grads(
+        [r_terms.reshape(devices * length, width), gate_terms], rows_in, down_in, act, gate_pre_grad, up_pre_grad, 4
+    )
+    grad_w_gate, grad_w_up, grad_w_down = grad_w_gate[None], grad_w_up[None], grad_w_down.T[None]
 
     gate_grad = gate_grad.T
     sel_grad = gate * (gate_grad - jnp.sum(gate * gate_grad, -1, keepdims=True))

time: 1000 us -> 971 us (0.971)
  matrix products: 54.6 us -> 5.78 us
  local copies, waits for them, and re-layouts: 27.2 us -> 43.8 us
    pallas_call x0 -> x1, Pallas kernels: none -> 142 us  [scatter_with_grads(): pl.pallas_call(functools.partial(scatter_grads_kernel, nz, plan, count),...]
    pallas_call x2 -> x1, Pallas kernels: 293 us -> 153 us  [scatter_sum(): pl.pallas_call(functools.partial(scatter_kernel, nz, count), out_shape=[j...]
    dot_general x3 -> x0, matrix products: 48.8 us -> none  [the longest x1 26.9 us: per_device_gather(): grad_w_down = jnp.dot(act.T, down_in, preferred_element_type=F32)[None]]
    unnamed x62 -> x61, local copies, waits for them, and re-layouts: 7.1 us -> 23.8 us
where the time goes in v6:
time: 971 us; the launch traced here: 963 us
  Pallas kernels  889 us (92%)
  local copies, waits for them, and re-layouts  43.8 us (5%)
  other arithmetic  22.8 us (2%)
    pallas_call x1, Pallas kernels, gather_with_experts(): pl.pallas_call(functools.partial(gather_expert_kernel, nz, cap, group), o...  165 us
    pallas_call x1, Pallas kernels, gather_all(): pl.pallas_call(functools.partial(gather_kernel, nz, count), out_shape=[ja...  155 us
    pallas_call x1, Pallas kernels, scatter_sum(): pl.pallas_call(functools.partial(scatter_kernel, nz, count), out_shape=[j...  153 us
    pallas_call x1, Pallas kernels, scatter_with_grads(): pl.pallas_call(functools.partial(scatter_grads_kernel, nz, plan, count),...  142 us
    pallas_call x1, Pallas kernels, gather_with_attention(): pl.pallas_call(functools.partial(gather_attention_kernel, nz, [1, 0, 1, 1...  141 us
    pallas_call x1, Pallas kernels, scatter_with_attention(): pl.pallas_call(functools.partial(scatter_attention_kernel, nz, plan), out...  133 us
    unnamed x61, local copies, waits for them, and re-layouts  23.8 us

profile of v6, /device:TPU:0, one launch (start us, length us, event | category | flops | bytes accessed | tf_op | source)
XLA Modules:
  0.0 963.4 jit_solution(10069117764641738349)
XLA Ops:
  2.1 2.0 pad_maximum_fusion
  5.6 155.4 %gather_all.1 = (bf16[4,8,4,16,5120]{4,3,2,1,0:T(8,128)(2,1)}, bf16[4,8,4,32,2048]{4,3,2,1,0:T(8,128)(2,1)}, bf16[4,8,4,16,128]{4,3,2,1,0:T(8,128)(2,1)}) custom-call(bf16[4,16,5120]{2,1,0:T(8,128)(2,1)} %bitcast.87, bf16[4,32,2048]{2,1,0:T(8,128)(2,1)} %bitcast.92, bf16[4,16,128]{2,1,0:T(8,128)(2,1)} %concatenate.46.refs_2_), custom_call_target="tpu_custom_call" | custom-call | tf_op jit(solution)/shard_map/gather_all/pallas_call | solution.py:643
  162.9 2.5 slice_convert_fusion
  167.2 140.6 %gather_attention.1 = (bf16[4,8,4,64,2048]{4,3,2,1,0:T(8,128)(2,1)}, f32[256,5120]{1,0:T(8,128)}, bf16[256,2048]{1,0:T(8,128)(2,1)}, bf16[256,4096]{1,0:T(8,128)(2,1)}, f32[256,2048]{1,0:T(8,128)}) custom-call(bf16[4,64,2048]{2,1,0:T(8,128)(2,1)} %bitcast.83, bf16[256,2048]{1,0:T(8,128)(2,1)} %hidden.1, f32[1,2048]{1,0:T(1,128)} %bitcast.101, ...), custom_call_target="tpu_custom_call" | custom-call | tf_op jit(solution)/shard_map/gather_attention/pallas_call | solution.py:1574
  307.9 2.4 multiply_reduce_fusion.2
  314.2 165.3 %gather_experts.1 = (bf16[4,8,4,64,2048]{4,3,2,1,0:T(8,128)(2,1)}, bf16[4,8,4,64,128]{4,3,2,1,0:T(8,128)(2,1)}, bf16[4,8,256,2048]{3,2,1,0:T(8,128)(2,1)}, bf16[...) custom-call(bf16[4,64,2048]{2,1,0:T(8,128)(2,1)} %bitcast.72, ...), custom_call_target="tpu_custom_call" | custom-call | tf_op jit(solution)/shard_map/gather_experts/pallas_call | solution.py:1435
  480.3 1.2 broadcast_multiply_fusion.refs_1_
  481.4 141.8 %scatter_grads.1 = (f32[4,64,2048]{2,1,0:T(8,128)}, f32[4,8,256]{2,1,0:T(8,128)}, f32[2048,768]{1,0:T(8,128)}, f32[2048,768]{1,0:T(8,128)}, f32[2048,768]{1,0:T(8,128)}) custom-call(bf16[4,8,4,64,2048]{4,3,2,1,0:T(8,128)(2,1)} %bitcast.69, f32[4,8,4,8,256]{4,3,2,1,0:T(8,128)} %broadcast_multiply_fusion.refs_1_, ...), custom_call_target="tpu_custom_call" | custom-call | tf_op jit(solution)/shard_map/scatter_grads/pallas_call | solution.py:1712
  624.9 2.7 fusion.26
  627.6 2.5 multiply_reduce_fusion
  630.1 2.3 fusion.21
  632.5 133.4 %scatter_attention.1 = (f32[4,64,2048]{2,1,0:T(8,128)}, bf16[256,5120]{1,0:T(8,128)(2,1)}, f32[2,128]{1,0:T(2,128)}, f32[256,2048]{1,0:T(8,128)}, bf16[4096,2048...) custom-call(bf16[4,8,4,64,2048]{4,3,2,1,0:T(8,128)(2,1)} %bitcast.68, bf16[256,2048]{1,0:T(8,128)(2,1)} %get-tuple-element.122.refs_0_, ...), custom_call_target="tpu_custom_call" | custom-call | tf_op jit(solution)/shard_map/scatter_attention/pallas_call | solution.py:1122
  765.9 2.4 fusion.6
  770.5 2.0 concatenate.63
  772.5 1.8 concatenate.61
  775.4 4.5 concatenate.55.refs_2_
  779.9 152.9 %scatter_sum.1 = (f32[4,16,5120]{2,1,0:T(8,128)}, f32[4,32,2048]{2,1,0:T(8,128)}, f32[4,16,128]{2,1,0:T(8,128)}) custom-call(bf16[4,8,4,16,5120]{4,3,2,1,0:T(8,128)(2,1)} %bitcast.70, bf16[4,8,4,32,2048]{4,3,2,1,0:T(8,128)(2,1)} %bitcast.71, f32[4,8,4,16,128]{4,3,2,1,0:T(8,128)} %concatenate.55.refs_2_), custom_call_target="tpu_custom_call" | custom-call | tf_op jit(solution)/shard_map/scatter_sum/pallas_call | solution.py:892
  932.9 2.4 slice.71
  935.2 1.7 fusion.22
  940.2 4.3 fusion.3
  944.4 1.6 bitcast_add_fusion
  946.0 6.6 copy.92
  953.7 6.6 copy.112
  960.2 2.7 copy.113
  (103 shorter events, 20.2 us)
Async XLA Ops:
  0.6 3.5 copy-start.20
  0.7 3.6 copy-start.21
  0.7 3.8 copy-start.15
  0.7 3.9 copy-start.18
  0.7 4.0 copy-start.19
  162.9 3.5 copy-start.14
  307.8 2.5 copy-start.8
  310.3 1.3 copy-start
  310.3 1.3 copy-start.16
  310.7 1.9 copy-start.5
  311.6 1.0 copy-start.4
  481.4 146.2 %copy-start.6 = (bf16[4,8,4,16,128]{4,3,2,1,0:T(8,128)(2,1)S(1)}, bf16[4,8,4,16,128]{4,3,2,1,0:T(8,128)(2,1)}, u32[]{:S(2)}) copy-start(bf16[4,8,4,16,128]{4,3,2,1,0:T(8,128)(2,1)} %get-tuple-element.43) | copy-start | bytes 1572868
  623.2 4.4 copy-start.1
  627.6 2.5 copy-start.9
  632.5 133.4 %copy-start.13 = (f32[2048,1]{0,1:T(1,128)S(1)}, f32[2048,1]{0,1:T(1,128)}, u32[]{:S(2)}) copy-start(f32[2048,1]{0,1:T(1,128)} %copy.104) | copy-start | bytes 24580
  765.9 3.3 copy-start.17
  769.3 6.1 copy-start.7
  932.9 4.1 copy-start.12
  932.9 7.3 copy-start.3
  940.1 4.3 copy-start.2
  940.1 4.3 copy-start.10
  946.0 6.7 copy-start.11
  952.7 7.5 slice-start
  953.7 6.6 slice-start.1

commit v7 on v6

--- a/solution.py
+++ b/solution.py
@@ -768,6 +768,7 @@
             self.x2(i, zz).wait_recv()
             self.add(i, zz, 2, 0, 2, self.from_x2[i].at[zz])
             self.y3(i, zz).start()
+        for i in range(self.count):
             for which in (1, 2):
                 self.flow(i, j, which)
 
@@ -819,6 +820,7 @@
             self.add(i, zz, 3, 0, 3, self.from_x3[i].at[zz])
             self.y3(i, zz).wait_recv()
             self.add(i, zz, 3, 1, 3, self.from_y3[i].at[zz])
+        for i in range(self.count):
             self.flow(i, j, 0)
 
     def result(self):
@@ -1462,40 +1464,56 @@
 
 
 class Attention:
-    def __init__(self, hidden, gain, w_mixed, w_out, tables, gains, seg_col, seg_row, raw, normed, attended, branch,
-                 w_buf, o_buf, kv_buf, mask, k_rot, v_low, sems):
-        self.hidden, self.gain, self.w_mixed, self.w_out = hidden, gain, w_mixed, w_out
+    def __init__(self, columns, hidden, w_mixed, w_out, small, head_map, tables, seg_col, seg_row, raw, normed, attended, branch,
+                 w_buf, o_buf, kv_buf, small_buf, gains, mask, k_rot, v_low, sems):
+        self.columns, self.hidden, self.w_mixed, self.w_out = columns, hidden, w_mixed, w_out
+        self.small, self.head_map, self.small_buf = small, head_map, small_buf
         self.tables, self.gains, self.seg_col, self.seg_row = tables, gains, seg_col, seg_row
         self.raw, self.normed, self.attended, self.branch = raw, normed, attended, branch
         self.w_buf, self.o_buf, self.kv_buf, self.mask = w_buf, o_buf, kv_buf, mask
         self.k_rot, self.v_low, self.sems = k_rot, v_low, sems
-        self.cols = o_buf.shape[1]
-        self.query_cols = w_out.shape[0]
-        self.key_cols = kv_buf.shape[1] // 2
+        self.cols = w_buf.shape[-1]
+        self.query_cols = attended.shape[1]
+        self.key_cols = kv_buf.shape[-1] // 2
         self.count = self.query_cols // self.cols
         self.per_key = self.count // (self.key_cols // HEAD_DIM)
 
     def fetch(self, t, slot):
         at = pl.ds(pl.multiple_of(t * self.cols, self.cols), self.cols)
+        owners = self.o_buf.shape[1]
+        blocks = self.w_out.shape[1] // owners
         return (
-            pltpu.make_async_copy(self.w_mixed.at[:, at], self.w_buf.at[slot], self.sems.at[0, slot]),
-            pltpu.make_async_copy(self.w_out.at[at, :], self.o_buf.at[slot], self.sems.at[1, slot]),
+            pltpu.make_async_copy(self.w_mixed.at[:, :, :, :, at], self.w_buf.at[slot], self.sems.at[0, slot]),
+            pltpu.make_async_copy(
+                self.w_out.at[t // blocks, pl.ds(lax.rem(t, blocks) * owners, owners)], self.o_buf.at[slot], self.sems.at[1, slot]
+            ),
         )
 
     def prepare(self):
         kv = pltpu.make_async_copy(
-            self.w_mixed.at[:, pl.ds(self.query_cols, 2 * self.key_cols)], self.kv_buf, self.sems.at[2, 0]
+            self.w_mixed.at[:, :, :, :, pl.ds(self.query_cols, 2 * self.key_cols)], self.kv_buf, self.sems.at[2, 0]
         )
+        small = pltpu.make_async_copy(self.small, self.small_buf, self.sems.at[2, 1])
+        small.start()
         kv.start()
         for c in self.fetch(0, 0):
             c.start()
         values = self.hidden[...].astype(F32)
         scale = lax.rsqrt(jnp.mean(values * values, 1, keepdims=True) + EPS)
-        self.normed[...] = (values * scale * self.gain[...]).astype(BF16)
+        small.wait()
+        model, lanes = values.shape[1], self.small_buf.shape[-1]
+        lane = lax.broadcasted_iota(jnp.int32, (8, lanes), 1)
+        row = lax.broadcasted_iota(jnp.int32, (8, lanes), 0)
+        select = jnp.zeros((8, lanes), F32)
+        for k, column in enumerate(self.columns):
+            select = jnp.where(jnp.logical_and(row == k, lane == column), 1.0, select)
+        info = mm(select.astype(BF16), self.small_buf[...].reshape(model, lanes), 1, 1)
+        self.normed[...] = (values * scale * info[0:1]).astype(BF16)
+        self.gains[...] = mm(info.astype(BF16), self.head_map[...])
         self.branch[...] = jnp.zeros_like(self.branch)
         self.mask[...] = allowed_mask(self.seg_col, self.seg_row)
         kv.wait()
-        self.raw[:, self.query_cols :] = mm(self.normed[...], self.kv_buf[...])
+        self.raw[:, self.query_cols :] = mm(self.normed[...], self.kv_buf[...].reshape(model, 2 * self.key_cols))
 
     def step(self, t):
         slot = lax.rem(t, 2)
@@ -1512,18 +1530,18 @@
         @pl.when(lax.rem(t, self.per_key) == 0)
         def _():
             shift = pl.multiple_of(t // self.per_key * HEAD_DIM, HEAD_DIM)
-            key = head_norm(self.raw[:, pl.ds(self.query_cols + shift, HEAD_DIM)], self.gains[1:2, :])
+            key = head_norm(self.raw[:, pl.ds(self.query_cols + shift, HEAD_DIM)], self.gains[2:3, :])
             self.k_rot[...] = rope(key, cosine, sine).astype(BF16)
             self.v_low[...] = self.raw[:, pl.ds(self.query_cols + self.key_cols + shift, HEAD_DIM)].astype(BF16)
 
         at = pl.ds(pl.multiple_of(t * self.cols, self.cols), self.cols)
-        query_raw = mm(self.normed[...], self.w_buf[slot])
+        query_raw = mm(self.normed[...], self.w_buf[slot].reshape(self.normed.shape[1], self.cols))
         self.raw[:, at] = query_raw
         mask = self.mask[...] > 0.0
         k_rot, v_low = self.k_rot[...], self.v_low[...]
         outs = []
         for h in range(self.cols // HEAD_DIM):
-            query = head_norm(query_raw[:, h * HEAD_DIM : (h + 1) * HEAD_DIM], self.gains[0:1, :])
+            query = head_norm(query_raw[:, h * HEAD_DIM : (h + 1) * HEAD_DIM], self.gains[1:2, :])
             q_rot = rope(query, cosine, sine).astype(BF16)
             scores = mm(q_rot, k_rot, 1, 1) * (1.0 / math.sqrt(HEAD_DIM))
             raised = jnp.where(mask, jnp.exp(scores), 0.0)
@@ -1531,7 +1549,7 @@
             outs.append(mm(probs, v_low).astype(BF16))
         out = jnp.concatenate(outs, 1)
         self.attended[:, at] = out
-        self.branch[...] += mm(out, self.o_buf[slot])
+        self.branch[...] += mm(out, self.o_buf[slot].reshape(self.cols, self.normed.shape[1]))
 
 
 def head_norm(raw, gain):
@@ -1546,47 +1564,66 @@
     return jnp.where(jnp.logical_and(same, col <= row), 1.0, 0.0)
 
 
-def gather_attention_kernel(nz, plan, shard, hidden, gain, w_mixed, w_out, tables, gains, seg_col, seg_row,
-                            gathered, raw, normed, attended, branch, *scratch):
+def gather_attention_kernel(nz, plan, columns, *refs):
+    shards, inputs = refs[:4], refs[4:9]
+    gathered, outs = refs[9:13], refs[13:17]
+    scratch = refs[17:]
     z, e = place()
     greet(z, e, nz)
-    g = Gather(nz, [shard], [gathered], *scratch[:3])
-    a = Attention(hidden, gain, w_mixed, w_out, tables, gains, seg_col, seg_row, raw, normed, attended, branch, *scratch[3:])
-    steps = g.steps()
+    w = Gather(nz, shards[:3], gathered[:3], *scratch[:3])
+    g = Gather(nz, shards[3:], gathered[3:], *scratch[3:6])
+    hidden, head_map, tables, seg_col, seg_row = inputs
+    a = Attention(columns, hidden, *gathered[:3], head_map, tables, seg_col, seg_row, *outs, *scratch[6:])
+    first, steps = w.steps(), g.steps()
+    for step in first[:-2]:
+        step()
     steps[0]()
+    first[-2]()
+    steps[1]()
+    first[-1]()
+    for j in range(nz):
+        w.shared_near(j)
+        w.shared_far(j)
+    w.kept()
     a.prepare()
-    run_beside(a.count, a.step, steps[1:], plan)
+    run_beside(a.count, a.step, steps[2:], plan)
     for j in range(nz):
         g.shared_near(j)
         g.shared_far(j)
     for j in range(nz):
+        w.drain(j, True)
         g.drain(j)
 
 
-def gather_with_attention(rows, hidden, gain, w_mixed, w_out, tables, gains, segments, collective_id):
+def gather_with_attention(w_mixed, w_out, small, rows, columns, hidden, head_map, tables, segments, collective_id):
     nz, width = lax.axis_size("dp"), lax.axis_size("expert")
     length, model = hidden.shape
-    shard = rows.reshape(4, rows.shape[0] // 4, rows.shape[1])
+    shards = [a.reshape((4, a.shape[0] // 4) + a.shape[1:]) for a in (w_mixed, w_out, small, rows)]
     cols = 4 * HEAD_DIM
-    mixed, query_cols = w_mixed.shape[1], w_out.shape[0]
+    mixed, query_cols = w_mixed.shape[1], w_out.shape[0] * nz * width
+    owners = cols // w_out.shape[0]
     vmem = pl.BlockSpec(memory_space=pltpu.VMEM)
     hbm = pl.BlockSpec(memory_space=pl.ANY)
-    gathered, raw, normed, attended, branch = pl.pallas_call(
-        functools.partial(gather_attention_kernel, nz, [1, 0, 1, 1, 0, 1, 2, 2]),
-        out_shape=[
-            jax.ShapeDtypeStruct((nz, width) + shard.shape, shard.dtype),
+    lead = (nz, width) + shards[0].shape[:2]
+    outs = pl.pallas_call(
+        functools.partial(gather_attention_kernel, nz, [0, 0, 2, 1, 1, 1, 2, 2], columns),
+        out_shape=[jax.ShapeDtypeStruct((nz, width) + s.shape, s.dtype) for s in shards]
+        + [
             jax.ShapeDtypeStruct((length, mixed), F32),
             jax.ShapeDtypeStruct((length, model), BF16),
             jax.ShapeDtypeStruct((length, query_cols), BF16),
             jax.ShapeDtypeStruct((length, model), F32),
         ],
-        in_specs=[vmem, vmem, vmem, hbm, hbm, vmem, vmem, vmem, vmem],
-        out_specs=[hbm, vmem, vmem, vmem, vmem],
-        scratch_shapes=gather_scratch(nz, 1)
+        in_specs=[vmem] * 9,
+        out_specs=[hbm] * 4 + [vmem] * 4,
+        scratch_shapes=gather_scratch(nz, 3)
+        + gather_scratch(nz, 1)
         + [
-            pltpu.VMEM((2, model, cols), BF16),
-            pltpu.VMEM((2, cols, model), BF16),
-            pltpu.VMEM((model, mixed - query_cols), BF16),
+            pltpu.VMEM((2,) + lead + (cols,), BF16),
+            pltpu.VMEM((2, owners) + shards[1].shape, BF16),
+            pltpu.VMEM(lead + (mixed - query_cols,), BF16),
+            pltpu.VMEM((nz, width) + shards[2].shape, BF16),
+            pltpu.VMEM((8, HEAD_DIM), F32),
             pltpu.VMEM((length, length), F32),
             pltpu.VMEM((length, HEAD_DIM), BF16),
             pltpu.VMEM((length, HEAD_DIM), BF16),
@@ -1596,8 +1633,9 @@
             collective_id=collective_id, has_side_effects=True, vmem_limit_bytes=VMEM_LIMIT
         ),
         name="gather_attention",
-    )(shard, hidden, gain, w_mixed, w_out, tables, gains, segments[:, None], segments[None, :])
-    return gathered, raw, normed, attended, branch
+    )(*shards, hidden, head_map, tables, segments[:, None], segments[None, :])
+    whole = [o.reshape((-1, o.shape[-1])) for o in outs[:4]]
+    return whole + list(outs[4:])
 
 
 class ExpertGrads:
@@ -1776,22 +1814,25 @@
         [w_router, column(attn_gain), column(mlp_gain), column(query_gain), column(key_gain)], rows, lanes, BF16
     )
     w_mixed = jnp.concatenate([w_query, w_key, w_value], 1)
-    w_mixed, w_out, small = gather_all([w_mixed, w_output, small], 1)
+
+    cosine_table, sine_table = rope_tables(jnp.arange(length) % TOK_DEV, HEAD_DIM)
+    cosine, sine = cosine_table[:, 0], sine_table[:, 0]
+    tables = jnp.stack([jnp.concatenate([cosine, cosine], 1), jnp.concatenate([-sine, sine], 1)])
+    lane = jnp.arange(HEAD_DIM)
+    head_map = (jnp.arange(width)[:, None] == (lane // head_rows * rows + lane % head_rows)[None, :]).astype(BF16)
+    columns = (experts_total, experts_total + 2, experts_total + 3)
+    w_mixed, w_out, small, all_grads, mixed, normed_attn, attended, branch = gather_with_attention(
+        w_mixed, w_output, small, out_grad, columns, hidden_in, head_map, tables, segment_ids, 3
+    )
     router = small[:, :experts_total]
     attn_gain, mlp_gain = small[:, experts_total], small[:, experts_total + 1]
     heads_of = small.reshape(devices, rows, lanes)[:, :head_rows]
     query_gain = heads_of[:, :, experts_total + 2].reshape(-1)
     key_gain = heads_of[:, :, experts_total + 3].reshape(-1)
 
+    head_gains = jnp.stack([query_gain, key_gain]).astype(F32)
     plain_in = hidden_in.astype(F32)
     inv_attn = rms_scale(plain_in)
-    cosine_table, sine_table = rope_tables(jnp.arange(length) % TOK_DEV, HEAD_DIM)
-    cosine, sine = cosine_table[:, 0], sine_table[:, 0]
-    tables = jnp.stack([jnp.concatenate([cosine, cosine], 1), jnp.concatenate([-sine, sine], 1)])
-    head_gains = jnp.stack([query_gain, key_gain]).astype(F32)
-    all_grads, mixed, normed_attn, attended, branch = gather_with_attention(
-        out_grad, hidden_in, attn_gain.astype(F32)[None, :], w_mixed, w_out, tables, head_gains, segment_ids, 3
-    )
     residual = plain_in + branch
 
     inv_mlp = rms_scale(residual)

time: 971 us -> 955 us (0.984)
  Pallas kernels: 889 us -> 871 us
    pallas_call x2 -> x1, Pallas kernels: 296 us -> 279 us  [gather_with_attention(): pl.pallas_call(functools.partial(gather_attention_kernel, nz, [0, 0, 2, 1...]
    unnamed x61 -> x55, local copies, waits for them, and re-layouts: 23.8 us -> 23.9 us
where the time goes in v7:
time: 955 us; the launch traced here: 945 us
  Pallas kernels  871 us (91%)
  local copies, waits for them, and re-layouts  43.7 us (5%)
  other arithmetic  23.5 us (2%)
    pallas_call x1, Pallas kernels, gather_with_attention(): pl.pallas_call(functools.partial(gather_attention_kernel, nz, [0, 0, 2, 1...  279 us
    pallas_call x1, Pallas kernels, gather_with_experts(): pl.pallas_call(functools.partial(gather_expert_kernel, nz, cap, group), o...  164 us
    pallas_call x1, Pallas kernels, scatter_sum(): pl.pallas_call(functools.partial(scatter_kernel, nz, count), out_shape=[j...  153 us
    pallas_call x1, Pallas kernels, scatter_with_grads(): pl.pallas_call(functools.partial(scatter_grads_kernel, nz, plan, count),...  139 us
    pallas_call x1, Pallas kernels, scatter_with_attention(): pl.pallas_call(functools.partial(scatter_attention_kernel, nz, plan), out...  135 us
    unnamed x55, local copies, waits for them, and re-layouts  23.9 us

profile of v7, /device:TPU:0, one launch (start us, length us, event | category | flops | bytes accessed | tf_op | source)
XLA Modules:
  0.0 945.5 jit_solution(5834702948927818712)
XLA Ops:
  2.1 1.5 copy.75.refs_7_.refs_5_
  3.6 2.0 pad_maximum_fusion
  8.0 279.3 %gather_attention.1 = (bf16[4,8,4,16,5120]{4,3,2,1,0:T(8,128)(2,1)}, bf16[4,8,4,32,2048]{4,3,2,1,0:T(8,128)(2,1)}, bf16[4,8,4,16,128]{4,3,2,1,0:T(8,128)(2,1)}, ...) custom-call(bf16[4,16,5120]{2,1,0:T(8,128)(2,1)} %bitcast.84, ...), custom_call_target="tpu_custom_call" | custom-call | tf_op jit(solution)/shard_map/gather_attention/pallas_call | solution.py:1608
  287.4 2.6 slice_convert_fusion
  290.3 2.1 multiply_reduce_fusion.2
  295.5 164.1 %gather_experts.1 = (bf16[4,8,4,64,2048]{4,3,2,1,0:T(8,128)(2,1)}, bf16[4,8,4,64,128]{4,3,2,1,0:T(8,128)(2,1)}, bf16[4,8,256,2048]{3,2,1,0:T(8,128)(2,1)}, bf16[...) custom-call(bf16[4,64,2048]{2,1,0:T(8,128)(2,1)} %bitcast.68, ...), custom_call_target="tpu_custom_call" | custom-call | tf_op jit(solution)/shard_map/gather_experts/pallas_call | solution.py:1437
  461.5 139.4 %scatter_grads.1 = (f32[4,64,2048]{2,1,0:T(8,128)}, f32[4,8,256]{2,1,0:T(8,128)}, f32[2048,768]{1,0:T(8,128)}, f32[2048,768]{1,0:T(8,128)}, f32[2048,768]{1,0:T(8,128)}) custom-call(bf16[4,8,4,64,2048]{4,3,2,1,0:T(8,128)(2,1)} %bitcast.64, f32[4,8,4,8,256]{4,3,2,1,0:T(8,128)} %broadcast_multiply_fusion.refs_1_, ...), custom_call_target="tpu_custom_call" | custom-call | tf_op jit(solution)/shard_map/scatter_grads/pallas_call | solution.py:1750
  602.6 2.7 fusion.29
  605.3 2.5 multiply_reduce_fusion
  607.8 2.3 fusion.24
  611.2 135.0 %scatter_attention.1 = (f32[4,64,2048]{2,1,0:T(8,128)}, bf16[256,5120]{1,0:T(8,128)(2,1)}, f32[2,128]{1,0:T(2,128)}, f32[256,2048]{1,0:T(8,128)}, bf16[4096,2048...) custom-call(bf16[4,8,4,64,2048]{4,3,2,1,0:T(8,128)(2,1)} %bitcast.63, bf16[256,2048]{1,0:T(8,128)(2,1)} %get-tuple-element.122.refs_0_, ...), custom_call_target="tpu_custom_call" | custom-call | tf_op jit(solution)/shard_map/scatter_attention/pallas_call | solution.py:1124
  746.2 1.6 copy.105
  747.7 2.4 fusion.6
  752.3 2.0 concatenate.63
  754.3 1.8 concatenate.61
  757.2 4.5 concatenate.55.refs_2_
  761.7 153.1 %scatter_sum.1 = (f32[4,16,5120]{2,1,0:T(8,128)}, f32[4,32,2048]{2,1,0:T(8,128)}, f32[4,16,128]{2,1,0:T(8,128)}) custom-call(bf16[4,8,4,16,5120]{4,3,2,1,0:T(8,128)(2,1)} %bitcast.65, bf16[4,8,4,32,2048]{4,3,2,1,0:T(8,128)(2,1)} %bitcast.67, f32[4,8,4,16,128]{4,3,2,1,0:T(8,128)} %concatenate.55.refs_2_), custom_call_target="tpu_custom_call" | custom-call | tf_op jit(solution)/shard_map/scatter_sum/pallas_call | solution.py:894
  914.9 2.4 slice.71
  917.3 1.7 fusion.25
  922.2 4.3 fusion.3
  926.5 1.6 bitcast_add_fusion
  928.1 6.6 copy.92
  935.7 6.6 copy.112
  942.2 2.7 copy.113
  (98 shorter events, 19.2 us)
Async XLA Ops:
  0.6 5.9 copy-start.17
  0.7 6.1 copy-start.18
  0.7 6.2 copy-start.12
  0.7 6.3 copy-start.15
  0.7 6.5 copy-start.16
  287.4 2.9 copy-start.3
  292.4 1.9 copy-start
  292.4 0.7 copy-start.13
  292.4 1.5 copy-start.6
  293.2 1.2 copy-start.5
  600.9 4.4 copy-start.1
  605.3 2.5 copy-start.8
  747.7 3.3 copy-start.14
  751.2 6.1 copy-start.7
  914.9 4.1 copy-start.11
  914.9 7.3 copy-start.4
  922.2 4.3 copy-start.2
  922.2 4.3 copy-start.9
  928.1 6.7 copy-start.10
  934.7 7.5 slice-start
  935.7 6.6 slice-start.1

commit v8 on v7

--- a/solution.py
+++ b/solution.py
@@ -1464,8 +1464,9 @@
 
 
 class Attention:
-    def __init__(self, columns, hidden, w_mixed, w_out, small, head_map, tables, seg_col, seg_row, raw, normed, attended, branch,
-                 w_buf, o_buf, kv_buf, small_buf, gains, mask, k_rot, v_low, sems):
+    def __init__(self, columns, hidden, w_mixed, w_out, small, head_map, tables, seg_col, seg_row, raw, normed, attended, branch, wide_gains,
+                 gains, w_buf, o_buf, kv_buf, small_buf, mask, k_rot, v_low, sems):
+        self.wide_gains = wide_gains
         self.columns, self.hidden, self.w_mixed, self.w_out = columns, hidden, w_mixed, w_out
         self.small, self.head_map, self.small_buf = small, head_map, small_buf
         self.tables, self.gains, self.seg_col, self.seg_row = tables, gains, seg_col, seg_row
@@ -1509,6 +1510,7 @@
             select = jnp.where(jnp.logical_and(row == k, lane == column), 1.0, select)
         info = mm(select.astype(BF16), self.small_buf[...].reshape(model, lanes), 1, 1)
         self.normed[...] = (values * scale * info[0:1]).astype(BF16)
+        self.wide_gains[...] = info
         self.gains[...] = mm(info.astype(BF16), self.head_map[...])
         self.branch[...] = jnp.zeros_like(self.branch)
         self.mask[...] = allowed_mask(self.seg_col, self.seg_row)
@@ -1566,8 +1568,8 @@
 
 def gather_attention_kernel(nz, plan, columns, *refs):
     shards, inputs = refs[:4], refs[4:9]
-    gathered, outs = refs[9:13], refs[13:17]
-    scratch = refs[17:]
+    gathered, outs = refs[9:13], refs[13:19]
+    scratch = refs[19:]
     z, e = place()
     greet(z, e, nz)
     w = Gather(nz, shards[:3], gathered[:3], *scratch[:3])
@@ -1613,9 +1615,11 @@
             jax.ShapeDtypeStruct((length, model), BF16),
             jax.ShapeDtypeStruct((length, query_cols), BF16),
             jax.ShapeDtypeStruct((length, model), F32),
+            jax.ShapeDtypeStruct((8, model), F32),
+            jax.ShapeDtypeStruct((8, HEAD_DIM), F32),
         ],
         in_specs=[vmem] * 9,
-        out_specs=[hbm] * 4 + [vmem] * 4,
+        out_specs=[hbm] * 4 + [vmem] * 6,
         scratch_shapes=gather_scratch(nz, 3)
         + gather_scratch(nz, 1)
         + [
@@ -1623,7 +1627,6 @@
             pltpu.VMEM((2, owners) + shards[1].shape, BF16),
             pltpu.VMEM(lead + (mixed - query_cols,), BF16),
             pltpu.VMEM((nz, width) + shards[2].shape, BF16),
-            pltpu.VMEM((8, HEAD_DIM), F32),
             pltpu.VMEM((length, length), F32),
             pltpu.VMEM((length, HEAD_DIM), BF16),
             pltpu.VMEM((length, HEAD_DIM), BF16),
@@ -1775,11 +1778,6 @@
     return jnp.concatenate(parts + [jnp.zeros((rows, lanes - used), dtype)], 1)
 
 
-def spread(vector, devices, rows):
-    blocks = vector.reshape(devices, -1)
-    return jnp.pad(blocks, ((0, 0), (0, rows - blocks.shape[1]))).reshape(devices * rows, 1)
-
-
 def per_device_gather(
     hidden_in,
     segment_ids,
@@ -1820,17 +1818,13 @@
     tables = jnp.stack([jnp.concatenate([cosine, cosine], 1), jnp.concatenate([-sine, sine], 1)])
     lane = jnp.arange(HEAD_DIM)
     head_map = (jnp.arange(width)[:, None] == (lane // head_rows * rows + lane % head_rows)[None, :]).astype(BF16)
-    columns = (experts_total, experts_total + 2, experts_total + 3)
-    w_mixed, w_out, small, all_grads, mixed, normed_attn, attended, branch = gather_with_attention(
+    columns = (experts_total, experts_total + 2, experts_total + 3, experts_total + 1)
+    w_mixed, w_out, small, all_grads, mixed, normed_attn, attended, branch, wide_gains, head_gains = gather_with_attention(
         w_mixed, w_output, small, out_grad, columns, hidden_in, head_map, tables, segment_ids, 3
     )
     router = small[:, :experts_total]
-    attn_gain, mlp_gain = small[:, experts_total], small[:, experts_total + 1]
-    heads_of = small.reshape(devices, rows, lanes)[:, :head_rows]
-    query_gain = heads_of[:, :, experts_total + 2].reshape(-1)
-    key_gain = heads_of[:, :, experts_total + 3].reshape(-1)
-
-    head_gains = jnp.stack([query_gain, key_gain]).astype(F32)
+    attn_gain, mlp_gain = wide_gains[0], wide_gains[3]
+    head_gains = head_gains[1:3]
     plain_in = hidden_in.astype(F32)
     inv_attn = rms_scale(plain_in)
     residual = plain_in + branch
@@ -1861,7 +1855,7 @@
     gate_grad = gate_grad.T
     sel_grad = gate * (gate_grad - jnp.sum(gate * gate_grad, -1, keepdims=True))
     logit_grad = jnp.where(chosen, sel_grad, 0.0).astype(BF16)
-    grad_w_router = jnp.dot(normed_mlp.T, logit_grad, preferred_element_type=F32)
+    grad_w_router = jnp.dot(logit_grad.T, normed_mlp, preferred_element_type=F32)
     normed_mlp_grad = row_grad_sum + jnp.dot(logit_grad, router.T, preferred_element_type=F32)
     grad_mlp_gain = jnp.sum(normed_mlp_grad * residual * inv_mlp, 0)
     residual_grad = out_grad.astype(F32) + norm_grad(normed_mlp_grad, residual, inv_mlp, mlp_gain)
@@ -1872,22 +1866,12 @@
         normed_attn, attended, w_mixed, 5,
     )
     block_out = residual + mixed_out
-    grad_query_gain, grad_key_gain = gain_grads[0], gain_grads[1]
     grad_attn_gain = jnp.sum(normed_attn_grad * plain_in * inv_attn, 0)
     grad_in = residual_grad + norm_grad(normed_attn_grad, plain_in, inv_attn, attn_gain)
 
-    small_grads = pack_columns(
-        [
-            grad_w_router,
-            grad_attn_gain[:, None],
-            grad_mlp_gain[:, None],
-            spread(grad_query_gain, devices, rows),
-            spread(grad_key_gain, devices, rows),
-        ],
-        width,
-        lanes,
-        F32,
-    )
+    head_rows_grad = jnp.dot(gain_grads, head_map.T.astype(F32), precision=lax.Precision.HIGHEST)
+    small_rows = jnp.concatenate([grad_w_router, grad_attn_gain[None], grad_mlp_gain[None], head_rows_grad], 0)
+    small_grads = jnp.pad(small_rows, ((0, lanes - small_rows.shape[0]), (0, 0))).T
     share_mixed, share_w_output, share_small = scatter_sum([grad_w_mixed, grad_w_output, small_grads], 6)
     return (
         block_out,

time: 955 us -> 945 us (0.990)
    unnamed x55 -> x41, local copies, waits for them, and re-layouts: 23.9 us -> 23.8 us
where the time goes in v8:
time: 945 us; the launch traced here: 936 us
  Pallas kernels  871 us (92%)
  local copies, waits for them, and re-layouts  39.5 us (4%)
  other arithmetic  18.4 us (2%)
    pallas_call x1, Pallas kernels, gather_with_attention(): pl.pallas_call(functools.partial(gather_attention_kernel, nz, [0, 0, 2, 1...  279 us
    pallas_call x1, Pallas kernels, gather_with_experts(): pl.pallas_call(functools.partial(gather_expert_kernel, nz, cap, group), o...  164 us
    pallas_call x1, Pallas kernels, scatter_sum(): pl.pallas_call(functools.partial(scatter_kernel, nz, count), out_shape=[j...  153 us
    pallas_call x1, Pallas kernels, scatter_with_grads(): pl.pallas_call(functools.partial(scatter_grads_kernel, nz, plan, count),...  139 us
    pallas_call x1, Pallas kernels, scatter_with_attention(): pl.pallas_call(functools.partial(scatter_attention_kernel, nz, plan), out...  135 us
    unnamed x41, local copies, waits for them, and re-layouts  23.8 us

profile of v8, /device:TPU:0, one launch (start us, length us, event | category | flops | bytes accessed | tf_op | source)
XLA Modules:
  0.0 935.8 jit_solution(3289651097298642554)
XLA Ops:
  6.6 1.5 copy.65.refs_7_.refs_5_
  11.3 279.4 %gather_attention.1 = (bf16[4,8,4,16,5120]{4,3,2,1,0:T(8,128)(2,1)}, bf16[4,8,4,32,2048]{4,3,2,1,0:T(8,128)(2,1)}, bf16[4,8,4,16,128]{4,3,2,1,0:T(8,128)(2,1)}, ...) custom-call(bf16[4,16,5120]{2,1,0:T(8,128)(2,1)} %bitcast.84, ...), custom_call_target="tpu_custom_call" | custom-call | tf_op jit(solution)/shard_map/gather_attention/pallas_call | solution.py:1610
  290.6 1.2 slice.38.refs_4_
  291.9 2.4 multiply_reduce_fusion.2
  294.3 1.2 fusion.29
  297.6 164.1 %gather_experts.1 = (bf16[4,8,4,64,2048]{4,3,2,1,0:T(8,128)(2,1)}, bf16[4,8,4,64,128]{4,3,2,1,0:T(8,128)(2,1)}, bf16[4,8,256,2048]{3,2,1,0:T(8,128)(2,1)}, bf16[...) custom-call(bf16[4,64,2048]{2,1,0:T(8,128)(2,1)} %bitcast.72, ...), custom_call_target="tpu_custom_call" | custom-call | tf_op jit(solution)/shard_map/gather_experts/pallas_call | solution.py:1437
  462.4 1.2 broadcast_multiply_fusion.refs_1_
  463.6 139.4 %scatter_grads.1 = (f32[4,64,2048]{2,1,0:T(8,128)}, f32[4,8,256]{2,1,0:T(8,128)}, f32[2048,768]{1,0:T(8,128)}, f32[2048,768]{1,0:T(8,128)}, f32[2048,768]{1,0:T(8,128)}) custom-call(bf16[4,8,4,64,2048]{4,3,2,1,0:T(8,128)(2,1)} %bitcast.68, f32[4,8,4,8,256]{4,3,2,1,0:T(8,128)} %broadcast_multiply_fusion.refs_1_, ...), custom_call_target="tpu_custom_call" | custom-call | tf_op jit(solution)/shard_map/scatter_grads/pallas_call | solution.py:1753
  604.5 1.5 fusion.33
  606.0 3.2 multiply_reduce_fusion
  609.2 2.3 fusion.27
  611.6 135.0 %scatter_attention.1 = (f32[4,64,2048]{2,1,0:T(8,128)}, bf16[256,5120]{1,0:T(8,128)(2,1)}, f32[2,128]{1,0:T(2,128)}, f32[256,2048]{1,0:T(8,128)}, bf16[4096,2048...) custom-call(bf16[4,8,4,64,2048]{4,3,2,1,0:T(8,128)(2,1)} %bitcast.67, bf16[256,2048]{1,0:T(8,128)(2,1)} %get-tuple-element.122.refs_0_, ...), custom_call_target="tpu_custom_call" | custom-call | tf_op jit(solution)/shard_map/scatter_attention/pallas_call | solution.py:1124
  746.6 4.0 bitcast_add_fusion
  751.3 1.0 copy-done.5
  752.2 1.9 fusion.3
  754.8 1.3 copy.68
  756.1 153.0 %scatter_sum.1 = (f32[4,16,5120]{2,1,0:T(8,128)}, f32[4,32,2048]{2,1,0:T(8,128)}, f32[4,16,128]{2,1,0:T(8,128)}) custom-call(bf16[4,8,4,16,5120]{4,3,2,1,0:T(8,128)(2,1)} %bitcast.69, bf16[4,8,4,32,2048]{4,3,2,1,0:T(8,128)(2,1)} %bitcast.71, f32[4,8,4,16,128]{4,3,2,1,0:T(8,128)} %bitcast.79), custom_call_target="tpu_custom_call" | custom-call | tf_op jit(solution)/shard_map/scatter_sum/pallas_call | solution.py:894
  911.2 1.4 copy.80
  914.7 1.7 fusion.28
  916.4 2.3 slice.52
  918.6 6.6 copy.74
  925.3 1.0 copy.86
  926.3 6.6 copy.87
  932.8 2.7 copy.88
  (73 shorter events, 18.9 us)
Async XLA Ops:
  0.6 9.7 %copy-start.10 = (bf16[64,512]{1,0:T(8,128)(2,1)S(1)}, bf16[64,512]{1,0:T(8,128)(2,1)}, u32[]{:S(2)}) copy-start(bf16[64,512]{1,0:T(8,128)(2,1)} %param.24) | copy-start | bytes 196612
  0.7 9.7 %copy-start.11 = (bf16[64,512]{1,0:T(8,128)(2,1)S(1)}, bf16[64,512]{1,0:T(8,128)(2,1)}, u32[]{:S(2)}) copy-start(bf16[64,512]{1,0:T(8,128)(2,1)} %param.23) | copy-start | bytes 196612
  0.7 9.7 %copy-start.9 = (bf16[64,4096]{1,0:T(8,128)(2,1)S(1)}, bf16[64,4096]{1,0:T(8,128)(2,1)}, u32[]{:S(2)}) copy-start(bf16[64,4096]{1,0:T(8,128)(2,1)} %param.22) | copy-start | bytes 1572868
  294.2 2.1 copy-start
  294.3 1.6 copy-start.7
  295.7 1.0 copy-start.3
  606.0 3.2 copy-start.1
  606.0 3.2 copy-start.6
  746.6 4.1 copy-start.2
  746.6 4.0 copy-start.4
  750.6 1.6 copy-start.5
  752.2 1.9 copy-start.12
  918.6 6.7 copy-start.8
  925.3 7.5 slice-start
  926.3 6.6 slice-start.1
